TPU v7x, 32 devices: a whole 2x2x4 slice. The times are simulated.
32 devices in a mesh: kt: 8 (over z, y), tile: 4 (over x, core).
Axes of the slice: x: 2, y: 2, z: 4, core: 2. Of those that a mesh axis runs over, the one named last changes fastest.
Arguments:
- green_particle: bfloat16 [2, 64, 1024, 1024], P(None, 'kt', 'tile'), may hold values from -6 to 6
- green_hole: bfloat16 [2, 64, 1024, 1024], P(None, 'kt', 'tile'), may hold values from -6 to 6
- coulomb: bfloat16 [2, 64, 1024, 1024], P(None, 'kt'), may hold values from -3 to 3
Outputs:
- screened: float32 [2, 64, 1024, 1024], P(None, 'kt', 'tile')
All inputs are finite; a program needn't handle non-finite values.
Results may differ from a plain program's by a relative error of at most 0.0039.
Values may be sent and summed in bfloat16 or wider, within the bound.
No kernel may reach another device: no remote copies, remote signals or barrier semaphores. Data moves between devices by JAX's collectives and lax.ppermute only.
A program may use at most 192 MiB of HBM per device.

v0:
```python
import math

import jax
import jax.numpy as jnp
from jax import lax
from jax.sharding import PartitionSpec as P

KSIDE = 4
K = 64


HIGHEST = lax.Precision.HIGHEST


def phase_tables(points, side_count):
    point_index = jnp.arange(points, dtype=jnp.int32)
    digit_high = point_index // (side_count * side_count)
    digit_mid = point_index // side_count % side_count
    digit_low = point_index % side_count
    phase_turns = (
        digit_high[:, None] * digit_high[None, :]
        + digit_mid[:, None] * digit_mid[None, :]
        + digit_low[:, None] * digit_low[None, :]
    ) % side_count
    angles = phase_turns.astype(jnp.float32) * (2.0 * math.pi / side_count)
    return (jnp.cos(angles) / points, jnp.sin(angles) / points)


def to_cells(real_part, imag_part, cosine_table, sine_table):
    return (
        jnp.dot(cosine_table, real_part, precision=HIGHEST)
        - jnp.dot(sine_table, imag_part, precision=HIGHEST),
        jnp.dot(sine_table, real_part, precision=HIGHEST)
        + jnp.dot(cosine_table, imag_part, precision=HIGHEST),
    )


def to_momenta(real_part, imag_part, cosine_table, sine_table):
    return (
        jnp.dot(cosine_table, real_part, precision=HIGHEST)
        + jnp.dot(sine_table, imag_part, precision=HIGHEST),
        jnp.dot(cosine_table, imag_part, precision=HIGHEST)
        - jnp.dot(sine_table, real_part, precision=HIGHEST),
    )


def polarize(particle, hole_part):
    cosine_table, sine_table = phase_tables(K, KSIDE)
    part_real, part_imag = to_cells(
        particle[0].astype(jnp.float32), particle[1].astype(jnp.float32), cosine_table, sine_table
    )
    hole_real, hole_imag = to_cells(
        hole_part[0].astype(jnp.float32), hole_part[1].astype(jnp.float32), cosine_table, sine_table
    )
    cell_real = part_real * hole_real - part_imag * hole_imag
    cell_imag = part_real * hole_imag + part_imag * hole_real
    mom_real, mom_imag = to_momenta(cell_real, cell_imag, cosine_table, sine_table)
    return jnp.stack([mom_real, mom_imag]).astype(jnp.bfloat16)


def product_of(left_side, right_side):
    return jnp.einsum("kij,kjl->kil", left_side, right_side, preferred_element_type=jnp.float32)


def complex_batched(left_real, left_imag, right_real, right_imag):
    real_out = product_of(left_real, right_real) - product_of(left_imag, right_imag)
    imag_out = product_of(left_real, right_imag) + product_of(left_imag, right_real)
    return (real_out, imag_out)


def body(green_particle, green_hole, coulomb):
    tile_rows = green_particle.shape[2]
    moved_part, moved_hole = (
        lax.all_to_all(green_particle, "kt", split_axis=3, concat_axis=1, tiled=True),
        lax.all_to_all(green_hole, "kt", split_axis=3, concat_axis=1, tiled=True),
    )
    points = moved_part.shape[1]
    narrow = moved_part.shape[3]
    polar_q = polarize(
        moved_part.reshape(2, points, tile_rows * narrow),
        moved_hole.reshape(2, points, tile_rows * narrow),
    )
    polar_q = polar_q.reshape(2, points, tile_rows, narrow)
    polar_rows = lax.all_to_all(polar_q, "kt", split_axis=1, concat_axis=3, tiled=True)
    mid_real, mid_imag = complex_batched(polar_rows[0], polar_rows[1], coulomb[0], coulomb[1])
    mid_stack = jnp.stack([mid_real.astype(jnp.bfloat16), mid_imag.astype(jnp.bfloat16)])
    row_start = lax.axis_index("tile") * tile_rows
    coulomb_rows = lax.dynamic_slice_in_dim(coulomb, row_start, tile_rows, 2)
    segment = lax.all_gather(mid_stack, "tile", axis=2, tiled=True)
    left_real = coulomb_rows[0]
    left_imag = coulomb_rows[1]
    more_real, more_imag = complex_batched(left_real, left_imag, segment[0], segment[1])
    summed = jnp.stack([more_real, more_imag])
    return coulomb_rows.astype(jnp.float32) + summed


def solution(mesh):
    return jax.shard_map(
        body,
        mesh=mesh,
        in_specs=(
            P(None, "kt", "tile", None),
            P(None, "kt", "tile", None),
            P(None, "kt", None, None),
        ),
        out_specs=P(None, "kt", "tile", None),
        check_vma=False,
    )
```

profile of v0, /device:TPU:0, one launch (start us, length us, event | category | flops | bytes accessed | tf_op | source)
XLA Modules:
  0.0 1116.9 jit_solution(6014429570869471573)
XLA Ops:
  6.5 12.6 %copy.8 = bf16[2,8,256,1024]{2,1,0,3:T(8,128)(2,1)} copy(bf16[2,8,256,1024]{3,2,1,0:T(8,128)(2,1)} %param.3) | data formatting | bytes 16777216 | tf_op args[0]
  19.1 7.3 all-to-all-start
  26.4 12.5 %copy.10 = bf16[2,8,256,1024]{2,1,0,3:T(8,128)(2,1)} copy(bf16[2,8,256,1024]{3,2,1,0:T(8,128)(2,1)} %param.4) | data formatting | bytes 16777216 | tf_op args[1]
  38.9 170.7 %all-to-all-done = bf16[2,8,256,1024]{2,1,0,3:T(8,128)(2,1)} async-done(((bf16[2,8,256,1024]{2,1,0,3:T(8,128)(2,1)}), bf16[2,8,256,1024]{2,1,0,3:T(8,128)(2,1)}, u32[]{:S(2)}, u32[]{:S(2)}) %all-to-all-start) | async-done | bytes 8388640 | tf_op jit(solution)/shard_map/all_to_all | solution.py:74
  209.6 5.0 all-to-all-start.1
  214.6 0.0 all-gather.2.cloned.1.call-start
  214.7 12.5 %copy.9 = bf16[2,8,256,8,128]{4,2,1,3,0:T(8,128)(2,1)} copy(bf16[2,8,256,8,128]{2,1,0,4,3:T(8,128)(2,1)} %bitcast.1) | data formatting | bytes 16777216 | tf_op jit(solution)/shard_map/all_to_all | solution.py:74
  227.2 5.3 slice_bitcast_fusion.8
  232.5 14.0 %fusion.28 = f32[64,32768]{1,0:T(8,128)} fusion(bf16[8,8,256,128]{3,2,1,0:T(8,128)(2,1)S(1)} %get-tuple-element.12, s32[64]{0:T(128)S(1)} %get-tuple-element.13, s32[64]{0:T(128)S(1)} %get-tuple-element.14, s32[64]{0:T(128)S(1)} %and_select_fusion.3), kind=kOutput, calls=%fused_computation.48 | convolution fusion | flops 1610690560 | bytes 12583680 | tf_op jit(solution)/shard_map/dot_general | solution.py:33
  246.5 14.2 %fusion.30 = f32[64,32768]{1,0:T(8,128)} fusion(bf16[8,8,256,128]{3,2,1,0:T(8,128)(2,1)S(1)} %get-tuple-element.12, s32[64]{0:T(128)S(1)} %get-tuple-element.13, s32[64]{0:T(128)S(1)} %get-tuple-element.14, s32[64]{0:T(128)S(1)} %and_select_fusion.3), kind=kOutput, calls=%fused_computation.50 | convolution fusion | flops 1610690560 | bytes 12583680 | tf_op jit(solution)/shard_map/dot_general | solution.py:31
  260.7 136.1 %all-to-all-done.1 = bf16[2,8,256,1024]{2,1,0,3:T(8,128)(2,1)} async-done(((bf16[2,8,256,1024]{2,1,0,3:T(8,128)(2,1)}), bf16[2,8,256,1024]{2,1,0,3:T(8,128)(2,1)}, u32[]{:S(2)}, u32[]{:S(2)}) %all-to-all-start.1) | async-done | bytes 8388640 | tf_op jit(solution)/shard_map/all_to_all | solution.py:75
  396.9 12.2 %copy.11 = bf16[2,8,256,8,128]{4,2,1,3,0:T(8,128)(2,1)} copy(bf16[2,8,256,8,128]{2,1,0,4,3:T(8,128)(2,1)} %bitcast.3) | data formatting | bytes 16777216 | tf_op jit(solution)/shard_map/all_to_all | solution.py:75
  409.1 4.2 slice_bitcast_fusion.6
  413.3 5.4 fusion.22
  418.7 5.4 fusion.24
  424.1 0.0 slice-start.2
  424.1 14.6 %convolution_add_fusion = f32[64,32768]{1,0:T(8,128)} fusion(f32[64,32768]{1,0:T(8,128)S(1)} %fusion.22, bf16[8,8,256,128]{3,2,1,0:T(8,128)(2,1)S(1)} %get-tuple-element.9, s32[64]{0:T(128)S(1)} %get-tuple-element.13, s32[64]{0:T(128)S(1)} %get-tuple-element.14, s32[64]{0:T(128)S(1)} %and_select_fusion.3), kind=kOutput, calls=%fused_computation | convolution fusion | flops 1612787712 | bytes 20972288 | tf_op jit(solution)/shard_map/dot_general | solution.py:34
  438.7 14.6 %convolution_subtract_fusion = f32[64,32768]{1,0:T(8,128)} fusion(f32[64,32768]{1,0:T(8,128)S(1)} %fusion.24, bf16[8,8,256,128]{3,2,1,0:T(8,128)(2,1)S(1)} %get-tuple-element.9, s32[64]{0:T(128)S(1)} %get-tuple-element.13, s32[64]{0:T(128)S(1)} %get-tuple-element.14, s32[64]{0:T(128)S(1)} %and_select_fusion.3), kind=kOutput, calls=%fused_computation.2 | convolution fusion | flops 1612787712 | bytes 20972288 | tf_op jit(solution)/shard_map/dot_general | solution.py:32
  453.3 14.4 %convolution_subtract_fusion.1 = f32[64,32768]{1,0:T(8,128)} fusion(f32[64,32768]{1,0:T(8,128)S(1)} %bitcast.119, bf16[8,8,256,128]{3,2,1,0:T(8,128)(2,1)S(1)} %copy-done.1, s32[64]{0:T(128)S(1)} %get-tuple-element.13, s32[64]{0:T(128)S(1)} %get-tuple-element.14, s32[64]{0:T(128)S(1)} %and_select_fusion.3), kind=kOutput, calls=%fused_computation.3 | convolution fusion | flops 1612787712 | bytes 20972288 | tf_op jit(solution)/shard_map/dot_general | solution.py:32
  467.7 22.5 %multiply_subtract_fusion = (f32[64,32768]{1,0:T(8,128)}, f32[64,32768]{1,0:T(8,128)}) fusion(f32[64,32768]{1,0:T(8,128)} %convolution_add_fusion, f32[64,32768]{1,0:T(8,128)} %convolution_subtract_fusion.1, f32[64,32768]{1,0:T(8,128)} %convolution_subtract_fusion, f32[64,32768]{1,0:T(8,128)} %fusion.28, bf16[8,8,256,128]{3,2,1,0:T(8,128)(2,1)} %get-tuple-element.11, ...), kind=kOutput, calls=%fused_computation.35 | convolution fusion | flops 1625370624 | bytes 54526720 | tf_op jit(solution)/shard_map/dot_general | solution.py:34
  490.2 12.6 %fusion.50 = f32[64,32768]{1,0:T(8,128)} fusion(f32[64,32768]{1,0:T(8,128)} %get-tuple-element.5, s32[64]{0:T(128)S(1)} %get-tuple-element.13, s32[64]{0:T(128)S(1)} %get-tuple-element.14, s32[64]{0:T(128)S(1)} %and_select_fusion.3), kind=kOutput, calls=%fused_computation.77 | convolution fusion | flops 1610690560 | bytes 16777984 | tf_op jit(solution)/shard_map/dot_general | solution.py:40
  502.8 7.8 fusion.49
  510.6 0.0 slice-start.1
  510.6 12.9 %fusion.45 = bf16[8,8,256,128]{3,1,2,0:T(8,128)(2,1)} fusion(f32[64,32768]{1,0:T(8,128)} %fusion.50, f32[64,32768]{1,0:T(8,128)S(1)} %copy-done, s32[64]{0:T(128)S(1)} %get-tuple-element.13, s32[64]{0:T(128)S(1)} %get-tuple-element.14, s32[64]{0:T(128)S(1)} %and_select_fusion.3), kind=kOutput, calls=%fused_computation.67 | convolution fusion | flops 1614884864 | bytes 20972288 | tf_op jit(solution)/shard_map/dot_general | solution.py:41
  523.5 8.9 fusion.44
  532.4 1.2 copy.20
  533.5 0.5 bitcast_bitcast_fusion
  534.0 0.5 copy-done.2
  534.5 1.2 copy.19
  535.7 2.2 bitcast_bitcast_fusion.1
  537.9 6.4 pad_maximum_fusion
  544.3 187.7 %all_to_all.45 = bf16[2,64,256,128]{3,2,0,1:T(8,128)(2,1)} all-to-all(bf16[2,64,256,128]{3,2,0,1:T(8,128)(2,1)} %pad_maximum_fusion), channel_id=1, replica_groups=mesh['kt'=8,'tile'=4] {'kt'}, dimensions={1} | all-to-all | bytes 16777216 | tf_op jit(solution)/shard_map/all_to_all | solution.py:84
  732.0 13.9 %copy.56 = bf16[2,8,8,256,128]{4,1,3,2,0:T(8,128)(2,1)} copy(bf16[2,8,8,256,128]{4,3,0,2,1:T(8,128)(2,1)} %bitcast.123) | data formatting | bytes 16777216 | tf_op jit(solution)/shard_map/all_to_all | solution.py:84
  745.9 5.8 fusion.116
  751.7 7.3 squeeze.43
  759.0 7.7 squeeze.41
  766.7 15.1 %fusion.2 = f32[8,256,1024]{2,1,0:T(8,128)} fusion(bf16[8,256,1024]{2,1,0:T(8,128)(2,1)} %squeeze.41, bf16[2,8,1024,1024]{3,2,1,0:T(8,128)(2,1)} %param.5), kind=kOutput, calls=%fused_computation.11 | convolution fusion | flops 4294967296 | bytes 29360128 | tf_op jit(solution)/shard_map/kij,kjl->kil/dot_general | solution.py:62
  781.8 13.6 %fusion.4 = f32[8,256,1024]{2,1,0:T(8,128)} fusion(bf16[8,256,1024]{2,1,0:T(8,128)(2,1)S(1)} %copy-done.3, bf16[2,8,1024,1024]{3,2,1,0:T(8,128)(2,1)} %param.5), kind=kOutput, calls=%fused_computation.13 | convolution fusion | flops 4294967296 | bytes 29360128 | tf_op jit(solution)/shard_map/kij,kjl->kil/dot_general | solution.py:62
  795.4 14.7 %fusion.19 = bf16[1,8,256,1024]{3,2,1,0:T(8,128)(2,1)} fusion(f32[8,256,1024]{2,1,0:T(8,128)} %fusion.2, bf16[8,256,1024]{2,1,0:T(8,128)(2,1)S(1)} %copy-done.3, bf16[2,8,1024,1024]{3,2,1,0:T(8,128)(2,1)} %param.5), kind=kOutput, calls=%fused_computation.37 | convolution fusion | flops 4299161600 | bytes 33554432 | tf_op jit(solution)/shard_map/kij,kjl->kil/dot_general | solution.py:62
  810.1 13.7 %fusion.18 = bf16[1,8,256,1024]{3,2,1,0:T(8,128)(2,1)} fusion(f32[8,256,1024]{2,1,0:T(8,128)} %fusion.4, bf16[8,256,1024]{2,1,0:T(8,128)(2,1)} %squeeze.41, bf16[2,8,1024,1024]{3,2,1,0:T(8,128)(2,1)} %param.5), kind=kOutput, calls=%fused_computation.36 | convolution fusion | flops 4299161600 | bytes 33554432 | tf_op jit(solution)/shard_map/kij,kjl->kil/dot_general | solution.py:62
  823.8 6.4 pad_maximum_fusion.1
  830.2 0.0 all-gather.2.cloned.1.call-update
  830.2 200.5 %all-gather.2.cloned.1.call-done = bf16[2,8,1024,1024]{3,2,1,0:T(8,128)(2,1)} async-done(((bf16[2,8,256,1024]{3,2,1,0:T(8,128)(2,1)}), bf16[2,8,1024,1024]{3,2,1,0:T(8,128)(2,1)}) %all-gather.2.cloned.1.call-update) | async-done | bytes 33554448 | tf_op jit(solution)/shard_map/all_gather | solution.py:89
  1030.7 14.8 %fusion.11 = f32[8,256,1024]{2,1,0:T(8,128)} fusion(bf16[2,8,1024,1024]{3,2,1,0:T(8,128)(2,1)} %all-gather.2.cloned.1.call-done, bf16[2,8,1024,1024]{3,2,1,0:T(8,128)(2,1)} %param.5, s32[]{:T(128)S(6)} %select_n.170), kind=kOutput, calls=%fused_computation.20 | convolution fusion | flops 4294967296 | bytes 29360132 | tf_op jit(solution)/shard_map/kij,kjl->kil/dot_general | solution.py:62
  1045.5 15.0 %fusion.10 = f32[8,256,1024]{2,1,0:T(8,128)} fusion(bf16[2,8,1024,1024]{3,2,1,0:T(8,128)(2,1)} %all-gather.2.cloned.1.call-done, bf16[2,8,1024,1024]{3,2,1,0:T(8,128)(2,1)} %param.5, s32[]{:T(128)S(6)} %add.203, s32[]{:T(128)S(6)} %select_n.170), kind=kOutput, calls=%fused_computation.19 | convolution fusion | flops 4294967296 | bytes 29360136 | tf_op jit(solution)/shard_map/kij,kjl->kil/dot_general | solution.py:62
  1060.5 17.2 %add_bitcast_fusion = f32[1,8,256,1024]{3,2,1,0:T(8,128)} fusion(f32[8,256,1024]{2,1,0:T(8,128)} %fusion.10, bf16[2,8,1024,1024]{3,2,1,0:T(8,128)(2,1)} %all-gather.2.cloned.1.call-done, bf16[2,8,1024,1024]{3,2,1,0:T(8,128)(2,1)} %param.5, s32[]{:T(128)S(6)} %select_n.170), kind=kOutput, calls=%fused_computation.30 | convolution fusion | flops 4297064448 | bytes 37748740 | tf_op jit(solution)/shard_map/kij,kjl->kil/dot_general | solution.py:62
  1077.7 17.4 %subtract_bitcast_fusion = f32[1,8,256,1024]{3,2,1,0:T(8,128)} fusion(f32[8,256,1024]{2,1,0:T(8,128)} %fusion.11, bf16[2,8,1024,1024]{3,2,1,0:T(8,128)(2,1)} %all-gather.2.cloned.1.call-done, bf16[2,8,1024,1024]{3,2,1,0:T(8,128)(2,1)} %param.5, s32[]{:T(128)S(6)} %add.203, s32[]{:T(128)S(6)} %select_n.170), kind=kOutput, calls=%fused_computation.31 | convolution fusion | flops 4297064448 | bytes 37748744 | tf_op jit(solution)/shard_map/kij,kjl->kil/dot_general | solution.py:62
  1095.2 14.7 %maximum_add_fusion = f32[2,8,256,1024]{3,2,1,0:T(8,128)} fusion(f32[1,8,256,1024]{3,2,1,0:T(8,128)} %add_bitcast_fusion, f32[1,8,256,1024]{3,2,1,0:T(8,128)} %subtract_bitcast_fusion, bf16[2,8,1024,1024]{3,2,1,0:T(8,128)(2,1)} %param.5, s32[]{:T(128)S(6)} %select_n.170), kind=kLoop, calls=%fused_computation.10 | loop fusion | flops 12582912 | bytes 41943044 | tf_op jit(solution)/shard_map/add | solution.py:94
  (19 shorter events, 0.0 us)
Async XLA Ops:
  19.1 190.5 %all-to-all-start = ((bf16[2,8,256,1024]{2,1,0,3:T(8,128)(2,1)}), bf16[2,8,256,1024]{2,1,0,3:T(8,128)(2,1)}, u32[]{:S(2)}, u32[]{:S(2)}) async-start(bf16[2,8,256,1024]{2,1,0,3:T(8,128)(2,1)} %copy.8), calls=%async_computation | async-start | bytes 16777216 | tf_op jit(solution)/shard_map/all_to_all | solution.py:74
  209.6 187.3 %all-to-all-start.1 = ((bf16[2,8,256,1024]{2,1,0,3:T(8,128)(2,1)}), bf16[2,8,256,1024]{2,1,0,3:T(8,128)(2,1)}, u32[]{:S(2)}, u32[]{:S(2)}) async-start(bf16[2,8,256,1024]{2,1,0,3:T(8,128)(2,1)} %copy.10), calls=%async_computation.1 | async-start | bytes 16777216 | tf_op jit(solution)/shard_map/all_to_all | solution.py:75
  214.6 816.1 %all-gather.2.cloned.1.call-start = ((), (), s32[]{:S(2)}) async-start(), calls=%async_computation.3 | async-start | bytes 41943040 | tf_op jit(solution)/shard_map/all_gather | solution.py:89
  424.1 29.2 %slice-start.2 = ((s8[8388608]{0:T(1024)(128)(4,1)}), s8[4194304]{0:T(1024)(128)(4,1)S(1)}, s32[]{:S(2)}) async-start(s8[8388608]{0:T(1024)(128)(4,1)} %bitcast.118), calls=%async_computation.6 | async-start | bytes 8388608
  438.7 14.6 %copy-start.1 = (bf16[8,8,256,128]{3,2,1,0:T(8,128)(2,1)S(1)}, bf16[8,8,256,128]{3,2,1,0:T(8,128)(2,1)}, u32[]{:S(2)}) copy-start(bf16[8,8,256,128]{3,2,1,0:T(8,128)(2,1)} %get-tuple-element.11) | copy-start | bytes 12582916
  438.7 14.6 %slice-start.3 = ((s8[8388608]{0:T(1024)(128)(4,1)}), s8[4194304]{0:T(1024)(128)(4,1)S(1)}, s32[]{:S(2)}) async-start(s8[8388608]{0:T(1024)(128)(4,1)} %bitcast.118), calls=%async_computation.7 | async-start | bytes 8388608
  490.2 12.6 %copy-start = (f32[64,32768]{1,0:T(8,128)S(1)}, f32[64,32768]{1,0:T(8,128)}, u32[]{:S(2)}) copy-start(f32[64,32768]{1,0:T(8,128)} %get-tuple-element.6) | copy-start | bytes 25165828
  502.8 20.7 %slice-start = ((s8[8388608]{0:T(1024)(128)(4,1)}), s8[4194304]{0:T(1024)(128)(4,1)S(1)}, s32[]{:S(2)}) async-start(s8[8388608]{0:T(1024)(128)(4,1)} %bitcast.116), calls=%async_computation.4 | async-start | bytes 8388608
  510.6 12.9 %slice-start.1 = ((s8[8388608]{0:T(1024)(128)(4,1)}), s8[4194304]{0:T(1024)(128)(4,1)S(1)}, s32[]{:S(2)}) async-start(s8[8388608]{0:T(1024)(128)(4,1)} %bitcast.116), calls=%async_computation.5 | async-start | bytes 8388608
  532.4 2.2 copy-start.2
  766.7 15.1 %copy-start.3 = (bf16[8,256,1024]{2,1,0:T(8,128)(2,1)S(1)}, bf16[8,256,1024]{2,1,0:T(8,128)(2,1)}, u32[]{:S(2)}) copy-start(bf16[8,256,1024]{2,1,0:T(8,128)(2,1)} %squeeze.43) | copy-start | bytes 12582916
  810.1 13.7 %copy-start.4 = (bf16[1,8,256,1024]{3,2,1,0:T(8,128)(2,1)S(1)}, bf16[1,8,256,1024]{3,2,1,0:T(8,128)(2,1)}, u32[]{:S(2)}) copy-start(bf16[1,8,256,1024]{3,2,1,0:T(8,128)(2,1)} %fusion.19) | copy-start | bytes 12582916
Sparse Core Ops, SparseCore 0:
  830.3 200.3 all-gather.1
where the time goes:
time: 1120 us
  waiting for transfers between devices  507 us (45%)
  matrix products  269 us (24%)
  blocking collectives  188 us (17%)
  local copies, waits for them, and re-layouts  99.5 us (9%)
  other arithmetic  27.4 us (2%)
  between operations  13.8 us (1%)
  starting transfers between devices  12.4 us (1%)
    all_gather x1, waiting for transfers between devices, body(): segment = lax.all_gather(mid_stack, 'tile', axis=2, tiled=True)  201 us
    all_to_all x1, blocking collectives, body(): lax.all_to_all(polar_q, 'kt', split_axis=1, concat_axis=3, tiled=True)  188 us
    all_to_all x1, waiting for transfers between devices, body(): lax.all_to_all(green_particle, 'kt', split_axis=3, concat_axis=1, tiled=T...  171 us
    all_to_all x1, waiting for transfers between devices, body(): lax.all_to_all(green_hole, 'kt', split_axis=3, concat_axis=1, tiled=True)  136 us
    dot_general x8, matrix products, product_of(): jnp.einsum('kij,kjl->kil', left_side, right_side, preferred_element_type=...  122 us
    unnamed x24, local copies, waits for them, and re-layouts  37.4 us
    dot_general x2, matrix products, to_cells(): jnp.dot(cosine_table, imag_part, precision=HIGHEST)  37.1 us
    dot_general x2, matrix products, to_cells(): jnp.dot(sine_table, imag_part, precision=HIGHEST)  28.9 us
  transfers between devices with their start and end apart: 3, of which 3 were waited for; matrix products, arithmetic and copies ran while one was open for 5% of the time, Pallas kernels for 0%

commit v1 on v0

--- a/solution.py
+++ b/solution.py
@@ -3,10 +3,14 @@
 import jax
 import jax.numpy as jnp
 from jax import lax
+from jax.experimental import pallas as pl
+from jax.experimental.pallas import tpu as pltpu
 from jax.sharding import PartitionSpec as P
 
+
 KSIDE = 4
-K = 64
+LANES = 128
+SUB = 16
 
 
 HIGHEST = lax.Precision.HIGHEST
@@ -45,7 +49,7 @@
 
 
 def polarize(particle, hole_part):
-    cosine_table, sine_table = phase_tables(K, KSIDE)
+    cosine_table, sine_table = phase_tables(particle.shape[1], KSIDE)
     part_real, part_imag = to_cells(
         particle[0].astype(jnp.float32), particle[1].astype(jnp.float32), cosine_table, sine_table
     )
@@ -68,7 +72,7 @@
     return (real_out, imag_out)
 
 
-def body(green_particle, green_hole, coulomb):
+def generic_body(green_particle, green_hole, coulomb):
     tile_rows = green_particle.shape[2]
     moved_part, moved_hole = (
         lax.all_to_all(green_particle, "kt", split_axis=3, concat_axis=1, tiled=True),
@@ -87,22 +91,420 @@
     row_start = lax.axis_index("tile") * tile_rows
     coulomb_rows = lax.dynamic_slice_in_dim(coulomb, row_start, tile_rows, 2)
     segment = lax.all_gather(mid_stack, "tile", axis=2, tiled=True)
-    left_real = coulomb_rows[0]
-    left_imag = coulomb_rows[1]
-    more_real, more_imag = complex_batched(left_real, left_imag, segment[0], segment[1])
-    summed = jnp.stack([more_real, more_imag])
-    return coulomb_rows.astype(jnp.float32) + summed
+    more_real, more_imag = complex_batched(coulomb_rows[0], coulomb_rows[1], segment[0], segment[1])
+    return coulomb_rows.astype(jnp.float32) + jnp.stack([more_real, more_imag])
+
+
+ANY = pl.BlockSpec(memory_space=pl.ANY)
+
+
+def dft4(values, sign):
+    (r0, i0), (r1, i1), (r2, i2), (r3, i3) = values
+    er, ei, fr, fi = r0 + r2, i0 + i2, r0 - r2, i0 - i2
+    gr, gi, hr, hi = r1 + r3, i1 + i3, r1 - r3, i1 - i3
+    plus = (fr - hi, fi + hr)
+    minus = (fr + hi, fi - hr)
+    one, three = (plus, minus) if sign > 0 else (minus, plus)
+    return [(er + gr, ei + gi), one, (er - gr, ei - gi), three]
+
+
+def split_call(index, particle, hole, token, count, start, width):
+    _, local, tile_rows, _ = particle.shape
+    rows = tile_rows // count
+    half = local // 2
+
+    def kernel(index_ref, token_ref, *rest):
+        ins, outs = rest[: 2 * count], rest[2 * count :]
+        for shift in range(count):
+            outs[shift][0] = ins[shift][...]
+            outs[shift][1] = ins[count + shift][...]
+
+    def source(shift):
+        return pl.BlockSpec(
+            (2, half, rows, width),
+            lambda j, ix: (0, j, lax.rem(ix[0] + shift, count), start // width),
+        )
+
+    return pl.pallas_call(
+        kernel,
+        grid_spec=pltpu.PrefetchScalarGridSpec(
+            num_scalar_prefetch=1,
+            grid=(2,),
+            in_specs=[ANY] + [source(shift) for shift in range(count)] * 2,
+            out_specs=[pl.BlockSpec((2, 2, half, rows, width), lambda j, ix: (0, 0, j, 0, 0))]
+            * count,
+        ),
+        out_shape=[jax.ShapeDtypeStruct((2, 2, local, rows, width), particle.dtype)] * count,
+    )(index, token, *([particle] * count), *([hole] * count))
+
+
+def polar_kernel(count, local, sizes):
+    groups = len(sizes)
+    group_of = [g for g, size in enumerate(sizes) for _ in range(size)]
+    points = count * local
+    quarter = points // KSIDE
+    low = KSIDE
+    scale = 1.0 / float(points) ** 3
+
+    def kernel(me_ref, token_ref, *rest):
+        pieces = rest[:count]
+        outs = rest[count : count + count * groups]
+        sc = rest[-1]
+        me = me_ref[0]
+        for shift in range(count):
+            base = lax.rem(me + (count - shift), count) * local
+            for which in range(2):
+                for block in range(local // low):
+                    offset = block * low
+                    values = [
+                        (
+                            pieces[shift][which, 0, offset + n].astype(jnp.float32),
+                            pieces[shift][which, 1, offset + n].astype(jnp.float32),
+                        )
+                        for n in range(low)
+                    ]
+                    for n, (real, imag) in enumerate(dft4(values, 1)):
+                        sc[which, 0, base + offset + n] = real
+                        sc[which, 1, base + offset + n] = imag
+
+        def middle_digit(which, sign):
+            def step(t, carry):
+                first = (t // low) * (low * low) + lax.rem(t, low)
+                where = [first + n * low for n in range(KSIDE)]
+                values = [(sc[which, 0, w], sc[which, 1, w]) for w in where]
+                for w, (real, imag) in zip(where, dft4(values, sign)):
+                    sc[which, 0, w] = real
+                    sc[which, 1, w] = imag
+                return carry
+
+            lax.fori_loop(0, quarter, step, 0, unroll=2)
+
+        middle_digit(0, 1)
+        middle_digit(1, 1)
+
+        def high_digit(t, carry):
+            where = [t + n * quarter for n in range(KSIDE)]
+            part = dft4([(sc[0, 0, w], sc[0, 1, w]) for w in where], 1)
+            hole = dft4([(sc[1, 0, w], sc[1, 1, w]) for w in where], 1)
+            cells = [
+                (pr * hr - pi * hi, pr * hi + pi * hr) for (pr, pi), (hr, hi) in zip(part, hole)
+            ]
+            for w, (real, imag) in zip(where, dft4(cells, -1)):
+                sc[0, 0, w] = real
+                sc[0, 1, w] = imag
+            return carry
+
+        lax.fori_loop(0, quarter, high_digit, 0, unroll=2)
+        middle_digit(0, -1)
+        for shift in range(count):
+            base = lax.rem(me + shift, count) * local
+            for block in range(local // low):
+                offset = block * low
+                values = [
+                    (sc[0, 0, base + offset + n], sc[0, 1, base + offset + n]) for n in range(low)
+                ]
+                for n, (real, imag) in enumerate(dft4(values, -1)):
+                    spot = offset + n
+                    group = group_of[spot]
+                    out = outs[shift * groups + group]
+                    place = spot - sum(sizes[:group])
+                    out[0, place] = (real * scale).astype(jnp.bfloat16)
+                    out[1, place] = (imag * scale).astype(jnp.bfloat16)
+
+    return kernel
+
+
+def polar_call(me, token, pieces, sizes):
+    count = len(pieces)
+    _, _, local, rows, width = pieces[0].shape
+    result = pl.pallas_call(
+        polar_kernel(count, local, sizes),
+        grid=(width // LANES, rows // SUB),
+        in_specs=[pl.BlockSpec(memory_space=pltpu.SMEM), ANY]
+        + [pl.BlockSpec((2, 2, local, SUB, LANES), lambda c, r: (0, 0, 0, r, c))] * count,
+        out_specs=[
+            pl.BlockSpec((2, size, SUB, LANES), lambda c, r: (0, 0, r, c)) for size in sizes
+        ]
+        * count,
+        out_shape=[jax.ShapeDtypeStruct((2, size, rows, width), jnp.bfloat16) for size in sizes]
+        * count,
+        scratch_shapes=[pltpu.VMEM((2, 2, count * local, SUB, LANES), jnp.float32)],
+        name="polar",
+    )(me, token, *pieces)
+    groups = len(sizes)
+    return [[result[shift * groups + g] for shift in range(count)] for g in range(groups)]
+
+
+def join_call(token, pieces):
+    count = len(pieces)
+    _, momenta, rows, width = pieces[0].shape
+    steps = 2 if momenta % 2 == 0 else 1
+    part = momenta // steps
+
+    def kernel(token_ref, *rest):
+        for n in range(count):
+            rest[count][n] = rest[n][...]
+
+    return pl.pallas_call(
+        kernel,
+        grid=(steps,),
+        in_specs=[ANY] + [pl.BlockSpec((2, part, rows, width), lambda j: (0, j, 0, 0))] * count,
+        out_specs=pl.BlockSpec((count, 2, part, rows, width), lambda j: (0, 0, j, 0, 0)),
+        out_shape=jax.ShapeDtypeStruct((count,) + pieces[0].shape, pieces[0].dtype),
+        name="join",
+    )(token, *pieces)
+
+
+def dot(left, right):
+    return jnp.dot(left, right, preferred_element_type=jnp.float32)
+
+
+def fill_rows(index_ref, blocks, polar, count, rows, width):
+    me = index_ref[0]
+    for slot, block in enumerate(blocks):
+        first = index_ref[2 + slot] * (count * rows)
+        for shift in range(count):
+            source = lax.rem(me + (count - shift), count)
+            row = pl.multiple_of(first + source * rows, rows)
+            real, imag = block[shift, 0, 0], block[shift, 1, 0]
+            polar[0, pl.ds(row, rows), :width] = real
+            polar[0, pl.ds(row, rows), width:] = imag
+            polar[1, pl.ds(row, rows), :width] = -imag
+            polar[1, pl.ds(row, rows), width:] = real
+
+
+def left_product(mine, polar, width):
+    made = dot(mine[0], polar[0]) + dot(mine[1], polar[1])
+    return made[:, :width].astype(jnp.bfloat16), made[:, width:].astype(jnp.bfloat16)
+
+
+def left_call(index, token, coulomb, blocks):
+    count, _, momenta, rows, width = blocks[0].shape
+    points = coulomb.shape[3]
+    tile_rows = count * rows
+
+    def kernel(index_ref, rows_ref, token_ref, *rest):
+        block_refs, out, polar = rest[: len(blocks)], rest[-2], rest[-1]
+        fill_rows(index_ref, block_refs, polar, count, rows, width)
+        out[0, 0], out[1, 0] = left_product(rows_ref[:, 0], polar, width)
+
+    return pl.pallas_call(
+        kernel,
+        grid_spec=pltpu.PrefetchScalarGridSpec(
+            num_scalar_prefetch=1,
+            grid=(momenta,),
+            in_specs=[
+                pl.BlockSpec((2, 1, tile_rows, points), lambda q, ix: (0, q, ix[1], 0)),
+                ANY,
+            ]
+            + [pl.BlockSpec((count, 2, 1, rows, width), lambda q, ix: (0, 0, q, 0, 0))]
+            * len(blocks),
+            out_specs=pl.BlockSpec((2, 1, tile_rows, width), lambda q, ix: (0, q, 0, 0)),
+            scratch_shapes=[pltpu.VMEM((2, points, 2 * width), jnp.bfloat16)],
+        ),
+        out_shape=jax.ShapeDtypeStruct((2, momenta, tile_rows, width), jnp.bfloat16),
+        name="left",
+    )(index, coulomb, token, *blocks)
+
+
+def screen_call(index, previous, coulomb, lefts, blocks, first):
+    count, _, momenta, rows, width = blocks[0].shape
+    points = coulomb.shape[3]
+    tile_rows = count * rows
+    widths = [left.shape[3] for left in lefts] + [width]
+    out_shape = jax.ShapeDtypeStruct((2, coulomb.shape[1], tile_rows, points), jnp.float32)
+    n_prev = 0 if previous is None else 1
+
+    def kernel(index_ref, coulomb_ref, *rest):
+        rest = rest[n_prev:]
+        left_refs = rest[: len(lefts)]
+        block_refs = rest[len(lefts) : len(lefts) + len(blocks)]
+        out, polar, left = rest[-3], rest[-2], rest[-1]
+        fill_rows(index_ref, block_refs, polar, count, rows, width)
+        row = pl.multiple_of(index_ref[1] * tile_rows, tile_rows)
+        mine = coulomb_ref[:, 0, pl.ds(row, tile_rows), :]
+        last = [left_product(mine, polar, width)]
+        column = 0
+        for w, (real, imag) in zip(widths, [(ref[0, 0], ref[1, 0]) for ref in left_refs] + last):
+            left[0, :, column : column + w] = real
+            left[0, :, points + column : points + column + w] = -imag
+            left[1, :, column : column + w] = imag
+            left[1, :, points + column : points + column + w] = real
+            column += w
+        stacked = coulomb_ref[...].reshape(2 * points, points)
+        made = dot(left[...].reshape(2 * tile_rows, 2 * points), stacked)
+        out[:, 0] = mine.astype(jnp.float32) + made.reshape(2, tile_rows, points)
+
+    return pl.pallas_call(
+        kernel,
+        grid_spec=pltpu.PrefetchScalarGridSpec(
+            num_scalar_prefetch=1,
+            grid=(momenta,),
+            in_specs=[pl.BlockSpec((2, 1, points, points), lambda q, ix: (0, first + q, 0, 0))]
+            + [ANY] * n_prev
+            + [
+                pl.BlockSpec((2, 1, tile_rows, w), lambda q, ix: (0, first + q, 0, 0))
+                for w in widths[:-1]
+            ]
+            + [pl.BlockSpec((count, 2, 1, rows, width), lambda q, ix: (0, 0, q, 0, 0))]
+            * len(blocks),
+            out_specs=pl.BlockSpec(
+                (2, 1, tile_rows, points), lambda q, ix: (0, first + q, 0, 0)
+            ),
+            scratch_shapes=[
+                pltpu.VMEM((2, points, 2 * width), jnp.bfloat16),
+                pltpu.VMEM((2, tile_rows, 2 * points), jnp.bfloat16),
+            ],
+        ),
+        out_shape=out_shape,
+        input_output_aliases={2: 0} if n_prev else {},
+    )(index, coulomb, *([] if previous is None else [previous]), *lefts, *blocks)
+
+
+def order_of(chunks, groups):
+    last = chunks - 1
+    order = [("split", n, 0) for n in range(min(2, chunks))]
+    for n in range(chunks):
+        order.append(("transform", n, 0))
+        if n + 2 < chunks:
+            order.append(("split", n + 2, 0))
+        if n >= 2:
+            order.append(("ahead", n - 2, 0))
+        if n >= 1:
+            order.append(("join", n - 1, 0))
+        if n >= 2:
+            order.append(("left", n - 2, 0))
+    order += [("join", last, 0), ("ahead", last - 1, 0), ("left", last - 1, 0)]
+    order += [("join", last, g) for g in range(1, groups)]
+    for g in range(groups):
+        order += [("ahead", last, g), ("screen", last, g)]
+    return order
+
+
+def pipelined(count, tiles, plan, sizes):
+    chips = tiles // 2
+
+    def exchange(pieces):
+        arrived = [pieces[0]] + [None] * (count - 1)
+        for shift in sorted(range(1, count), key=lambda shift: abs(2 * shift - count)):
+            arrived[shift] = lax.ppermute(
+                pieces[shift], "kt", [(d, (d + shift) % count) for d in range(count)]
+            )
+        return arrived
+
+    def across_chips(block):
+        return [block] + [
+            lax.ppermute(
+                block,
+                "tile",
+                [(t, ((t // 2 + shift) % chips) * 2 + t % 2) for t in range(tiles)],
+            )
+            for shift in range(1, chips)
+        ]
+
+    def across_cores(block):
+        return lax.ppermute(block, "tile", [(t, t ^ 1) for t in range(tiles)])
+
+    def body(particle, hole, coulomb):
+        me = lax.axis_index("kt").astype(jnp.int32)
+        tile = lax.axis_index("tile").astype(jnp.int32)
+        slots = [
+            lax.rem(tile // 2 + (chips - shift), chips) * 2 + (lax.rem(tile, 2) + core) % 2
+            for core in range(2)
+            for shift in range(chips)
+        ]
+        me_only = me.reshape(1)
+        index = jnp.stack([me, tile] + slots).astype(jnp.int32)
+        starts = [sum(plan[:n]) for n in range(len(plan))]
+        last = len(plan) - 1
+        everything = [coulomb.shape[1]]
+        green, polar, near, over, lefts = {}, {}, {}, {}, {}
+
+        def send_green(n, token):
+            pieces = split_call(index, particle, hole, token, count, starts[n], plan[n])
+            green[n] = exchange(pieces)
+            return pieces[0]
+
+        def send_polar(n, token):
+            made = polar_call(me_only, token, green[n], sizes if n == last else everything)
+            polar[n] = [exchange(pieces) for pieces in made]
+            return made[0][0]
+
+        def send_rows(n, g, token):
+            block = join_call(token, polar[n][g])
+            near[n, g] = across_chips(block)
+            over[n, g] = [across_cores(block)]
+            return block
+
+        def forward_rows(n, g, token):
+            for block in near[n, g][1:]:
+                over[n, g].append(across_cores(block))
+            return token
+
+        def take_left(n, g, token):
+            lefts[n] = left_call(index, token, coulomb, near[n, 0] + over[n, 0])
+            return lefts[n]
+
+        def screen(n, g, token):
+            before = [lefts[m] for m in range(last)]
+            return screen_call(
+                index, token, coulomb, before, near[n, g] + over[n, g], sum(sizes[:g])
+            )
+
+        token = me_only
+        steps = {"split": send_green, "transform": send_polar}
+        rows_steps = {
+            "join": send_rows,
+            "ahead": forward_rows,
+            "left": take_left,
+            "screen": screen,
+        }
+        out = None
+        for kind, n, g in order_of(len(plan), len(sizes)):
+            if kind in steps:
+                token = steps[kind](n, token)
+            elif kind == "screen":
+                out = screen(n, g, out)
+            else:
+                token = rows_steps[kind](n, g, token)
+        return out
+
+    return body
 
 
 def solution(mesh):
-    return jax.shard_map(
-        body,
-        mesh=mesh,
-        in_specs=(
-            P(None, "kt", "tile", None),
-            P(None, "kt", "tile", None),
-            P(None, "kt", None, None),
-        ),
-        out_specs=P(None, "kt", "tile", None),
-        check_vma=False,
-    )
+    count, tiles = mesh.shape["kt"], mesh.shape["tile"]
+
+    def sharded(body):
+        return jax.shard_map(
+            body,
+            mesh=mesh,
+            in_specs=(
+                P(None, "kt", "tile", None),
+                P(None, "kt", "tile", None),
+                P(None, "kt", None, None),
+            ),
+            out_specs=P(None, "kt", "tile", None),
+            check_vma=False,
+        )
+
+    def step(particle, hole, coulomb):
+        _, points_k, points, _ = particle.shape
+        local, tile_rows = points_k // count, points // tiles
+        fits = (
+            points_k == KSIDE**3
+            and local % KSIDE == 0
+            and tile_rows % (count * SUB) == 0
+            and points % (2 * LANES) == 0
+            and points >= 4 * LANES
+            and tiles % 2 == 0
+            and tiles > 2
+        )
+        if not fits:
+            return sharded(generic_body)(particle, hole, coulomb)
+        plan = [2 * LANES] * (points // (2 * LANES) - 1) + [LANES, LANES]
+        sizes = [local - local // 4, local // 4]
+        whole = sharded(pipelined(count, tiles, plan, sizes))
+        return whole(particle, hole, coulomb)
+
+    return step

time: 1120 us -> 780 us (0.70)
  starting transfers between devices: 12.4 us -> 350 us
  matrix products: 269 us -> 0 us
  waiting for transfers between devices: 507 us -> 266 us
  blocking collectives: 188 us -> 0 us
  Pallas kernels: 0 us -> 153 us
  local copies, waits for them, and re-layouts: 99.5 us -> 8.41 us
  other arithmetic: 27.4 us -> 0 us
  between operations: 13.8 us -> 0.98 us
    ppermute x0 -> x95, starting transfers between devices: none -> 350 us  [the longest x77 344 us: exchange(): lax.ppermute(pieces[shift], 'kt', [(d, (d + shift) % count) for d in rang...]
    all_to_all x2 -> x0, waiting for transfers between devices: 307 us -> none  [the longest x1 171 us: body(): lax.all_to_all(green_particle, 'kt', split_axis=3, concat_axis=1, tiled=T...]
    dot_general x20 -> x0, matrix products: 269 us -> none  [the longest x8 122 us: product_of(): jnp.einsum('kij,kjl->kil', left_side, right_side, preferred_element_type=...]
    ppermute x0 -> x95, waiting for transfers between devices: none -> 266 us  [the longest x77 221 us: exchange(): lax.ppermute(pieces[shift], 'kt', [(d, (d + shift) % count) for d in rang...]
    all_gather x1 -> x0, waiting for transfers between devices: 201 us -> none  [body(): segment = lax.all_gather(mid_stack, 'tile', axis=2, tiled=True)]
    all_to_all x1 -> x0, blocking collectives: 188 us -> none  [body(): lax.all_to_all(polar_q, 'kt', split_axis=1, concat_axis=3, tiled=True)]
    pallas_call x0 -> x22, Pallas kernels: none -> 153 us  [the longest x4 47.9 us: left_call(): pl.pallas_call(kernel, grid_spec=pltpu.PrefetchScalarGridSpec(num_scalar_...]
    all_to_all x3 -> x0, local copies, waits for them, and re-layouts: 38.6 us -> none  [the longest x1 13.9 us: body(): lax.all_to_all(polar_q, 'kt', split_axis=1, concat_axis=3, tiled=True)]
  transfers between devices with their start and end apart: 3 -> 95, of which waited for: 3 -> 35; matrix products, arithmetic and copies ran while one was open for 5% -> 0% of each run, Pallas kernels for 0% -> 17%
where the time goes in v1:
time: 780 us; the launch traced here: 778 us
  starting transfers between devices  350 us (45%)
  waiting for transfers between devices  266 us (34%)
  Pallas kernels  153 us (20%)
  local copies, waits for them, and re-layouts  8.41 us (1%)
    ppermute x77, starting transfers between devices, exchange(): lax.ppermute(pieces[shift], 'kt', [(d, (d + shift) % count) for d in rang...  344 us
    ppermute x77, waiting for transfers between devices, exchange(): lax.ppermute(pieces[shift], 'kt', [(d, (d + shift) % count) for d in rang...  221 us
    pallas_call x4, Pallas kernels, left_call(): pl.pallas_call(kernel, grid_spec=pltpu.PrefetchScalarGridSpec(num_scalar_...  47.9 us
    ppermute x6, waiting for transfers between devices, across_chips(): lax.ppermute(block, 'tile', [(t, (t // 2 + shift) % chips * 2 + t % 2) fo...  44.2 us
    pallas_call x5, Pallas kernels, polar_call(): pl.pallas_call(polar_kernel(count, local, sizes), grid=(width // LANES, r...  35 us
    pallas_call x2, Pallas kernels, screen_call(): pl.pallas_call(kernel, grid_spec=pltpu.PrefetchScalarGridSpec(num_scalar_...  34 us
    pallas_call x5, Pallas kernels, split_call(): pl.pallas_call(kernel, grid_spec=pltpu.PrefetchScalarGridSpec(num_scalar_...  21.6 us
  transfers between devices with their start and end apart: 95, of which 35 were waited for; matrix products, arithmetic and copies ran while one was open for 0% of the time, Pallas kernels for 17%

profile of v1, /device:TPU:0, one launch (start us, length us, event | category | flops | bytes accessed | tf_op | source)
XLA Modules:
  0.0 778.0 jit_solution(8569266134341499306)
XLA Ops:
  16.3 8.2 %collective-permute-done.rest_1_ = bf16[2,2,8,32,256]{4,3,2,1,0:T(8,128)(2,1)S(1)} collective-permute-done((bf16[2,2,8,32,256]{4,3,2,1,0:T(8,128)(2,1)}, bf16[2,2,8,32,256]{4,3,2,1,0:T(8,128)(2,1)S(1)}, u32[]{:S(2)}, u32[]{:S(2)}) %collective-permute-start) | collective-permute-done | bytes 524320 | tf_op jit(solution)/shard_map/ppermute | solution.py:390
  31.1 5.7 collective-permute-start.6
  36.8 31.8 %collective-permute-done.2.rest_3_ = bf16[2,2,8,32,256]{4,3,2,1,0:T(8,128)(2,1)S(1)} collective-permute-done((bf16[2,2,8,32,256]{4,3,2,1,0:T(8,128)(2,1)}, bf16[2,2,8,32,256]{4,3,2,1,0:T(8,128)(2,1)S(1)}, u32[]{:S(2)}, u32[]{:S(2)}) %collective-permute-start.2) | collective-permute-done | bytes 524320 | tf_op jit(solution)/shard_map/ppermute | solution.py:390
  69.4 22.1 %collective-permute-start.8 = (bf16[2,2,8,32,256]{4,3,2,1,0:T(8,128)(2,1)}, bf16[2,2,8,32,256]{4,3,2,1,0:T(8,128)(2,1)S(1)}, u32[]{:S(2)}, u32[]{:S(2)}) collective-permute-start(bf16[2,2,8,32,256]{4,3,2,1,0:T(8,128)(2,1)} %get-tuple-element.105), channel_id=1, source_target_pairs={{0,8},{4,12},{8,16},{12,20},{16,24},{20,28},{24,0},{28,4},{1,9},{5... | collective-permute-start | bytes 1572872 | tf_op jit(solution)/shard_map/ppermute | solution.py:390
  91.5 11.4 %collective-permute-start.9 = (bf16[2,2,8,32,256]{4,3,2,1,0:T(8,128)(2,1)}, bf16[2,2,8,32,256]{4,3,2,1,0:T(8,128)(2,1)S(1)}, u32[]{:S(2)}, u32[]{:S(2)}) collective-permute-start(bf16[2,2,8,32,256]{4,3,2,1,0:T(8,128)(2,1)} %get-tuple-element.106), channel_id=1, source_target_pairs={{0,12},{4,16},{8,20},{12,24},{16,28},{20,0},{24,4},{28,8},{1,13},{... | collective-permute-start | bytes 1572872 | tf_op jit(solution)/shard_map/ppermute | solution.py:390
  107.1 29.4 %collective-permute-start.11 = (bf16[2,2,8,32,256]{4,3,2,1,0:T(8,128)(2,1)}, bf16[2,2,8,32,256]{4,3,2,1,0:T(8,128)(2,1)S(1)}, u32[]{:S(2)}, u32[]{:S(2)}) collective-permute-start(bf16[2,2,8,32,256]{4,3,2,1,0:T(8,128)(2,1)} %get-tuple-element.108), channel_id=1, source_target_pairs={{0,20},{4,24},{8,28},{12,0},{16,4},{20,8},{24,12},{28,16},{1,21},{... | collective-permute-start | bytes 1572872 | tf_op jit(solution)/shard_map/ppermute | solution.py:390
  140.2 8.3 %polar.5 = (bf16[2,8,32,256]{3,2,1,0:T(8,128)(2,1)}, bf16[2,8,32,256]{3,2,1,0:T(8,128)(2,1)}, bf16[2,8,32,256]{3,2,1,0:T(8,128)(2,1)}, bf16[2,8,32,256]{3,2,1,0:...) custom-call(s32[1]{0:T(128)} %bitcast.token_ref.me_ref, ...), custom_call_target="tpu_custom_call" | custom-call | tf_op jit(solution)/shard_map/polar/pallas_call | solution.py:220
  148.5 10.1 %collective-permute-done.9.rest_3_ = bf16[2,2,8,32,256]{4,3,2,1,0:T(8,128)(2,1)S(1)} collective-permute-done((bf16[2,2,8,32,256]{4,3,2,1,0:T(8,128)(2,1)}, bf16[2,2,8,32,256]{4,3,2,1,0:T(8,128)(2,1)S(1)}, u32[]{:S(2)}, u32[]{:S(2)}) %collective-permute-start.9) | collective-permute-done | bytes 524320 | tf_op jit(solution)/shard_map/ppermute | solution.py:390
  158.9 22.6 %collective-permute-start.15 = (bf16[2,8,32,256]{3,2,1,0:T(8,128)(2,1)}, bf16[2,8,32,256]{3,2,1,0:T(8,128)(2,1)S(1)}, u32[]{:S(2)}, u32[]{:S(2)}) collective-permute-start(bf16[2,8,32,256]{3,2,1,0:T(8,128)(2,1)} %get-tuple-element.114), channel_id=1, source_target_pairs={{0,8},{4,12},{8,16},{12,20},{16,24},{20,28},{24,0},{28,4},{1,9},{5... | collective-permute-start | bytes 786440 | tf_op jit(solution)/shard_map/ppermute | solution.py:390
  181.5 10.8 %collective-permute-start.16 = (bf16[2,8,32,256]{3,2,1,0:T(8,128)(2,1)}, bf16[2,8,32,256]{3,2,1,0:T(8,128)(2,1)S(1)}, u32[]{:S(2)}, u32[]{:S(2)}) collective-permute-start(bf16[2,8,32,256]{3,2,1,0:T(8,128)(2,1)} %get-tuple-element.115), channel_id=1, source_target_pairs={{0,12},{4,16},{8,20},{12,24},{16,28},{20,0},{24,4},{28,8},{1,13},{... | collective-permute-start | bytes 786440 | tf_op jit(solution)/shard_map/ppermute | solution.py:390
  196.9 12.2 %collective-permute-start.18 = (bf16[2,8,32,256]{3,2,1,0:T(8,128)(2,1)}, bf16[2,8,32,256]{3,2,1,0:T(8,128)(2,1)S(1)}, u32[]{:S(2)}, u32[]{:S(2)}) collective-permute-start(bf16[2,8,32,256]{3,2,1,0:T(8,128)(2,1)} %get-tuple-element.117), channel_id=1, source_target_pairs={{0,20},{4,24},{8,28},{12,0},{16,4},{20,8},{24,12},{28,16},{1,21},{... | collective-permute-start | bytes 786440 | tf_op jit(solution)/shard_map/ppermute | solution.py:390
  218.8 8.3 %polar.6 = (bf16[2,8,32,256]{3,2,1,0:T(8,128)(2,1)}, bf16[2,8,32,256]{3,2,1,0:T(8,128)(2,1)}, bf16[2,8,32,256]{3,2,1,0:T(8,128)(2,1)}, bf16[2,8,32,256]{3,2,1,0:...) custom-call(s32[1]{0:T(128)} %bitcast.token_ref.me_ref, ...), custom_call_target="tpu_custom_call" | custom-call | tf_op jit(solution)/shard_map/polar/pallas_call | solution.py:220
  238.2 6.2 collective-permute-start.29
  252.3 6.0 collective-permute-start.21
  258.3 16.3 %collective-permute-done.30.rest_3_ = bf16[2,8,32,256]{3,2,1,0:T(8,128)(2,1)S(1)} collective-permute-done((bf16[2,8,32,256]{3,2,1,0:T(8,128)(2,1)S(1)}, bf16[2,8,32,256]{3,2,1,0:T(8,128)(2,1)S(1)}, u32[]{:S(2)}, u32[]{:S(2)}) %collective-permute-start.30) | collective-permute-done | bytes 262176 | tf_op jit(solution)/shard_map/ppermute | solution.py:390
  274.6 6.9 collective-permute-start.33
  281.5 11.2 %collective-permute-start.34 = (bf16[2,8,32,256]{3,2,1,0:T(8,128)(2,1)}, bf16[2,8,32,256]{3,2,1,0:T(8,128)(2,1)S(1)}, u32[]{:S(2)}, u32[]{:S(2)}) collective-permute-start(bf16[2,8,32,256]{3,2,1,0:T(8,128)(2,1)} %get-tuple-element.135), channel_id=1, source_target_pairs={{0,28},{4,0},{8,4},{12,8},{16,12},{20,16},{24,20},{28,24},{1,29},{... | collective-permute-start | bytes 786440 | tf_op jit(solution)/shard_map/ppermute | solution.py:390
  299.2 30.6 %collective-permute-start.23 = (bf16[2,2,8,32,256]{4,3,2,1,0:T(8,128)(2,1)}, bf16[2,2,8,32,256]{4,3,2,1,0:T(8,128)(2,1)}, u32[]{:S(2)}, u32[]{:S(2)}) collective-permute-start(bf16[2,2,8,32,256]{4,3,2,1,0:T(8,128)(2,1)} %get-tuple-element.122), channel_id=1, source_target_pairs={{0,12},{4,16},{8,20},{12,24},{16,28},{20,0},{24,4},{28,8},{1,13},{... | collective-permute-start | bytes 1572872 | tf_op jit(solution)/shard_map/ppermute | solution.py:390
  330.4 14.2 %collective-permute-start.25 = (bf16[2,2,8,32,256]{4,3,2,1,0:T(8,128)(2,1)}, bf16[2,2,8,32,256]{4,3,2,1,0:T(8,128)(2,1)}, u32[]{:S(2)}, u32[]{:S(2)}) collective-permute-start(bf16[2,2,8,32,256]{4,3,2,1,0:T(8,128)(2,1)} %get-tuple-element.124), channel_id=1, source_target_pairs={{0,20},{4,24},{8,28},{12,0},{16,4},{20,8},{24,12},{28,16},{1,21},{... | collective-permute-start | bytes 1572872 | tf_op jit(solution)/shard_map/ppermute | solution.py:390
  344.7 8.5 %collective-permute-done.23.rest_3_ = bf16[2,2,8,32,256]{4,3,2,1,0:T(8,128)(2,1)} collective-permute-done((bf16[2,2,8,32,256]{4,3,2,1,0:T(8,128)(2,1)}, bf16[2,2,8,32,256]{4,3,2,1,0:T(8,128)(2,1)}, u32[]{:S(2)}, u32[]{:S(2)}) %collective-permute-start.23) | collective-permute-done | bytes 524320 | tf_op jit(solution)/shard_map/ppermute | solution.py:390
  353.2 48.2 %collective-permute-start.26 = (bf16[2,2,8,32,256]{4,3,2,1,0:T(8,128)(2,1)}, bf16[2,2,8,32,256]{4,3,2,1,0:T(8,128)(2,1)}, u32[]{:S(2)}, u32[]{:S(2)}) collective-permute-start(bf16[2,2,8,32,256]{4,3,2,1,0:T(8,128)(2,1)} %get-tuple-element.125), channel_id=1, source_target_pairs={{0,24},{4,28},{8,0},{12,4},{16,8},{20,12},{24,16},{28,20},{1,25},{... | collective-permute-start | bytes 1572872 | tf_op jit(solution)/shard_map/ppermute | solution.py:390
  401.4 10.6 %collective-permute-start.27 = (bf16[2,2,8,32,256]{4,3,2,1,0:T(8,128)(2,1)}, bf16[2,2,8,32,256]{4,3,2,1,0:T(8,128)(2,1)}, u32[]{:S(2)}, u32[]{:S(2)}) collective-permute-start(bf16[2,2,8,32,256]{4,3,2,1,0:T(8,128)(2,1)} %get-tuple-element.126), channel_id=1, source_target_pairs={{0,28},{4,0},{8,4},{12,8},{16,12},{20,16},{24,20},{28,24},{1,29},{... | collective-permute-start | bytes 1572872 | tf_op jit(solution)/shard_map/ppermute | solution.py:390
  412.0 12.5 %collective-permute-done.27.rest_7_ = bf16[2,2,8,32,256]{4,3,2,1,0:T(8,128)(2,1)} collective-permute-done((bf16[2,2,8,32,256]{4,3,2,1,0:T(8,128)(2,1)}, bf16[2,2,8,32,256]{4,3,2,1,0:T(8,128)(2,1)}, u32[]{:S(2)}, u32[]{:S(2)}) %collective-permute-start.27) | collective-permute-done | bytes 524320 | tf_op jit(solution)/shard_map/ppermute | solution.py:390
  424.6 8.2 %polar.7 = (bf16[2,8,32,256]{3,2,1,0:T(8,128)(2,1)}, bf16[2,8,32,256]{3,2,1,0:T(8,128)(2,1)}, bf16[2,8,32,256]{3,2,1,0:T(8,128)(2,1)}, bf16[2,8,32,256]{3,2,1,0:...) custom-call(s32[1]{0:T(128)} %bitcast.token_ref.me_ref, ...), custom_call_target="tpu_custom_call" | custom-call | tf_op jit(solution)/shard_map/polar/pallas_call | solution.py:220
  442.6 6.6 collective-permute-done.41.rest_4_
  449.2 6.3 collective-permute-start.43
  455.5 11.9 %collective-permute-start.44 = (bf16[2,2,8,32,128]{4,3,2,1,0:T(8,128)(2,1)S(1)}, bf16[2,2,8,32,128]{4,3,2,1,0:T(8,128)(2,1)S(1)}, u32[]{:S(2)}, u32[]{:S(2)}) collective-permute-start(bf16[2,2,8,32,128]{4,3,2,1,0:T(8,128)(2,1)S(1)} %copy-done.69), channel_id=1, source_target_pairs={{0,28},{4,0},{8,4},{12,8},{16,12},{20,16},{24,20},{28,24},{1,29},{... | collective-permute-start | bytes 786440 | tf_op jit(solution)/shard_map/ppermute | solution.py:390
  467.5 5.7 collective-permute-done.44.rest_7_
  478.3 8.6 %collective-permute-done.46.rest_2_ = bf16[2,8,32,256]{3,2,1,0:T(8,128)(2,1)S(1)} collective-permute-done((bf16[2,8,32,256]{3,2,1,0:T(8,128)(2,1)}, bf16[2,8,32,256]{3,2,1,0:T(8,128)(2,1)S(1)}, u32[]{:S(2)}, u32[]{:S(2)}) %collective-permute-start.46) | collective-permute-done | bytes 262176 | tf_op jit(solution)/shard_map/ppermute | solution.py:390
  487.1 15.1 %collective-permute-done.47.rest_3_ = bf16[2,8,32,256]{3,2,1,0:T(8,128)(2,1)S(1)} collective-permute-done((bf16[2,8,32,256]{3,2,1,0:T(8,128)(2,1)}, bf16[2,8,32,256]{3,2,1,0:T(8,128)(2,1)S(1)}, u32[]{:S(2)}, u32[]{:S(2)}) %collective-permute-start.47) | collective-permute-done | bytes 262176 | tf_op jit(solution)/shard_map/ppermute | solution.py:390
  503.4 12.5 %left.4.token_ref.rest_0_.rest_1_ = bf16[2,8,256,256]{3,2,1,0:T(8,128)(2,1)} custom-call(s32[6]{0:T(128)} %stack.27.index_ref, bf16[2,8,1024,1024]{3,2,1,0:T(8,128)(2,1)} %coulomb_ref.3, bf16[8,2,8,32,256]{4,3,2,1,0:T(8,128)(2,1)} %join.7.token_ref.rest_0_, bf16[8,2,8,32,256]{4,3,2,1,0:T(8,128)(2,1)} %join.6.token_ref.rest_0_, ...), custom_call_target="tpu_custom_call" | custom-call | tf_op jit(solution)/shard_map/left/pallas_call | solution.py:291
  532.4 5.6 collective-permute-done.55.rest_1_
  540.5 19.4 %collective-permute-done.57.rest_3_ = bf16[2,2,8,32,128]{4,3,2,1,0:T(8,128)(2,1)S(1)} collective-permute-done((bf16[2,2,8,32,128]{4,3,2,1,0:T(8,128)(2,1)S(1)}, bf16[2,2,8,32,128]{4,3,2,1,0:T(8,128)(2,1)S(1)}, u32[]{:S(2)}, u32[]{:S(2)}) %collective-permute-start.57) | collective-permute-done | bytes 262176 | tf_op jit(solution)/shard_map/ppermute | solution.py:390
  560.0 11.9 %collective-permute-done.69.rest_1_ = bf16[8,2,8,32,256]{4,3,2,1,0:T(8,128)(2,1)} collective-permute-done((bf16[8,2,8,32,256]{4,3,2,1,0:T(8,128)(2,1)}, bf16[8,2,8,32,256]{4,3,2,1,0:T(8,128)(2,1)}, u32[]{:S(2)}, u32[]{:S(2)}) %collective-permute-start.69) | collective-permute-done | bytes 2097184 | tf_op jit(solution)/shard_map/ppermute | solution.py:397
  576.3 6.5 collective-permute-done.60.rest_6_
  587.7 5.6 collective-permute-done.61.rest_7_
  605.2 7.6 collective-permute-done.64.rest_3_
  617.0 12.5 %left.5.token_ref.rest_1_.rest_2_ = bf16[2,8,256,256]{3,2,1,0:T(8,128)(2,1)} custom-call(s32[6]{0:T(128)} %stack.27.index_ref, bf16[2,8,1024,1024]{3,2,1,0:T(8,128)(2,1)} %coulomb_ref.3, bf16[8,2,8,32,256]{4,3,2,1,0:T(8,128)(2,1)} %join.8.token_ref.rest_0_, bf16[8,2,8,32,256]{4,3,2,1,0:T(8,128)(2,1)} %join.7.token_ref.rest_0_, ...), custom_call_target="tpu_custom_call" | custom-call | tf_op jit(solution)/shard_map/left/pallas_call | solution.py:291
  646.8 7.9 %collective-permute-done.74.rest_3_ = bf16[2,6,32,128]{3,2,1,0:T(8,128)(2,1)S(1)} collective-permute-done((bf16[2,6,32,128]{3,2,1,0:T(8,128)(2,1)S(1)}, bf16[2,6,32,128]{3,2,1,0:T(8,128)(2,1)S(1)}, u32[]{:S(2)}, u32[]{:S(2)}) %collective-permute-start.74) | collective-permute-done | bytes 98336 | tf_op jit(solution)/shard_map/ppermute | solution.py:390
  654.9 7.0 collective-permute-done.79.rest_1_
  662.7 12.5 %left.6.token_ref.rest_2_.rest_3_ = bf16[2,8,256,256]{3,2,1,0:T(8,128)(2,1)} custom-call(s32[6]{0:T(128)} %stack.27.index_ref, bf16[2,8,1024,1024]{3,2,1,0:T(8,128)(2,1)} %coulomb_ref.3, bf16[8,2,8,32,128]{4,3,2,1,0:T(8,128)(2,1)} %join.9.token_ref.rest_0_, bf16[8,2,8,32,256]{4,3,2,1,0:T(8,128)(2,1)} %join.8.token_ref.rest_0_, ...), custom_call_target="tpu_custom_call" | custom-call | tf_op jit(solution)/shard_map/left/pallas_call | solution.py:291
  677.9 19.3 %collective-permute-done.82.rest_5_ = bf16[8,2,6,32,128]{4,3,2,1,0:T(8,128)(2,1)} collective-permute-done((bf16[8,2,6,32,128]{4,3,2,1,0:T(8,128)(2,1)}, bf16[8,2,6,32,128]{4,3,2,1,0:T(8,128)(2,1)}, u32[]{:S(2)}, u32[]{:S(2)}) %collective-permute-start.82) | collective-permute-done | bytes 786464 | tf_op jit(solution)/shard_map/ppermute | solution.py:397
  703.8 5.7 collective-permute-done.86.rest_2_
  709.6 5.9 collective-permute-done.87.rest_3_
  723.2 10.3 %left.7.rest_3_.token_ref.rest_4_ = bf16[2,8,256,128]{3,2,1,0:T(8,128)(2,1)} custom-call(s32[6]{0:T(128)} %stack.27.index_ref, bf16[2,8,1024,1024]{3,2,1,0:T(8,128)(2,1)} %coulomb_ref.3, bf16[8,2,6,32,128]{4,3,2,1,0:T(8,128)(2,1)} %join.10.token_ref.rest_4_, bf16[8,2,8,32,128]{4,3,2,1,0:T(8,128)(2,1)} %join.9.token_ref.rest_0_, ...), custom_call_target="tpu_custom_call" | custom-call | tf_op jit(solution)/shard_map/left/pallas_call | solution.py:291
  736.5 6.0 collective-permute-done.92.rest_6_
  742.5 23.4 %shard_map.42.rest_0_ = f32[2,8,256,1024]{3,2,1,0:T(8,128)} custom-call(s32[6]{0:T(128)} %stack.27.index_ref, bf16[2,8,1024,1024]{3,2,1,0:T(8,128)(2,1)} %coulomb_ref.3, bf16[2,8,256,256]{3,2,1,0:T(8,128)(2,1)} %left.4.token_ref.rest_0_.rest_1_, bf16[2,8,256,256]{3,2,1,0:T(8,128)(2,1)} %left.5.token_ref.rest_1_.rest_2_, ...), custom_call_target="tpu_custom_call" | custom-call | tf_op jit(solution)/shard_map/pallas_call | solution.py:338
  767.3 10.6 %shard_map.43 = f32[2,8,256,1024]{3,2,1,0:T(8,128)} custom-call(s32[6]{0:T(128)} %stack.27.index_ref, bf16[2,8,1024,1024]{3,2,1,0:T(8,128)(2,1)} %coulomb_ref.3, f32[2,8,256,1024]{3,2,1,0:T(8,128)} %shard_map.42.rest_0_, bf16[2,8,256,256]{3,2,1,0:T(8,128)(2,1)} %left.4.token_ref.rest_0_.rest_1_, ...), custom_call_target="tpu_custom_call", output_to_operand_aliasing={{}: (2, {})} | custom-call | tf_op jit(solution)/shard_map/pallas_call | solution.py:338
  (345 shorter events, 171.9 us)
Async XLA Ops:
  9.9 58.7 %collective-permute-start.2 = (bf16[2,2,8,32,256]{4,3,2,1,0:T(8,128)(2,1)}, bf16[2,2,8,32,256]{4,3,2,1,0:T(8,128)(2,1)S(1)}, u32[]{:S(2)}, u32[]{:S(2)}) collective-permute-start(bf16[2,2,8,32,256]{4,3,2,1,0:T(8,128)(2,1)} %get-tuple-element.97), channel_id=1, source_target_pairs={{0,12},{4,16},{8,20},{12,24},{16,28},{20,0},{24,4},{28,8},{1,13},{... | collective-permute-start | bytes 1572872 | tf_op jit(solution)/shard_map/ppermute | solution.py:390
  12.4 56.4 %collective-permute-start.3 = (bf16[2,2,8,32,256]{4,3,2,1,0:T(8,128)(2,1)}, bf16[2,2,8,32,256]{4,3,2,1,0:T(8,128)(2,1)S(1)}, u32[]{:S(2)}, u32[]{:S(2)}) collective-permute-start(bf16[2,2,8,32,256]{4,3,2,1,0:T(8,128)(2,1)} %get-tuple-element.98), channel_id=1, source_target_pairs={{0,16},{4,20},{8,24},{12,28},{16,0},{20,4},{24,8},{28,12},{1,17},{... | collective-permute-start | bytes 1572872 | tf_op jit(solution)/shard_map/ppermute | solution.py:390
  13.7 77.9 %collective-permute-start.4 = (bf16[2,2,8,32,256]{4,3,2,1,0:T(8,128)(2,1)}, bf16[2,2,8,32,256]{4,3,2,1,0:T(8,128)(2,1)S(1)}, u32[]{:S(2)}, u32[]{:S(2)}) collective-permute-start(bf16[2,2,8,32,256]{4,3,2,1,0:T(8,128)(2,1)} %get-tuple-element.99), channel_id=1, source_target_pairs={{0,20},{4,24},{8,28},{12,0},{16,4},{20,8},{24,12},{28,16},{1,21},{... | collective-permute-start | bytes 1572872 | tf_op jit(solution)/shard_map/ppermute | solution.py:390
  24.5 78.4 %collective-permute-start.5 = (bf16[2,2,8,32,256]{4,3,2,1,0:T(8,128)(2,1)}, bf16[2,2,8,32,256]{4,3,2,1,0:T(8,128)(2,1)S(1)}, u32[]{:S(2)}, u32[]{:S(2)}) collective-permute-start(bf16[2,2,8,32,256]{4,3,2,1,0:T(8,128)(2,1)} %get-tuple-element.100), channel_id=1, source_target_pairs={{0,24},{4,28},{8,0},{12,4},{16,8},{20,12},{24,16},{28,20},{1,25},{... | collective-permute-start | bytes 1572872 | tf_op jit(solution)/shard_map/ppermute | solution.py:390
  31.1 76.0 %collective-permute-start.6 = (bf16[2,2,8,32,256]{4,3,2,1,0:T(8,128)(2,1)}, bf16[2,2,8,32,256]{4,3,2,1,0:T(8,128)(2,1)S(1)}, u32[]{:S(2)}, u32[]{:S(2)}) collective-permute-start(bf16[2,2,8,32,256]{4,3,2,1,0:T(8,128)(2,1)} %get-tuple-element.101), channel_id=1, source_target_pairs={{0,28},{4,0},{8,4},{12,8},{16,12},{20,16},{24,20},{28,24},{1,29},{... | collective-permute-start | bytes 1572872 | tf_op jit(solution)/shard_map/ppermute | solution.py:390
  68.6 67.9 %collective-permute-start.7 = (bf16[2,2,8,32,256]{4,3,2,1,0:T(8,128)(2,1)}, bf16[2,2,8,32,256]{4,3,2,1,0:T(8,128)(2,1)S(1)}, u32[]{:S(2)}, u32[]{:S(2)}) collective-permute-start(bf16[2,2,8,32,256]{4,3,2,1,0:T(8,128)(2,1)} %get-tuple-element.104), channel_id=1, source_target_pairs={{0,4},{4,8},{8,12},{12,16},{16,20},{20,24},{24,28},{28,0},{1,5},{5... | collective-permute-start | bytes 1572872 | tf_op jit(solution)/shard_map/ppermute | solution.py:390
  69.4 70.7 %collective-permute-start.8 = (bf16[2,2,8,32,256]{4,3,2,1,0:T(8,128)(2,1)}, bf16[2,2,8,32,256]{4,3,2,1,0:T(8,128)(2,1)S(1)}, u32[]{:S(2)}, u32[]{:S(2)}) collective-permute-start(bf16[2,2,8,32,256]{4,3,2,1,0:T(8,128)(2,1)} %get-tuple-element.105), channel_id=1, source_target_pairs={{0,8},{4,12},{8,16},{12,20},{16,24},{20,28},{24,0},{28,4},{1,9},{5... | collective-permute-start | bytes 1572872 | tf_op jit(solution)/shard_map/ppermute | solution.py:390
  91.5 67.1 %collective-permute-start.9 = (bf16[2,2,8,32,256]{4,3,2,1,0:T(8,128)(2,1)}, bf16[2,2,8,32,256]{4,3,2,1,0:T(8,128)(2,1)S(1)}, u32[]{:S(2)}, u32[]{:S(2)}) collective-permute-start(bf16[2,2,8,32,256]{4,3,2,1,0:T(8,128)(2,1)} %get-tuple-element.106), channel_id=1, source_target_pairs={{0,12},{4,16},{8,20},{12,24},{16,28},{20,0},{24,4},{28,8},{1,13},{... | collective-permute-start | bytes 1572872 | tf_op jit(solution)/shard_map/ppermute | solution.py:390
  103.0 55.9 %collective-permute-start.10 = (bf16[2,2,8,32,256]{4,3,2,1,0:T(8,128)(2,1)}, bf16[2,2,8,32,256]{4,3,2,1,0:T(8,128)(2,1)S(1)}, u32[]{:S(2)}, u32[]{:S(2)}) collective-permute-start(bf16[2,2,8,32,256]{4,3,2,1,0:T(8,128)(2,1)} %get-tuple-element.107), channel_id=1, source_target_pairs={{0,16},{4,20},{8,24},{12,28},{16,0},{20,4},{24,8},{28,12},{1,17},{... | collective-permute-start | bytes 1572872 | tf_op jit(solution)/shard_map/ppermute | solution.py:390
  107.1 74.4 %collective-permute-start.11 = (bf16[2,2,8,32,256]{4,3,2,1,0:T(8,128)(2,1)}, bf16[2,2,8,32,256]{4,3,2,1,0:T(8,128)(2,1)S(1)}, u32[]{:S(2)}, u32[]{:S(2)}) collective-permute-start(bf16[2,2,8,32,256]{4,3,2,1,0:T(8,128)(2,1)} %get-tuple-element.108), channel_id=1, source_target_pairs={{0,20},{4,24},{8,28},{12,0},{16,4},{20,8},{24,12},{28,16},{1,21},{... | collective-permute-start | bytes 1572872 | tf_op jit(solution)/shard_map/ppermute | solution.py:390
  136.5 55.7 %collective-permute-start.12 = (bf16[2,2,8,32,256]{4,3,2,1,0:T(8,128)(2,1)}, bf16[2,2,8,32,256]{4,3,2,1,0:T(8,128)(2,1)S(1)}, u32[]{:S(2)}, u32[]{:S(2)}) collective-permute-start(bf16[2,2,8,32,256]{4,3,2,1,0:T(8,128)(2,1)} %get-tuple-element.109), channel_id=1, source_target_pairs={{0,24},{4,28},{8,0},{12,4},{16,8},{20,12},{24,16},{28,20},{1,25},{... | collective-permute-start | bytes 1572872 | tf_op jit(solution)/shard_map/ppermute | solution.py:390
  140.2 56.8 %collective-permute-start.13 = (bf16[2,2,8,32,256]{4,3,2,1,0:T(8,128)(2,1)}, bf16[2,2,8,32,256]{4,3,2,1,0:T(8,128)(2,1)}, u32[]{:S(2)}, u32[]{:S(2)}) collective-permute-start(bf16[2,2,8,32,256]{4,3,2,1,0:T(8,128)(2,1)} %get-tuple-element.110), channel_id=1, source_target_pairs={{0,28},{4,0},{8,4},{12,8},{16,12},{20,16},{24,20},{28,24},{1,29},{... | collective-permute-start | bytes 1572872 | tf_op jit(solution)/shard_map/ppermute | solution.py:390
  158.6 50.5 %collective-permute-start.14 = (bf16[2,8,32,256]{3,2,1,0:T(8,128)(2,1)}, bf16[2,8,32,256]{3,2,1,0:T(8,128)(2,1)S(1)}, u32[]{:S(2)}, u32[]{:S(2)}) collective-permute-start(bf16[2,8,32,256]{3,2,1,0:T(8,128)(2,1)} %get-tuple-element.113), channel_id=1, source_target_pairs={{0,4},{4,8},{8,12},{12,16},{16,20},{20,24},{24,28},{28,0},{1,5},{5... | collective-permute-start | bytes 786440 | tf_op jit(solution)/shard_map/ppermute | solution.py:390
  158.9 55.0 %collective-permute-start.15 = (bf16[2,8,32,256]{3,2,1,0:T(8,128)(2,1)}, bf16[2,8,32,256]{3,2,1,0:T(8,128)(2,1)S(1)}, u32[]{:S(2)}, u32[]{:S(2)}) collective-permute-start(bf16[2,8,32,256]{3,2,1,0:T(8,128)(2,1)} %get-tuple-element.114), channel_id=1, source_target_pairs={{0,8},{4,12},{8,16},{12,20},{16,24},{20,28},{24,0},{28,4},{1,9},{5... | collective-permute-start | bytes 786440 | tf_op jit(solution)/shard_map/ppermute | solution.py:390
  181.5 49.4 %collective-permute-start.16 = (bf16[2,8,32,256]{3,2,1,0:T(8,128)(2,1)}, bf16[2,8,32,256]{3,2,1,0:T(8,128)(2,1)S(1)}, u32[]{:S(2)}, u32[]{:S(2)}) collective-permute-start(bf16[2,8,32,256]{3,2,1,0:T(8,128)(2,1)} %get-tuple-element.115), channel_id=1, source_target_pairs={{0,12},{4,16},{8,20},{12,24},{16,28},{20,0},{24,4},{28,8},{1,13},{... | collective-permute-start | bytes 786440 | tf_op jit(solution)/shard_map/ppermute | solution.py:390
  192.2 38.6 %collective-permute-start.17 = (bf16[2,8,32,256]{3,2,1,0:T(8,128)(2,1)}, bf16[2,8,32,256]{3,2,1,0:T(8,128)(2,1)S(1)}, u32[]{:S(2)}, u32[]{:S(2)}) collective-permute-start(bf16[2,8,32,256]{3,2,1,0:T(8,128)(2,1)} %get-tuple-element.116), channel_id=1, source_target_pairs={{0,16},{4,20},{8,24},{12,28},{16,0},{20,4},{24,8},{28,12},{1,17},{... | collective-permute-start | bytes 786440 | tf_op jit(solution)/shard_map/ppermute | solution.py:390
  196.9 34.0 %collective-permute-start.18 = (bf16[2,8,32,256]{3,2,1,0:T(8,128)(2,1)}, bf16[2,8,32,256]{3,2,1,0:T(8,128)(2,1)S(1)}, u32[]{:S(2)}, u32[]{:S(2)}) collective-permute-start(bf16[2,8,32,256]{3,2,1,0:T(8,128)(2,1)} %get-tuple-element.117), channel_id=1, source_target_pairs={{0,20},{4,24},{8,28},{12,0},{16,4},{20,8},{24,12},{28,16},{1,21},{... | collective-permute-start | bytes 786440 | tf_op jit(solution)/shard_map/ppermute | solution.py:390
  234.5 95.4 %collective-permute-start.35 = (bf16[8,2,8,32,256]{4,3,2,1,0:T(8,128)(2,1)}, bf16[8,2,8,32,256]{4,3,2,1,0:T(8,128)(2,1)S(1)}, u32[]{:S(2)}, u32[]{:S(2)}) collective-permute-start(bf16[8,2,8,32,256]{4,3,2,1,0:T(8,128)(2,1)} %join.6.token_ref.rest_0_), channel_id=1, source_target_pairs={{0,2},{1,3},{2,0},{3,1},{4,6},{5,7},{6,4},{7,5},{8,10},{9,11},{10,... | collective-permute-start | bytes 6291464 | tf_op jit(solution)/shard_map/ppermute | solution.py:397
  244.5 30.1 %collective-permute-start.30 = (bf16[2,8,32,256]{3,2,1,0:T(8,128)(2,1)S(1)}, bf16[2,8,32,256]{3,2,1,0:T(8,128)(2,1)S(1)}, u32[]{:S(2)}, u32[]{:S(2)}) collective-permute-start(bf16[2,8,32,256]{3,2,1,0:T(8,128)(2,1)S(1)} %copy-done.76), channel_id=1, source_target_pairs={{0,12},{4,16},{8,20},{12,24},{16,28},{20,0},{24,4},{28,8},{1,13},{... | collective-permute-start | bytes 786440 | tf_op jit(solution)/shard_map/ppermute | solution.py:390
  244.5 37.0 %collective-permute-start.31 = (bf16[2,8,32,256]{3,2,1,0:T(8,128)(2,1)}, bf16[2,8,32,256]{3,2,1,0:T(8,128)(2,1)S(1)}, u32[]{:S(2)}, u32[]{:S(2)}) collective-permute-start(bf16[2,8,32,256]{3,2,1,0:T(8,128)(2,1)} %get-tuple-element.132), channel_id=1, source_target_pairs={{0,16},{4,20},{8,24},{12,28},{16,0},{20,4},{24,8},{28,12},{1,17},{... | collective-permute-start | bytes 786440 | tf_op jit(solution)/shard_map/ppermute | solution.py:390
  252.1 40.6 %collective-permute-start.32 = (bf16[2,8,32,256]{3,2,1,0:T(8,128)(2,1)}, bf16[2,8,32,256]{3,2,1,0:T(8,128)(2,1)S(1)}, u32[]{:S(2)}, u32[]{:S(2)}) collective-permute-start(bf16[2,8,32,256]{3,2,1,0:T(8,128)(2,1)} %get-tuple-element.133), channel_id=1, source_target_pairs={{0,20},{4,24},{8,28},{12,0},{16,4},{20,8},{24,12},{28,16},{1,21},{... | collective-permute-start | bytes 786440 | tf_op jit(solution)/shard_map/ppermute | solution.py:390
  252.3 77.5 %collective-permute-start.21 = (bf16[2,2,8,32,256]{4,3,2,1,0:T(8,128)(2,1)}, bf16[2,2,8,32,256]{4,3,2,1,0:T(8,128)(2,1)S(1)}, u32[]{:S(2)}, u32[]{:S(2)}) collective-permute-start(bf16[2,2,8,32,256]{4,3,2,1,0:T(8,128)(2,1)} %get-tuple-element.120), channel_id=1, source_target_pairs={{0,4},{4,8},{8,12},{12,16},{16,20},{20,24},{24,28},{28,0},{1,5},{5... | collective-permute-start | bytes 1572872 | tf_op jit(solution)/shard_map/ppermute | solution.py:390
  292.8 37.0 %collective-permute-start.38 = (bf16[2,2,8,32,128]{4,3,2,1,0:T(8,128)(2,1)}, bf16[2,2,8,32,128]{4,3,2,1,0:T(8,128)(2,1)S(1)}, u32[]{:S(2)}, u32[]{:S(2)}) collective-permute-start(bf16[2,2,8,32,128]{4,3,2,1,0:T(8,128)(2,1)} %get-tuple-element.136), channel_id=1, source_target_pairs={{0,4},{4,8},{8,12},{12,16},{16,20},{20,24},{24,28},{28,0},{1,5},{5... | collective-permute-start | bytes 786440 | tf_op jit(solution)/shard_map/ppermute | solution.py:390
  293.5 36.9 %collective-permute-start.22 = (bf16[2,2,8,32,256]{4,3,2,1,0:T(8,128)(2,1)}, bf16[2,2,8,32,256]{4,3,2,1,0:T(8,128)(2,1)S(1)}, u32[]{:S(2)}, u32[]{:S(2)}) collective-permute-start(bf16[2,2,8,32,256]{4,3,2,1,0:T(8,128)(2,1)} %get-tuple-element.121), channel_id=1, source_target_pairs={{0,8},{4,12},{8,16},{12,20},{16,24},{20,28},{24,0},{28,4},{1,9},{5... | collective-permute-start | bytes 1572872 | tf_op jit(solution)/shard_map/ppermute | solution.py:390
  299.2 54.0 %collective-permute-start.23 = (bf16[2,2,8,32,256]{4,3,2,1,0:T(8,128)(2,1)}, bf16[2,2,8,32,256]{4,3,2,1,0:T(8,128)(2,1)}, u32[]{:S(2)}, u32[]{:S(2)}) collective-permute-start(bf16[2,2,8,32,256]{4,3,2,1,0:T(8,128)(2,1)} %get-tuple-element.122), channel_id=1, source_target_pairs={{0,12},{4,16},{8,20},{12,24},{16,28},{20,0},{24,4},{28,8},{1,13},{... | collective-permute-start | bytes 1572872 | tf_op jit(solution)/shard_map/ppermute | solution.py:390
  329.8 71.6 %collective-permute-start.24 = (bf16[2,2,8,32,256]{4,3,2,1,0:T(8,128)(2,1)}, bf16[2,2,8,32,256]{4,3,2,1,0:T(8,128)(2,1)}, u32[]{:S(2)}, u32[]{:S(2)}) collective-permute-start(bf16[2,2,8,32,256]{4,3,2,1,0:T(8,128)(2,1)} %get-tuple-element.123), channel_id=1, source_target_pairs={{0,16},{4,20},{8,24},{12,28},{16,0},{20,4},{24,8},{28,12},{1,17},{... | collective-permute-start | bytes 1572872 | tf_op jit(solution)/shard_map/ppermute | solution.py:390
  329.8 172.4 %collective-permute-start.36 = (bf16[8,2,8,32,256]{4,3,2,1,0:T(8,128)(2,1)}, bf16[8,2,8,32,256]{4,3,2,1,0:T(8,128)(2,1)}, u32[]{:S(2)}, u32[]{:S(2)}) collective-permute-start(bf16[8,2,8,32,256]{4,3,2,1,0:T(8,128)(2,1)} %join.6.token_ref.rest_0_), channel_id=1, source_target_pairs={{0,1},{1,0},{2,3},{3,2},{4,5},{5,4},{6,7},{7,6},{8,9},{9,8},{10,11... | collective-permute-start | bytes 6291464 | tf_op jit(solution)/shard_map/ppermute | solution.py:406
  329.9 172.3 %collective-permute-start.37 = (bf16[8,2,8,32,256]{4,3,2,1,0:T(8,128)(2,1)S(1)}, bf16[8,2,8,32,256]{4,3,2,1,0:T(8,128)(2,1)}, u32[]{:S(2)}, u32[]{:S(2)}) collective-permute-start(bf16[8,2,8,32,256]{4,3,2,1,0:T(8,128)(2,1)S(1)} %collective-permute-done.35.rest_1_), channel_id=1, source_target_pairs={{0,1},{1,0},{2,3},{3,2},{4,5},{5,4},{6,7},{7,6},{8,9},{9,8},{10,11... | collective-permute-start | bytes 6291464 | tf_op jit(solution)/shard_map/ppermute | solution.py:406
  330.4 81.5 %collective-permute-start.25 = (bf16[2,2,8,32,256]{4,3,2,1,0:T(8,128)(2,1)}, bf16[2,2,8,32,256]{4,3,2,1,0:T(8,128)(2,1)}, u32[]{:S(2)}, u32[]{:S(2)}) collective-permute-start(bf16[2,2,8,32,256]{4,3,2,1,0:T(8,128)(2,1)} %get-tuple-element.124), channel_id=1, source_target_pairs={{0,20},{4,24},{8,28},{12,0},{16,4},{20,8},{24,12},{28,16},{1,21},{... | collective-permute-start | bytes 1572872 | tf_op jit(solution)/shard_map/ppermute | solution.py:390
  353.2 58.7 %collective-permute-start.26 = (bf16[2,2,8,32,256]{4,3,2,1,0:T(8,128)(2,1)}, bf16[2,2,8,32,256]{4,3,2,1,0:T(8,128)(2,1)}, u32[]{:S(2)}, u32[]{:S(2)}) collective-permute-start(bf16[2,2,8,32,256]{4,3,2,1,0:T(8,128)(2,1)} %get-tuple-element.125), channel_id=1, source_target_pairs={{0,24},{4,28},{8,0},{12,4},{16,8},{20,12},{24,16},{28,20},{1,25},{... | collective-permute-start | bytes 1572872 | tf_op jit(solution)/shard_map/ppermute | solution.py:390
  411.9 27.4 %collective-permute-start.39 = (bf16[2,2,8,32,128]{4,3,2,1,0:T(8,128)(2,1)}, bf16[2,2,8,32,128]{4,3,2,1,0:T(8,128)(2,1)}, u32[]{:S(2)}, u32[]{:S(2)}) collective-permute-start(bf16[2,2,8,32,128]{4,3,2,1,0:T(8,128)(2,1)} %get-tuple-element.137), channel_id=1, source_target_pairs={{0,8},{4,12},{8,16},{12,20},{16,24},{20,28},{24,0},{28,4},{1,9},{5... | collective-permute-start | bytes 786440 | tf_op jit(solution)/shard_map/ppermute | solution.py:390
  411.9 28.0 %collective-permute-start.40 = (bf16[2,2,8,32,128]{4,3,2,1,0:T(8,128)(2,1)}, bf16[2,2,8,32,128]{4,3,2,1,0:T(8,128)(2,1)}, u32[]{:S(2)}, u32[]{:S(2)}) collective-permute-start(bf16[2,2,8,32,128]{4,3,2,1,0:T(8,128)(2,1)} %get-tuple-element.138), channel_id=1, source_target_pairs={{0,12},{4,16},{8,20},{12,24},{16,28},{20,0},{24,4},{28,8},{1,13},{... | collective-permute-start | bytes 786440 | tf_op jit(solution)/shard_map/ppermute | solution.py:390
  424.6 24.6 %collective-permute-start.41 = (bf16[2,2,8,32,128]{4,3,2,1,0:T(8,128)(2,1)}, bf16[2,2,8,32,128]{4,3,2,1,0:T(8,128)(2,1)}, u32[]{:S(2)}, u32[]{:S(2)}) collective-permute-start(bf16[2,2,8,32,128]{4,3,2,1,0:T(8,128)(2,1)} %get-tuple-element.139), channel_id=1, source_target_pairs={{0,16},{4,20},{8,24},{12,28},{16,0},{20,4},{24,8},{28,12},{1,17},{... | collective-permute-start | bytes 786440 | tf_op jit(solution)/shard_map/ppermute | solution.py:390
  439.4 85.8 %collective-permute-start.52 = (bf16[8,2,8,32,256]{4,3,2,1,0:T(8,128)(2,1)}, bf16[8,2,8,32,256]{4,3,2,1,0:T(8,128)(2,1)}, u32[]{:S(2)}, u32[]{:S(2)}) collective-permute-start(bf16[8,2,8,32,256]{4,3,2,1,0:T(8,128)(2,1)} %join.7.token_ref.rest_0_), channel_id=1, source_target_pairs={{0,2},{1,3},{2,0},{3,1},{4,6},{5,7},{6,4},{7,5},{8,10},{9,11},{10,... | collective-permute-start | bytes 6291464 | tf_op jit(solution)/shard_map/ppermute | solution.py:397
  478.3 23.9 %collective-permute-start.47 = (bf16[2,8,32,256]{3,2,1,0:T(8,128)(2,1)}, bf16[2,8,32,256]{3,2,1,0:T(8,128)(2,1)S(1)}, u32[]{:S(2)}, u32[]{:S(2)}) collective-permute-start(bf16[2,8,32,256]{3,2,1,0:T(8,128)(2,1)} %get-tuple-element.146), channel_id=1, source_target_pairs={{0,12},{4,16},{8,20},{12,24},{16,28},{20,0},{24,4},{28,8},{1,13},{... | collective-permute-start | bytes 786440 | tf_op jit(solution)/shard_map/ppermute | solution.py:390
  486.9 34.1 %collective-permute-start.48 = (bf16[2,8,32,256]{3,2,1,0:T(8,128)(2,1)}, bf16[2,8,32,256]{3,2,1,0:T(8,128)(2,1)}, u32[]{:S(2)}, u32[]{:S(2)}) collective-permute-start(bf16[2,8,32,256]{3,2,1,0:T(8,128)(2,1)} %get-tuple-element.147), channel_id=1, source_target_pairs={{0,16},{4,20},{8,24},{12,28},{16,0},{20,4},{24,8},{28,12},{1,17},{... | collective-permute-start | bytes 786440 | tf_op jit(solution)/shard_map/ppermute | solution.py:390
  524.6 47.3 %collective-permute-start.69 = (bf16[8,2,8,32,256]{4,3,2,1,0:T(8,128)(2,1)}, bf16[8,2,8,32,256]{4,3,2,1,0:T(8,128)(2,1)}, u32[]{:S(2)}, u32[]{:S(2)}) collective-permute-start(bf16[8,2,8,32,256]{4,3,2,1,0:T(8,128)(2,1)} %join.8.token_ref.rest_0_), channel_id=1, source_target_pairs={{0,2},{1,3},{2,0},{3,1},{4,6},{5,7},{6,4},{7,5},{8,10},{9,11},{10,... | collective-permute-start | bytes 6291464 | tf_op jit(solution)/shard_map/ppermute | solution.py:397
  525.1 70.4 %collective-permute-start.53 = (bf16[8,2,8,32,256]{4,3,2,1,0:T(8,128)(2,1)S(1)}, bf16[8,2,8,32,256]{4,3,2,1,0:T(8,128)(2,1)S(1)}, u32[]{:S(2)}, u32[]{:S(2)}) collective-permute-start(bf16[8,2,8,32,256]{4,3,2,1,0:T(8,128)(2,1)S(1)} %copy-done), channel_id=1, source_target_pairs={{0,1},{1,0},{2,3},{3,2},{4,5},{5,4},{6,7},{7,6},{8,9},{9,8},{10,11... | collective-permute-start | bytes 6291464 | tf_op jit(solution)/shard_map/ppermute | solution.py:406
  525.1 90.5 %collective-permute-start.54 = (bf16[8,2,8,32,256]{4,3,2,1,0:T(8,128)(2,1)}, bf16[8,2,8,32,256]{4,3,2,1,0:T(8,128)(2,1)}, u32[]{:S(2)}, u32[]{:S(2)}) collective-permute-start(bf16[8,2,8,32,256]{4,3,2,1,0:T(8,128)(2,1)} %collective-permute-done.52.rest_1_), channel_id=1, source_target_pairs={{0,1},{1,0},{2,3},{3,2},{4,5},{5,4},{6,7},{7,6},{8,9},{9,8},{10,11... | collective-permute-start | bytes 6291464 | tf_op jit(solution)/shard_map/ppermute | solution.py:406
  559.9 102.3 %collective-permute-start.70 = (bf16[8,2,8,32,256]{4,3,2,1,0:T(8,128)(2,1)}, bf16[8,2,8,32,256]{4,3,2,1,0:T(8,128)(2,1)}, u32[]{:S(2)}, u32[]{:S(2)}) collective-permute-start(bf16[8,2,8,32,256]{4,3,2,1,0:T(8,128)(2,1)} %join.8.token_ref.rest_0_), channel_id=1, source_target_pairs={{0,1},{1,0},{2,3},{3,2},{4,5},{5,4},{6,7},{7,6},{8,9},{9,8},{10,11... | collective-permute-start | bytes 6291464 | tf_op jit(solution)/shard_map/ppermute | solution.py:406
  571.9 90.3 %collective-permute-start.71 = (bf16[8,2,8,32,256]{4,3,2,1,0:T(8,128)(2,1)}, bf16[8,2,8,32,256]{4,3,2,1,0:T(8,128)(2,1)}, u32[]{:S(2)}, u32[]{:S(2)}) collective-permute-start(bf16[8,2,8,32,256]{4,3,2,1,0:T(8,128)(2,1)} %collective-permute-done.69.rest_1_), channel_id=1, source_target_pairs={{0,1},{1,0},{2,3},{3,2},{4,5},{5,4},{6,7},{7,6},{8,9},{9,8},{10,11... | collective-permute-start | bytes 6291464 | tf_op jit(solution)/shard_map/ppermute | solution.py:406
  637.6 24.3 %collective-permute-start.79 = (bf16[8,2,8,32,128]{4,3,2,1,0:T(8,128)(2,1)}, bf16[8,2,8,32,128]{4,3,2,1,0:T(8,128)(2,1)S(1)}, u32[]{:S(2)}, u32[]{:S(2)}) collective-permute-start(bf16[8,2,8,32,128]{4,3,2,1,0:T(8,128)(2,1)} %join.9.token_ref.rest_0_), channel_id=1, source_target_pairs={{0,2},{1,3},{2,0},{3,1},{4,6},{5,7},{6,4},{7,5},{8,10},{9,11},{10,... | collective-permute-start | bytes 3145736 | tf_op jit(solution)/shard_map/ppermute | solution.py:397
  662.2 58.1 %collective-permute-start.80 = (bf16[8,2,8,32,128]{4,3,2,1,0:T(8,128)(2,1)}, bf16[8,2,8,32,128]{4,3,2,1,0:T(8,128)(2,1)S(1)}, u32[]{:S(2)}, u32[]{:S(2)}) collective-permute-start(bf16[8,2,8,32,128]{4,3,2,1,0:T(8,128)(2,1)} %join.9.token_ref.rest_0_), channel_id=1, source_target_pairs={{0,1},{1,0},{2,3},{3,2},{4,5},{5,4},{6,7},{7,6},{8,9},{9,8},{10,11... | collective-permute-start | bytes 3145736 | tf_op jit(solution)/shard_map/ppermute | solution.py:406
  662.2 59.4 %collective-permute-start.81 = (bf16[8,2,8,32,128]{4,3,2,1,0:T(8,128)(2,1)S(1)}, bf16[8,2,8,32,128]{4,3,2,1,0:T(8,128)(2,1)S(1)}, u32[]{:S(2)}, u32[]{:S(2)}) collective-permute-start(bf16[8,2,8,32,128]{4,3,2,1,0:T(8,128)(2,1)S(1)} %collective-permute-done.79.rest_1_), channel_id=1, source_target_pairs={{0,1},{1,0},{2,3},{3,2},{4,5},{5,4},{6,7},{7,6},{8,9},{9,8},{10,11... | collective-permute-start | bytes 3145736 | tf_op jit(solution)/shard_map/ppermute | solution.py:406
  677.9 64.6 %collective-permute-start.83 = (bf16[8,2,6,32,128]{4,3,2,1,0:T(8,128)(2,1)}, bf16[8,2,6,32,128]{4,3,2,1,0:T(8,128)(2,1)}, u32[]{:S(2)}, u32[]{:S(2)}) collective-permute-start(bf16[8,2,6,32,128]{4,3,2,1,0:T(8,128)(2,1)} %join.10.token_ref.rest_4_), channel_id=1, source_target_pairs={{0,1},{1,0},{2,3},{3,2},{4,5},{5,4},{6,7},{7,6},{8,9},{9,8},{10,11... | collective-permute-start | bytes 2359304 | tf_op jit(solution)/shard_map/ppermute | solution.py:406
  697.2 45.3 %collective-permute-start.84 = (bf16[8,2,6,32,128]{4,3,2,1,0:T(8,128)(2,1)}, bf16[8,2,6,32,128]{4,3,2,1,0:T(8,128)(2,1)}, u32[]{:S(2)}, u32[]{:S(2)}) collective-permute-start(bf16[8,2,6,32,128]{4,3,2,1,0:T(8,128)(2,1)} %collective-permute-done.82.rest_5_), channel_id=1, source_target_pairs={{0,1},{1,0},{2,3},{3,2},{4,5},{5,4},{6,7},{7,6},{8,9},{9,8},{10,11... | collective-permute-start | bytes 2359304 | tf_op jit(solution)/shard_map/ppermute | solution.py:406
  736.5 29.4 %collective-permute-start.93 = (bf16[8,2,2,32,128]{4,3,2,1,0:T(8,128)(2,1)}, bf16[8,2,2,32,128]{4,3,2,1,0:T(8,128)(2,1)S(1)}, u32[]{:S(2)}, u32[]{:S(2)}) collective-permute-start(bf16[8,2,2,32,128]{4,3,2,1,0:T(8,128)(2,1)} %join.11.rest_5_), channel_id=1, source_target_pairs={{0,1},{1,0},{2,3},{3,2},{4,5},{5,4},{6,7},{7,6},{8,9},{9,8},{10,11... | collective-permute-start | bytes 786440 | tf_op jit(solution)/shard_map/ppermute | solution.py:406
  742.5 23.4 %collective-permute-start.94 = (bf16[8,2,2,32,128]{4,3,2,1,0:T(8,128)(2,1)S(1)}, bf16[8,2,2,32,128]{4,3,2,1,0:T(8,128)(2,1)S(1)}, u32[]{:S(2)}, u32[]{:S(2)}) collective-permute-start(bf16[8,2,2,32,128]{4,3,2,1,0:T(8,128)(2,1)S(1)} %collective-permute-done.92.rest_6_), channel_id=1, source_target_pairs={{0,1},{1,0},{2,3},{3,2},{4,5},{5,4},{6,7},{7,6},{8,9},{9,8},{10,11... | collective-permute-start | bytes 786440 | tf_op jit(solution)/shard_map/ppermute | solution.py:406
  (137 other events, 3226.4 us)

commit v2 on v1

--- a/solution.py
+++ b/solution.py
@@ -138,9 +138,7 @@
     )(index, token, *([particle] * count), *([hole] * count))
 
 
-def polar_kernel(count, local, sizes):
-    groups = len(sizes)
-    group_of = [g for g, size in enumerate(sizes) for _ in range(size)]
+def polar_kernel(count, local):
     points = count * local
     quarter = points // KSIDE
     low = KSIDE
@@ -148,7 +146,7 @@
 
     def kernel(me_ref, token_ref, *rest):
         pieces = rest[:count]
-        outs = rest[count : count + count * groups]
+        outs = rest[count : 2 * count]
         sc = rest[-1]
         me = me_ref[0]
         for shift in range(count):
@@ -204,42 +202,32 @@
                     (sc[0, 0, base + offset + n], sc[0, 1, base + offset + n]) for n in range(low)
                 ]
                 for n, (real, imag) in enumerate(dft4(values, -1)):
-                    spot = offset + n
-                    group = group_of[spot]
-                    out = outs[shift * groups + group]
-                    place = spot - sum(sizes[:group])
-                    out[0, place] = (real * scale).astype(jnp.bfloat16)
-                    out[1, place] = (imag * scale).astype(jnp.bfloat16)
+                    outs[shift][0, offset + n] = (real * scale).astype(jnp.bfloat16)
+                    outs[shift][1, offset + n] = (imag * scale).astype(jnp.bfloat16)
 
     return kernel
 
 
-def polar_call(me, token, pieces, sizes):
+def polar_call(me, token, pieces):
     count = len(pieces)
     _, _, local, rows, width = pieces[0].shape
-    result = pl.pallas_call(
-        polar_kernel(count, local, sizes),
+    return pl.pallas_call(
+        polar_kernel(count, local),
         grid=(width // LANES, rows // SUB),
         in_specs=[pl.BlockSpec(memory_space=pltpu.SMEM), ANY]
         + [pl.BlockSpec((2, 2, local, SUB, LANES), lambda c, r: (0, 0, 0, r, c))] * count,
-        out_specs=[
-            pl.BlockSpec((2, size, SUB, LANES), lambda c, r: (0, 0, r, c)) for size in sizes
-        ]
-        * count,
-        out_shape=[jax.ShapeDtypeStruct((2, size, rows, width), jnp.bfloat16) for size in sizes]
-        * count,
+        out_specs=[pl.BlockSpec((2, local, SUB, LANES), lambda c, r: (0, 0, r, c))] * count,
+        out_shape=[jax.ShapeDtypeStruct((2, local, rows, width), jnp.bfloat16)] * count,
         scratch_shapes=[pltpu.VMEM((2, 2, count * local, SUB, LANES), jnp.float32)],
         name="polar",
     )(me, token, *pieces)
-    groups = len(sizes)
-    return [[result[shift * groups + g] for shift in range(count)] for g in range(groups)]
-
-
-def join_call(token, pieces):
+
+
+def join_call(token, pieces, first, momenta):
     count = len(pieces)
-    _, momenta, rows, width = pieces[0].shape
-    steps = 2 if momenta % 2 == 0 else 1
-    part = momenta // steps
+    _, _, rows, width = pieces[0].shape
+    part = math.gcd(first, momenta) if first else momenta
+    part = part // 2 if part % 2 == 0 and part == momenta else part
 
     def kernel(token_ref, *rest):
         for n in range(count):
@@ -247,10 +235,11 @@
 
     return pl.pallas_call(
         kernel,
-        grid=(steps,),
-        in_specs=[ANY] + [pl.BlockSpec((2, part, rows, width), lambda j: (0, j, 0, 0))] * count,
+        grid=(momenta // part,),
+        in_specs=[ANY]
+        + [pl.BlockSpec((2, part, rows, width), lambda j: (0, first // part + j, 0, 0))] * count,
         out_specs=pl.BlockSpec((count, 2, part, rows, width), lambda j: (0, 0, j, 0, 0)),
-        out_shape=jax.ShapeDtypeStruct((count,) + pieces[0].shape, pieces[0].dtype),
+        out_shape=jax.ShapeDtypeStruct((count, 2, momenta, rows, width), pieces[0].dtype),
         name="join",
     )(token, *pieces)
 
@@ -259,23 +248,25 @@
     return jnp.dot(left, right, preferred_element_type=jnp.float32)
 
 
-def fill_rows(index_ref, blocks, polar, count, rows, width):
+def fill_rows(index_ref, blocks, q, polar, count, rows, column, width):
     me = index_ref[0]
+    here, there = pl.ds(column, width), pl.ds(polar.shape[1] // 2 + column, width)
     for slot, block in enumerate(blocks):
         first = index_ref[2 + slot] * (count * rows)
         for shift in range(count):
             source = lax.rem(me + (count - shift), count)
             row = pl.multiple_of(first + source * rows, rows)
-            real, imag = block[shift, 0, 0], block[shift, 1, 0]
-            polar[0, pl.ds(row, rows), :width] = real
-            polar[0, pl.ds(row, rows), width:] = imag
-            polar[1, pl.ds(row, rows), :width] = -imag
-            polar[1, pl.ds(row, rows), width:] = real
-
-
-def left_product(mine, polar, width):
-    made = dot(mine[0], polar[0]) + dot(mine[1], polar[1])
-    return made[:, :width].astype(jnp.bfloat16), made[:, width:].astype(jnp.bfloat16)
+            polar[pl.ds(row, rows), here] = block[shift, 0, q]
+            polar[pl.ds(row, rows), there] = block[shift, 1, q]
+
+
+def left_product(mine, polar):
+    _, rows, points = mine.shape
+    made = dot(mine.reshape(2 * rows, points), polar[...])
+    width = made.shape[1] // 2
+    real = made[:rows, :width] - made[rows:, width:]
+    imag = made[:rows, width:] + made[rows:, :width]
+    return real.astype(jnp.bfloat16), imag.astype(jnp.bfloat16)
 
 
 def left_call(index, token, coulomb, blocks):
@@ -283,49 +274,55 @@
     points = coulomb.shape[3]
     tile_rows = count * rows
 
+    each = 2 if momenta % 2 == 0 else 1
+
     def kernel(index_ref, rows_ref, token_ref, *rest):
         block_refs, out, polar = rest[: len(blocks)], rest[-2], rest[-1]
-        fill_rows(index_ref, block_refs, polar, count, rows, width)
-        out[0, 0], out[1, 0] = left_product(rows_ref[:, 0], polar, width)
+        for q in range(each):
+            fill_rows(index_ref, block_refs, q, polar.at[q], count, rows, 0, width)
+            out[0, q], out[1, q] = left_product(rows_ref[:, q], polar.at[q])
 
     return pl.pallas_call(
         kernel,
         grid_spec=pltpu.PrefetchScalarGridSpec(
             num_scalar_prefetch=1,
-            grid=(momenta,),
+            grid=(momenta // each,),
             in_specs=[
-                pl.BlockSpec((2, 1, tile_rows, points), lambda q, ix: (0, q, ix[1], 0)),
+                pl.BlockSpec((2, each, tile_rows, points), lambda q, ix: (0, q, ix[1], 0)),
                 ANY,
             ]
-            + [pl.BlockSpec((count, 2, 1, rows, width), lambda q, ix: (0, 0, q, 0, 0))]
+            + [pl.BlockSpec((count, 2, each, rows, width), lambda q, ix: (0, 0, q, 0, 0))]
             * len(blocks),
-            out_specs=pl.BlockSpec((2, 1, tile_rows, width), lambda q, ix: (0, q, 0, 0)),
-            scratch_shapes=[pltpu.VMEM((2, points, 2 * width), jnp.bfloat16)],
+            out_specs=pl.BlockSpec((2, each, tile_rows, width), lambda q, ix: (0, q, 0, 0)),
+            scratch_shapes=[pltpu.VMEM((each, points, 2 * width), jnp.bfloat16)],
         ),
         out_shape=jax.ShapeDtypeStruct((2, momenta, tile_rows, width), jnp.bfloat16),
         name="left",
     )(index, coulomb, token, *blocks)
 
 
-def screen_call(index, previous, coulomb, lefts, blocks, first):
-    count, _, momenta, rows, width = blocks[0].shape
+def screen_call(index, previous, coulomb, lefts, early, late, first):
+    count, _, momenta, rows, late_width = late[0].shape
+    early_width = early[0].shape[4]
+    fresh = early_width + late_width
     points = coulomb.shape[3]
     tile_rows = count * rows
-    widths = [left.shape[3] for left in lefts] + [width]
+    widths = [left.shape[3] for left in lefts] + [fresh]
     out_shape = jax.ShapeDtypeStruct((2, coulomb.shape[1], tile_rows, points), jnp.float32)
     n_prev = 0 if previous is None else 1
 
     def kernel(index_ref, coulomb_ref, *rest):
         rest = rest[n_prev:]
-        left_refs = rest[: len(lefts)]
-        block_refs = rest[len(lefts) : len(lefts) + len(blocks)]
-        out, polar, left = rest[-3], rest[-2], rest[-1]
-        fill_rows(index_ref, block_refs, polar, count, rows, width)
+        left_refs, rest = rest[: len(lefts)], rest[len(lefts) :]
+        early_refs, rest = rest[: len(early)], rest[len(early) :]
+        late_refs, (out, polar, left) = rest[: len(late)], rest[len(late) :]
+        fill_rows(index_ref, early_refs, 0, polar, count, rows, 0, early_width)
+        fill_rows(index_ref, late_refs, 0, polar, count, rows, early_width, late_width)
         row = pl.multiple_of(index_ref[1] * tile_rows, tile_rows)
         mine = coulomb_ref[:, 0, pl.ds(row, tile_rows), :]
-        last = [left_product(mine, polar, width)]
+        parts = [(ref[0, 0], ref[1, 0]) for ref in left_refs] + [left_product(mine, polar)]
         column = 0
-        for w, (real, imag) in zip(widths, [(ref[0, 0], ref[1, 0]) for ref in left_refs] + last):
+        for w, (real, imag) in zip(widths, parts):
             left[0, :, column : column + w] = real
             left[0, :, points + column : points + column + w] = -imag
             left[1, :, column : column + w] = imag
@@ -334,6 +331,11 @@
         stacked = coulomb_ref[...].reshape(2 * points, points)
         made = dot(left[...].reshape(2 * tile_rows, 2 * points), stacked)
         out[:, 0] = mine.astype(jnp.float32) + made.reshape(2, tile_rows, points)
+
+    def rows_spec(width, offset):
+        return pl.BlockSpec(
+            (count, 2, 1, rows, width), lambda q, ix: (0, 0, offset + q, 0, 0)
+        )
 
     return pl.pallas_call(
         kernel,
@@ -346,36 +348,40 @@
                 pl.BlockSpec((2, 1, tile_rows, w), lambda q, ix: (0, first + q, 0, 0))
                 for w in widths[:-1]
             ]
-            + [pl.BlockSpec((count, 2, 1, rows, width), lambda q, ix: (0, 0, q, 0, 0))]
-            * len(blocks),
+            + [rows_spec(early_width, first)] * len(early)
+            + [rows_spec(late_width, 0)] * len(late),
             out_specs=pl.BlockSpec(
                 (2, 1, tile_rows, points), lambda q, ix: (0, first + q, 0, 0)
             ),
             scratch_shapes=[
-                pltpu.VMEM((2, points, 2 * width), jnp.bfloat16),
+                pltpu.VMEM((points, 2 * fresh), jnp.bfloat16),
                 pltpu.VMEM((2, tile_rows, 2 * points), jnp.bfloat16),
             ],
         ),
         out_shape=out_shape,
         input_output_aliases={2: 0} if n_prev else {},
-    )(index, coulomb, *([] if previous is None else [previous]), *lefts, *blocks)
+    )(index, coulomb, *([] if previous is None else [previous]), *lefts, *early, *late)
 
 
 def order_of(chunks, groups):
     last = chunks - 1
     order = [("split", n, 0) for n in range(min(2, chunks))]
-    for n in range(chunks):
+    for n in range(last):
+        soon = n == last - 1
+        if soon and n >= 1:
+            order.append(("join", n - 1, 0))
         order.append(("transform", n, 0))
         if n + 2 < chunks:
             order.append(("split", n + 2, 0))
         if n >= 2:
             order.append(("ahead", n - 2, 0))
-        if n >= 1:
+        if not soon and n >= 1:
             order.append(("join", n - 1, 0))
         if n >= 2:
             order.append(("left", n - 2, 0))
-    order += [("join", last, 0), ("ahead", last - 1, 0), ("left", last - 1, 0)]
-    order += [("join", last, g) for g in range(1, groups)]
+    order += [("transform", last, 0), ("join", last - 1, 0), ("ahead", last - 2, 0)]
+    order += [("join", last, g) for g in range(groups)]
+    order += [("left", last - 2, 0), ("ahead", last - 1, 0)]
     for g in range(groups):
         order += [("ahead", last, g), ("screen", last, g)]
     return order
@@ -417,7 +423,6 @@
         index = jnp.stack([me, tile] + slots).astype(jnp.int32)
         starts = [sum(plan[:n]) for n in range(len(plan))]
         last = len(plan) - 1
-        everything = [coulomb.shape[1]]
         green, polar, near, over, lefts = {}, {}, {}, {}, {}
 
         def send_green(n, token):
@@ -426,12 +431,13 @@
             return pieces[0]
 
         def send_polar(n, token):
-            made = polar_call(me_only, token, green[n], sizes if n == last else everything)
-            polar[n] = [exchange(pieces) for pieces in made]
-            return made[0][0]
+            made = polar_call(me_only, token, green[n])
+            polar[n] = exchange(made)
+            return made[0]
 
         def send_rows(n, g, token):
-            block = join_call(token, polar[n][g])
+            first, momenta = (sum(sizes[:g]), sizes[g]) if n == last else (0, sum(sizes))
+            block = join_call(token, polar[n], first, momenta)
             near[n, g] = across_chips(block)
             over[n, g] = [across_cores(block)]
             return block
@@ -446,10 +452,9 @@
             return lefts[n]
 
         def screen(n, g, token):
-            before = [lefts[m] for m in range(last)]
-            return screen_call(
-                index, token, coulomb, before, near[n, g] + over[n, g], sum(sizes[:g])
-            )
+            before = [lefts[m] for m in range(last - 1)]
+            early, late = near[n - 1, 0] + over[n - 1, 0], near[n, g] + over[n, g]
+            return screen_call(index, token, coulomb, before, early, late, sum(sizes[:g]))
 
         token = me_only
         steps = {"split": send_green, "transform": send_polar}
@@ -503,7 +508,7 @@
         if not fits:
             return sharded(generic_body)(particle, hole, coulomb)
         plan = [2 * LANES] * (points // (2 * LANES) - 1) + [LANES, LANES]
-        sizes = [local - local // 4, local // 4]
+        sizes = [3 * local // 8, local - 3 * local // 8] if local >= 8 else [local]
         whole = sharded(pipelined(count, tiles, plan, sizes))
         return whole(particle, hole, coulomb)
 

time: 780 us -> 712 us (0.913)
  starting transfers between devices: 350 us -> 272 us
  waiting for transfers between devices: 266 us -> 294 us
  Pallas kernels: 153 us -> 138 us
    ppermute x77 -> x70, starting transfers between devices: 344 us -> 265 us  [exchange(): lax.ppermute(pieces[shift], 'kt', [(d, (d + shift) % count) for d in rang...]
    ppermute x77 -> x70, waiting for transfers between devices: 221 us -> 274 us  [exchange(): lax.ppermute(pieces[shift], 'kt', [(d, (d + shift) % count) for d in rang...]
    ppermute x6, waiting for transfers between devices: 44.2 us -> 19.9 us  [across_chips(): lax.ppermute(block, 'tile', [(t, (t // 2 + shift) % chips * 2 + t % 2) fo...]
    pallas_call x4 -> x3, Pallas kernels: 47.9 us -> 31.4 us  [left_call(): pl.pallas_call(kernel, grid_spec=pltpu.PrefetchScalarGridSpec(num_scalar_...]
  transfers between devices with their start and end apart: 95 -> 88, of which waited for: 35 -> 35; matrix products, arithmetic and copies ran while one was open for 0% -> 0% of each run, Pallas kernels for 17% -> 15%
where the time goes in v2:
time: 712 us; the launch traced here: 711 us
  waiting for transfers between devices  294 us (41%)
  starting transfers between devices  272 us (38%)
  Pallas kernels  138 us (19%)
    ppermute x70, waiting for transfers between devices, exchange(): lax.ppermute(pieces[shift], 'kt', [(d, (d + shift) % count) for d in rang...  274 us
    ppermute x70, starting transfers between devices, exchange(): lax.ppermute(pieces[shift], 'kt', [(d, (d + shift) % count) for d in rang...  265 us
    pallas_call x2, Pallas kernels, screen_call(): pl.pallas_call(kernel, grid_spec=pltpu.PrefetchScalarGridSpec(num_scalar_...  35.3 us
    pallas_call x5, Pallas kernels, polar_call(): pl.pallas_call(polar_kernel(count, local), grid=(width // LANES, rows //...  34.8 us
    pallas_call x3, Pallas kernels, left_call(): pl.pallas_call(kernel, grid_spec=pltpu.PrefetchScalarGridSpec(num_scalar_...  31.4 us
    pallas_call x5, Pallas kernels, split_call(): pl.pallas_call(kernel, grid_spec=pltpu.PrefetchScalarGridSpec(num_scalar_...  21.2 us
    ppermute x6, waiting for transfers between devices, across_chips(): lax.ppermute(block, 'tile', [(t, (t // 2 + shift) % chips * 2 + t % 2) fo...  19.9 us
    pallas_call x6, Pallas kernels, join_call(): pl.pallas_call(kernel, grid=(momenta // part,), in_specs=[ANY] + [pl.Bloc...  15.6 us
  transfers between devices with their start and end apart: 88, of which 35 were waited for; matrix products, arithmetic and copies ran while one was open for 0% of the time, Pallas kernels for 15%

profile of v2, /device:TPU:0, one launch (start us, length us, event | category | flops | bytes accessed | tf_op | source)
XLA Modules:
  0.0 711.1 jit_solution(5053603863886559360)
XLA Ops:
  16.3 8.2 %collective-permute-done.rest_1_ = bf16[2,2,8,32,256]{4,3,2,1,0:T(8,128)(2,1)S(1)} collective-permute-done((bf16[2,2,8,32,256]{4,3,2,1,0:T(8,128)(2,1)}, bf16[2,2,8,32,256]{4,3,2,1,0:T(8,128)(2,1)S(1)}, u32[]{:S(2)}, u32[]{:S(2)}) %collective-permute-start) | collective-permute-done | bytes 524320 | tf_op jit(solution)/shard_map/ppermute | solution.py:396
  31.0 5.8 collective-permute-start.6
  36.8 31.8 %collective-permute-done.2.rest_3_ = bf16[2,2,8,32,256]{4,3,2,1,0:T(8,128)(2,1)S(1)} collective-permute-done((bf16[2,2,8,32,256]{4,3,2,1,0:T(8,128)(2,1)}, bf16[2,2,8,32,256]{4,3,2,1,0:T(8,128)(2,1)S(1)}, u32[]{:S(2)}, u32[]{:S(2)}) %collective-permute-start.2) | collective-permute-done | bytes 524320 | tf_op jit(solution)/shard_map/ppermute | solution.py:396
  69.4 22.1 %collective-permute-start.8 = (bf16[2,2,8,32,256]{4,3,2,1,0:T(8,128)(2,1)}, bf16[2,2,8,32,256]{4,3,2,1,0:T(8,128)(2,1)S(1)}, u32[]{:S(2)}, u32[]{:S(2)}) collective-permute-start(bf16[2,2,8,32,256]{4,3,2,1,0:T(8,128)(2,1)} %get-tuple-element.97), channel_id=1, source_target_pairs={{0,8},{4,12},{8,16},{12,20},{16,24},{20,28},{24,0},{28,4},{1,9},{5... | collective-permute-start | bytes 1572872 | tf_op jit(solution)/shard_map/ppermute | solution.py:396
  91.5 11.5 %collective-permute-start.9 = (bf16[2,2,8,32,256]{4,3,2,1,0:T(8,128)(2,1)}, bf16[2,2,8,32,256]{4,3,2,1,0:T(8,128)(2,1)S(1)}, u32[]{:S(2)}, u32[]{:S(2)}) collective-permute-start(bf16[2,2,8,32,256]{4,3,2,1,0:T(8,128)(2,1)} %get-tuple-element.98), channel_id=1, source_target_pairs={{0,12},{4,16},{8,20},{12,24},{16,28},{20,0},{24,4},{28,8},{1,13},{... | collective-permute-start | bytes 1572872 | tf_op jit(solution)/shard_map/ppermute | solution.py:396
  107.0 29.4 %collective-permute-start.11 = (bf16[2,2,8,32,256]{4,3,2,1,0:T(8,128)(2,1)}, bf16[2,2,8,32,256]{4,3,2,1,0:T(8,128)(2,1)S(1)}, u32[]{:S(2)}, u32[]{:S(2)}) collective-permute-start(bf16[2,2,8,32,256]{4,3,2,1,0:T(8,128)(2,1)} %get-tuple-element.100), channel_id=1, source_target_pairs={{0,20},{4,24},{8,28},{12,0},{16,4},{20,8},{24,12},{28,16},{1,21},{... | collective-permute-start | bytes 1572872 | tf_op jit(solution)/shard_map/ppermute | solution.py:396
  140.2 8.2 %polar.5 = (bf16[2,8,32,256]{3,2,1,0:T(8,128)(2,1)}, bf16[2,8,32,256]{3,2,1,0:T(8,128)(2,1)}, bf16[2,8,32,256]{3,2,1,0:T(8,128)(2,1)}, bf16[2,8,32,256]{3,2,1,0:...) custom-call(s32[1]{0:T(128)} %bitcast.token_ref.me_ref, ...), custom_call_target="tpu_custom_call" | custom-call | tf_op jit(solution)/shard_map/polar/pallas_call | solution.py:214
  148.5 10.1 %collective-permute-done.9.rest_3_ = bf16[2,2,8,32,256]{4,3,2,1,0:T(8,128)(2,1)S(1)} collective-permute-done((bf16[2,2,8,32,256]{4,3,2,1,0:T(8,128)(2,1)}, bf16[2,2,8,32,256]{4,3,2,1,0:T(8,128)(2,1)S(1)}, u32[]{:S(2)}, u32[]{:S(2)}) %collective-permute-start.9) | collective-permute-done | bytes 524320 | tf_op jit(solution)/shard_map/ppermute | solution.py:396
  158.9 22.6 %collective-permute-start.15 = (bf16[2,8,32,256]{3,2,1,0:T(8,128)(2,1)}, bf16[2,8,32,256]{3,2,1,0:T(8,128)(2,1)S(1)}, u32[]{:S(2)}, u32[]{:S(2)}) collective-permute-start(bf16[2,8,32,256]{3,2,1,0:T(8,128)(2,1)} %get-tuple-element.106), channel_id=1, source_target_pairs={{0,8},{4,12},{8,16},{12,20},{16,24},{20,28},{24,0},{28,4},{1,9},{5... | collective-permute-start | bytes 786440 | tf_op jit(solution)/shard_map/ppermute | solution.py:396
  181.4 10.8 %collective-permute-start.16 = (bf16[2,8,32,256]{3,2,1,0:T(8,128)(2,1)}, bf16[2,8,32,256]{3,2,1,0:T(8,128)(2,1)S(1)}, u32[]{:S(2)}, u32[]{:S(2)}) collective-permute-start(bf16[2,8,32,256]{3,2,1,0:T(8,128)(2,1)} %get-tuple-element.107), channel_id=1, source_target_pairs={{0,12},{4,16},{8,20},{12,24},{16,28},{20,0},{24,4},{28,8},{1,13},{... | collective-permute-start | bytes 786440 | tf_op jit(solution)/shard_map/ppermute | solution.py:396
  196.9 12.2 %collective-permute-start.18 = (bf16[2,8,32,256]{3,2,1,0:T(8,128)(2,1)}, bf16[2,8,32,256]{3,2,1,0:T(8,128)(2,1)S(1)}, u32[]{:S(2)}, u32[]{:S(2)}) collective-permute-start(bf16[2,8,32,256]{3,2,1,0:T(8,128)(2,1)} %get-tuple-element.109), channel_id=1, source_target_pairs={{0,20},{4,24},{8,28},{12,0},{16,4},{20,8},{24,12},{28,16},{1,21},{... | collective-permute-start | bytes 786440 | tf_op jit(solution)/shard_map/ppermute | solution.py:396
  209.1 4.8 collective-permute-start.19
  218.7 8.2 %polar.6 = (bf16[2,8,32,256]{3,2,1,0:T(8,128)(2,1)}, bf16[2,8,32,256]{3,2,1,0:T(8,128)(2,1)}, bf16[2,8,32,256]{3,2,1,0:T(8,128)(2,1)}, bf16[2,8,32,256]{3,2,1,0:...) custom-call(s32[1]{0:T(128)} %bitcast.token_ref.me_ref, ...), custom_call_target="tpu_custom_call" | custom-call | tf_op jit(solution)/shard_map/polar/pallas_call | solution.py:214
  238.2 6.2 collective-permute-start.29
  247.4 4.9 collective-permute-done.28.rest_1_
  253.5 9.1 %collective-permute-start.23 = (bf16[2,2,8,32,256]{4,3,2,1,0:T(8,128)(2,1)}, bf16[2,2,8,32,256]{4,3,2,1,0:T(8,128)(2,1)S(1)}, u32[]{:S(2)}, u32[]{:S(2)}) collective-permute-start(bf16[2,2,8,32,256]{4,3,2,1,0:T(8,128)(2,1)} %get-tuple-element.114), channel_id=1, source_target_pairs={{0,12},{4,16},{8,20},{12,24},{16,28},{20,0},{24,4},{28,8},{1,13},{... | collective-permute-start | bytes 1572872 | tf_op jit(solution)/shard_map/ppermute | solution.py:396
  262.6 43.7 %collective-permute-done.30.rest_3_ = bf16[2,8,32,256]{3,2,1,0:T(8,128)(2,1)S(1)} collective-permute-done((bf16[2,8,32,256]{3,2,1,0:T(8,128)(2,1)S(1)}, bf16[2,8,32,256]{3,2,1,0:T(8,128)(2,1)S(1)}, u32[]{:S(2)}, u32[]{:S(2)}) %collective-permute-start.30) | collective-permute-done | bytes 262176 | tf_op jit(solution)/shard_map/ppermute | solution.py:396
  306.2 9.2 %collective-permute-done.31.rest_4_ = bf16[2,8,32,256]{3,2,1,0:T(8,128)(2,1)S(1)} collective-permute-done((bf16[2,8,32,256]{3,2,1,0:T(8,128)(2,1)}, bf16[2,8,32,256]{3,2,1,0:T(8,128)(2,1)S(1)}, u32[]{:S(2)}, u32[]{:S(2)}) %collective-permute-start.31) | collective-permute-done | bytes 262176 | tf_op jit(solution)/shard_map/ppermute | solution.py:396
  316.5 10.2 %collective-permute-start.25 = (bf16[2,2,8,32,256]{4,3,2,1,0:T(8,128)(2,1)}, bf16[2,2,8,32,256]{4,3,2,1,0:T(8,128)(2,1)S(1)}, u32[]{:S(2)}, u32[]{:S(2)}) collective-permute-start(bf16[2,2,8,32,256]{4,3,2,1,0:T(8,128)(2,1)} %get-tuple-element.116), channel_id=1, source_target_pairs={{0,20},{4,24},{8,28},{12,0},{16,4},{20,8},{24,12},{28,16},{1,21},{... | collective-permute-start | bytes 1572872 | tf_op jit(solution)/shard_map/ppermute | solution.py:396
  329.4 14.0 %collective-permute-done.24.rest_4_ = bf16[2,2,8,32,256]{4,3,2,1,0:T(8,128)(2,1)S(1)} collective-permute-done((bf16[2,2,8,32,256]{4,3,2,1,0:T(8,128)(2,1)}, bf16[2,2,8,32,256]{4,3,2,1,0:T(8,128)(2,1)S(1)}, u32[]{:S(2)}, u32[]{:S(2)}) %collective-permute-start.24) | collective-permute-done | bytes 524320 | tf_op jit(solution)/shard_map/ppermute | solution.py:396
  343.4 5.5 collective-permute-start.32
  351.2 27.6 %collective-permute-start.33 = (bf16[2,8,32,256]{3,2,1,0:T(8,128)(2,1)}, bf16[2,8,32,256]{3,2,1,0:T(8,128)(2,1)}, u32[]{:S(2)}, u32[]{:S(2)}) collective-permute-start(bf16[2,8,32,256]{3,2,1,0:T(8,128)(2,1)} %get-tuple-element.126), channel_id=1, source_target_pairs={{0,24},{4,28},{8,0},{12,4},{16,8},{20,12},{24,16},{28,20},{1,25},{... | collective-permute-start | bytes 786440 | tf_op jit(solution)/shard_map/ppermute | solution.py:396
  383.5 8.2 %polar.7 = (bf16[2,8,32,256]{3,2,1,0:T(8,128)(2,1)}, bf16[2,8,32,256]{3,2,1,0:T(8,128)(2,1)}, bf16[2,8,32,256]{3,2,1,0:T(8,128)(2,1)}, bf16[2,8,32,256]{3,2,1,0:...) custom-call(s32[1]{0:T(128)} %bitcast.token_ref.me_ref, ...), custom_call_target="tpu_custom_call" | custom-call | tf_op jit(solution)/shard_map/polar/pallas_call | solution.py:214
  403.1 8.1 %collective-permute-done.38.rest_1_ = bf16[2,8,32,256]{3,2,1,0:T(8,128)(2,1)S(1)} collective-permute-done((bf16[2,8,32,256]{3,2,1,0:T(8,128)(2,1)S(1)}, bf16[2,8,32,256]{3,2,1,0:T(8,128)(2,1)S(1)}, u32[]{:S(2)}, u32[]{:S(2)}) %collective-permute-start.38) | collective-permute-done | bytes 262176 | tf_op jit(solution)/shard_map/ppermute | solution.py:396
  412.3 20.2 %collective-permute-done.40.rest_3_ = bf16[2,8,32,256]{3,2,1,0:T(8,128)(2,1)S(1)} collective-permute-done((bf16[2,8,32,256]{3,2,1,0:T(8,128)(2,1)S(1)}, bf16[2,8,32,256]{3,2,1,0:T(8,128)(2,1)S(1)}, u32[]{:S(2)}, u32[]{:S(2)}) %collective-permute-start.40) | collective-permute-done | bytes 262176 | tf_op jit(solution)/shard_map/ppermute | solution.py:396
  432.6 4.8 collective-permute-start.43
  437.4 6.4 collective-permute-done.42.rest_5_
  446.5 10.5 %left.3.token_ref.rest_0_.rest_1_ = bf16[2,8,256,256]{3,2,1,0:T(8,128)(2,1)} custom-call(s32[6]{0:T(128)} %stack.27.index_ref, bf16[2,8,1024,1024]{3,2,1,0:T(8,128)(2,1)} %coulomb_ref.3, bf16[8,2,8,32,256]{4,3,2,1,0:T(8,128)(2,1)} %join.7.token_ref.rest_0_, bf16[8,2,8,32,256]{4,3,2,1,0:T(8,128)(2,1)} %join.6.token_ref.rest_0_, ...), custom_call_target="tpu_custom_call" | custom-call | tf_op jit(solution)/shard_map/left/pallas_call | solution.py:285
  467.0 6.8 collective-permute-done.46.rest_2_
  474.1 15.9 %collective-permute-done.47.rest_3_ = bf16[2,2,8,32,128]{4,3,2,1,0:T(8,128)(2,1)S(1)} collective-permute-done((bf16[2,2,8,32,128]{4,3,2,1,0:T(8,128)(2,1)}, bf16[2,2,8,32,128]{4,3,2,1,0:T(8,128)(2,1)S(1)}, u32[]{:S(2)}, u32[]{:S(2)}) %collective-permute-start.47) | collective-permute-done | bytes 262176 | tf_op jit(solution)/shard_map/ppermute | solution.py:396
  496.4 4.9 collective-permute-done.49.rest_5_
  510.2 7.9 %collective-permute-done.55.rest_1_ = bf16[2,2,8,32,128]{4,3,2,1,0:T(8,128)(2,1)S(1)} collective-permute-done((bf16[2,2,8,32,128]{4,3,2,1,0:T(8,128)(2,1)}, bf16[2,2,8,32,128]{4,3,2,1,0:T(8,128)(2,1)S(1)}, u32[]{:S(2)}, u32[]{:S(2)}) %collective-permute-start.55) | collective-permute-done | bytes 262176 | tf_op jit(solution)/shard_map/ppermute | solution.py:396
  519.3 7.5 %collective-permute-done.56.rest_2_ = bf16[2,2,8,32,128]{4,3,2,1,0:T(8,128)(2,1)S(1)} collective-permute-done((bf16[2,2,8,32,128]{4,3,2,1,0:T(8,128)(2,1)}, bf16[2,2,8,32,128]{4,3,2,1,0:T(8,128)(2,1)S(1)}, u32[]{:S(2)}, u32[]{:S(2)}) %collective-permute-start.56) | collective-permute-done | bytes 262176 | tf_op jit(solution)/shard_map/ppermute | solution.py:396
  526.9 13.1 %collective-permute-done.57.rest_3_ = bf16[2,2,8,32,128]{4,3,2,1,0:T(8,128)(2,1)S(1)} collective-permute-done((bf16[2,2,8,32,128]{4,3,2,1,0:T(8,128)(2,1)}, bf16[2,2,8,32,128]{4,3,2,1,0:T(8,128)(2,1)S(1)}, u32[]{:S(2)}, u32[]{:S(2)}) %collective-permute-start.57) | collective-permute-done | bytes 262176 | tf_op jit(solution)/shard_map/ppermute | solution.py:396
  540.0 6.6 collective-permute-done.58.rest_4_
  557.9 5.1 polar.8
  565.5 6.9 collective-permute-done.62.rest_1_
  574.2 9.1 %collective-permute-done.64.rest_3_ = bf16[2,8,32,128]{3,2,1,0:T(8,128)(2,1)S(1)} collective-permute-done((bf16[2,8,32,128]{3,2,1,0:T(8,128)(2,1)}, bf16[2,8,32,128]{3,2,1,0:T(8,128)(2,1)S(1)}, u32[]{:S(2)}, u32[]{:S(2)}) %collective-permute-start.64) | collective-permute-done | bytes 131104 | tf_op jit(solution)/shard_map/ppermute | solution.py:396
  588.1 10.5 %left.4.token_ref.rest_1_.rest_2_ = bf16[2,8,256,256]{3,2,1,0:T(8,128)(2,1)} custom-call(s32[6]{0:T(128)} %stack.27.index_ref, bf16[2,8,1024,1024]{3,2,1,0:T(8,128)(2,1)} %coulomb_ref.3, bf16[2,8,32,128]{3,2,1,0:T(8,128)(2,1)} %get-tuple-element.142.token_ref.rest_0_, bf16[8,2,8,32,256]{4,3,2,1,0:T(8,128)(2,1)} %join.7.token_ref.rest_0_, ...), custom_call_target="tpu_custom_call" | custom-call | tf_op jit(solution)/shard_map/left/pallas_call | solution.py:285
  598.6 5.1 polar.9
  614.9 5.7 collective-permute-done.71.rest_3_
  623.4 4.7 collective-permute-done.73.rest_5_
  628.1 4.8 collective-permute-start.75
  643.3 6.8 collective-permute-done.82.rest_8_
  650.7 13.1 %collective-permute-done.85.rest_9_ = bf16[8,2,5,32,128]{4,3,2,1,0:T(8,128)(2,1)} collective-permute-done((bf16[8,2,5,32,128]{4,3,2,1,0:T(8,128)(2,1)}, bf16[8,2,5,32,128]{4,3,2,1,0:T(8,128)(2,1)}, u32[]{:S(2)}, u32[]{:S(2)}) %collective-permute-start.85) | collective-permute-done | bytes 655392 | tf_op jit(solution)/shard_map/ppermute | solution.py:403
  664.3 10.5 %left.5.rest_2_.rest_3_ = bf16[2,8,256,256]{3,2,1,0:T(8,128)(2,1)} custom-call(s32[6]{0:T(128)} %stack.27.index_ref, bf16[2,8,1024,1024]{3,2,1,0:T(8,128)(2,1)} %coulomb_ref.3, bf16[8,2,5,32,128]{4,3,2,1,0:T(8,128)(2,1)} %join.11.token_ref.rest_8_, bf16[8,2,8,32,256]{4,3,2,1,0:T(8,128)(2,1)} %join.8.token_ref.rest_0_, ...), custom_call_target="tpu_custom_call" | custom-call | tf_op jit(solution)/shard_map/left/pallas_call | solution.py:285
  675.8 14.3 %shard_map.42.rest_0_ = f32[2,8,256,1024]{3,2,1,0:T(8,128)} custom-call(s32[6]{0:T(128)} %stack.27.index_ref, bf16[2,8,1024,1024]{3,2,1,0:T(8,128)(2,1)} %coulomb_ref.3, bf16[2,8,256,256]{3,2,1,0:T(8,128)(2,1)} %left.3.token_ref.rest_0_.rest_1_, bf16[2,8,256,256]{3,2,1,0:T(8,128)(2,1)} %left.4.token_ref.rest_1_.rest_2_, ...), custom_call_target="tpu_custom_call" | custom-call | tf_op jit(solution)/shard_map/pallas_call | solution.py:340
  690.1 21.0 %shard_map.43 = f32[2,8,256,1024]{3,2,1,0:T(8,128)} custom-call(s32[6]{0:T(128)} %stack.27.index_ref, bf16[2,8,1024,1024]{3,2,1,0:T(8,128)(2,1)} %coulomb_ref.3, f32[2,8,256,1024]{3,2,1,0:T(8,128)} %shard_map.42.rest_0_, bf16[2,8,256,256]{3,2,1,0:T(8,128)(2,1)} %left.3.token_ref.rest_0_.rest_1_, ...), custom_call_target="tpu_custom_call", output_to_operand_aliasing={{}: (2, {})} | custom-call | tf_op jit(solution)/shard_map/pallas_call | solution.py:340
  (306 shorter events, 155.7 us)
Async XLA Ops:
  8.3 22.6 %collective-permute-start.1 = (bf16[2,2,8,32,256]{4,3,2,1,0:T(8,128)(2,1)}, bf16[2,2,8,32,256]{4,3,2,1,0:T(8,128)(2,1)S(1)}, u32[]{:S(2)}, u32[]{:S(2)}) collective-permute-start(bf16[2,2,8,32,256]{4,3,2,1,0:T(8,128)(2,1)} %get-tuple-element.88), channel_id=1, source_target_pairs={{0,8},{4,12},{8,16},{12,20},{16,24},{20,28},{24,0},{28,4},{1,9},{5... | collective-permute-start | bytes 1572872 | tf_op jit(solution)/shard_map/ppermute | solution.py:396
  9.9 58.7 %collective-permute-start.2 = (bf16[2,2,8,32,256]{4,3,2,1,0:T(8,128)(2,1)}, bf16[2,2,8,32,256]{4,3,2,1,0:T(8,128)(2,1)S(1)}, u32[]{:S(2)}, u32[]{:S(2)}) collective-permute-start(bf16[2,2,8,32,256]{4,3,2,1,0:T(8,128)(2,1)} %get-tuple-element.89), channel_id=1, source_target_pairs={{0,12},{4,16},{8,20},{12,24},{16,28},{20,0},{24,4},{28,8},{1,13},{... | collective-permute-start | bytes 1572872 | tf_op jit(solution)/shard_map/ppermute | solution.py:396
  12.4 56.4 %collective-permute-start.3 = (bf16[2,2,8,32,256]{4,3,2,1,0:T(8,128)(2,1)}, bf16[2,2,8,32,256]{4,3,2,1,0:T(8,128)(2,1)S(1)}, u32[]{:S(2)}, u32[]{:S(2)}) collective-permute-start(bf16[2,2,8,32,256]{4,3,2,1,0:T(8,128)(2,1)} %get-tuple-element.90), channel_id=1, source_target_pairs={{0,16},{4,20},{8,24},{12,28},{16,0},{20,4},{24,8},{28,12},{1,17},{... | collective-permute-start | bytes 1572872 | tf_op jit(solution)/shard_map/ppermute | solution.py:396
  13.6 77.9 %collective-permute-start.4 = (bf16[2,2,8,32,256]{4,3,2,1,0:T(8,128)(2,1)}, bf16[2,2,8,32,256]{4,3,2,1,0:T(8,128)(2,1)S(1)}, u32[]{:S(2)}, u32[]{:S(2)}) collective-permute-start(bf16[2,2,8,32,256]{4,3,2,1,0:T(8,128)(2,1)} %get-tuple-element.91), channel_id=1, source_target_pairs={{0,20},{4,24},{8,28},{12,0},{16,4},{20,8},{24,12},{28,16},{1,21},{... | collective-permute-start | bytes 1572872 | tf_op jit(solution)/shard_map/ppermute | solution.py:396
  24.5 78.5 %collective-permute-start.5 = (bf16[2,2,8,32,256]{4,3,2,1,0:T(8,128)(2,1)}, bf16[2,2,8,32,256]{4,3,2,1,0:T(8,128)(2,1)S(1)}, u32[]{:S(2)}, u32[]{:S(2)}) collective-permute-start(bf16[2,2,8,32,256]{4,3,2,1,0:T(8,128)(2,1)} %get-tuple-element.92), channel_id=1, source_target_pairs={{0,24},{4,28},{8,0},{12,4},{16,8},{20,12},{24,16},{28,20},{1,25},{... | collective-permute-start | bytes 1572872 | tf_op jit(solution)/shard_map/ppermute | solution.py:396
  31.0 76.1 %collective-permute-start.6 = (bf16[2,2,8,32,256]{4,3,2,1,0:T(8,128)(2,1)}, bf16[2,2,8,32,256]{4,3,2,1,0:T(8,128)(2,1)S(1)}, u32[]{:S(2)}, u32[]{:S(2)}) collective-permute-start(bf16[2,2,8,32,256]{4,3,2,1,0:T(8,128)(2,1)} %get-tuple-element.93), channel_id=1, source_target_pairs={{0,28},{4,0},{8,4},{12,8},{16,12},{20,16},{24,20},{28,24},{1,29},{... | collective-permute-start | bytes 1572872 | tf_op jit(solution)/shard_map/ppermute | solution.py:396
  68.6 67.9 %collective-permute-start.7 = (bf16[2,2,8,32,256]{4,3,2,1,0:T(8,128)(2,1)}, bf16[2,2,8,32,256]{4,3,2,1,0:T(8,128)(2,1)S(1)}, u32[]{:S(2)}, u32[]{:S(2)}) collective-permute-start(bf16[2,2,8,32,256]{4,3,2,1,0:T(8,128)(2,1)} %get-tuple-element.96), channel_id=1, source_target_pairs={{0,4},{4,8},{8,12},{12,16},{16,20},{20,24},{24,28},{28,0},{1,5},{5... | collective-permute-start | bytes 1572872 | tf_op jit(solution)/shard_map/ppermute | solution.py:396
  69.4 70.7 %collective-permute-start.8 = (bf16[2,2,8,32,256]{4,3,2,1,0:T(8,128)(2,1)}, bf16[2,2,8,32,256]{4,3,2,1,0:T(8,128)(2,1)S(1)}, u32[]{:S(2)}, u32[]{:S(2)}) collective-permute-start(bf16[2,2,8,32,256]{4,3,2,1,0:T(8,128)(2,1)} %get-tuple-element.97), channel_id=1, source_target_pairs={{0,8},{4,12},{8,16},{12,20},{16,24},{20,28},{24,0},{28,4},{1,9},{5... | collective-permute-start | bytes 1572872 | tf_op jit(solution)/shard_map/ppermute | solution.py:396
  91.5 67.1 %collective-permute-start.9 = (bf16[2,2,8,32,256]{4,3,2,1,0:T(8,128)(2,1)}, bf16[2,2,8,32,256]{4,3,2,1,0:T(8,128)(2,1)S(1)}, u32[]{:S(2)}, u32[]{:S(2)}) collective-permute-start(bf16[2,2,8,32,256]{4,3,2,1,0:T(8,128)(2,1)} %get-tuple-element.98), channel_id=1, source_target_pairs={{0,12},{4,16},{8,20},{12,24},{16,28},{20,0},{24,4},{28,8},{1,13},{... | collective-permute-start | bytes 1572872 | tf_op jit(solution)/shard_map/ppermute | solution.py:396
  103.0 55.9 %collective-permute-start.10 = (bf16[2,2,8,32,256]{4,3,2,1,0:T(8,128)(2,1)}, bf16[2,2,8,32,256]{4,3,2,1,0:T(8,128)(2,1)S(1)}, u32[]{:S(2)}, u32[]{:S(2)}) collective-permute-start(bf16[2,2,8,32,256]{4,3,2,1,0:T(8,128)(2,1)} %get-tuple-element.99), channel_id=1, source_target_pairs={{0,16},{4,20},{8,24},{12,28},{16,0},{20,4},{24,8},{28,12},{1,17},{... | collective-permute-start | bytes 1572872 | tf_op jit(solution)/shard_map/ppermute | solution.py:396
  107.0 74.4 %collective-permute-start.11 = (bf16[2,2,8,32,256]{4,3,2,1,0:T(8,128)(2,1)}, bf16[2,2,8,32,256]{4,3,2,1,0:T(8,128)(2,1)S(1)}, u32[]{:S(2)}, u32[]{:S(2)}) collective-permute-start(bf16[2,2,8,32,256]{4,3,2,1,0:T(8,128)(2,1)} %get-tuple-element.100), channel_id=1, source_target_pairs={{0,20},{4,24},{8,28},{12,0},{16,4},{20,8},{24,12},{28,16},{1,21},{... | collective-permute-start | bytes 1572872 | tf_op jit(solution)/shard_map/ppermute | solution.py:396
  136.5 55.7 %collective-permute-start.12 = (bf16[2,2,8,32,256]{4,3,2,1,0:T(8,128)(2,1)}, bf16[2,2,8,32,256]{4,3,2,1,0:T(8,128)(2,1)S(1)}, u32[]{:S(2)}, u32[]{:S(2)}) collective-permute-start(bf16[2,2,8,32,256]{4,3,2,1,0:T(8,128)(2,1)} %get-tuple-element.101), channel_id=1, source_target_pairs={{0,24},{4,28},{8,0},{12,4},{16,8},{20,12},{24,16},{28,20},{1,25},{... | collective-permute-start | bytes 1572872 | tf_op jit(solution)/shard_map/ppermute | solution.py:396
  140.1 56.8 %collective-permute-start.13 = (bf16[2,2,8,32,256]{4,3,2,1,0:T(8,128)(2,1)}, bf16[2,2,8,32,256]{4,3,2,1,0:T(8,128)(2,1)}, u32[]{:S(2)}, u32[]{:S(2)}) collective-permute-start(bf16[2,2,8,32,256]{4,3,2,1,0:T(8,128)(2,1)} %get-tuple-element.102), channel_id=1, source_target_pairs={{0,28},{4,0},{8,4},{12,8},{16,12},{20,16},{24,20},{28,24},{1,29},{... | collective-permute-start | bytes 1572872 | tf_op jit(solution)/shard_map/ppermute | solution.py:396
  158.6 50.5 %collective-permute-start.14 = (bf16[2,8,32,256]{3,2,1,0:T(8,128)(2,1)}, bf16[2,8,32,256]{3,2,1,0:T(8,128)(2,1)S(1)}, u32[]{:S(2)}, u32[]{:S(2)}) collective-permute-start(bf16[2,8,32,256]{3,2,1,0:T(8,128)(2,1)} %get-tuple-element.105), channel_id=1, source_target_pairs={{0,4},{4,8},{8,12},{12,16},{16,20},{20,24},{24,28},{28,0},{1,5},{5... | collective-permute-start | bytes 786440 | tf_op jit(solution)/shard_map/ppermute | solution.py:396
  158.9 55.0 %collective-permute-start.15 = (bf16[2,8,32,256]{3,2,1,0:T(8,128)(2,1)}, bf16[2,8,32,256]{3,2,1,0:T(8,128)(2,1)S(1)}, u32[]{:S(2)}, u32[]{:S(2)}) collective-permute-start(bf16[2,8,32,256]{3,2,1,0:T(8,128)(2,1)} %get-tuple-element.106), channel_id=1, source_target_pairs={{0,8},{4,12},{8,16},{12,20},{16,24},{20,28},{24,0},{28,4},{1,9},{5... | collective-permute-start | bytes 786440 | tf_op jit(solution)/shard_map/ppermute | solution.py:396
  181.4 49.0 %collective-permute-start.16 = (bf16[2,8,32,256]{3,2,1,0:T(8,128)(2,1)}, bf16[2,8,32,256]{3,2,1,0:T(8,128)(2,1)S(1)}, u32[]{:S(2)}, u32[]{:S(2)}) collective-permute-start(bf16[2,8,32,256]{3,2,1,0:T(8,128)(2,1)} %get-tuple-element.107), channel_id=1, source_target_pairs={{0,12},{4,16},{8,20},{12,24},{16,28},{20,0},{24,4},{28,8},{1,13},{... | collective-permute-start | bytes 786440 | tf_op jit(solution)/shard_map/ppermute | solution.py:396
  192.2 38.3 %collective-permute-start.17 = (bf16[2,8,32,256]{3,2,1,0:T(8,128)(2,1)}, bf16[2,8,32,256]{3,2,1,0:T(8,128)(2,1)S(1)}, u32[]{:S(2)}, u32[]{:S(2)}) collective-permute-start(bf16[2,8,32,256]{3,2,1,0:T(8,128)(2,1)} %get-tuple-element.108), channel_id=1, source_target_pairs={{0,16},{4,20},{8,24},{12,28},{16,0},{20,4},{24,8},{28,12},{1,17},{... | collective-permute-start | bytes 786440 | tf_op jit(solution)/shard_map/ppermute | solution.py:396
  196.9 33.6 %collective-permute-start.18 = (bf16[2,8,32,256]{3,2,1,0:T(8,128)(2,1)}, bf16[2,8,32,256]{3,2,1,0:T(8,128)(2,1)S(1)}, u32[]{:S(2)}, u32[]{:S(2)}) collective-permute-start(bf16[2,8,32,256]{3,2,1,0:T(8,128)(2,1)} %get-tuple-element.109), channel_id=1, source_target_pairs={{0,20},{4,24},{8,28},{12,0},{16,4},{20,8},{24,12},{28,16},{1,21},{... | collective-permute-start | bytes 786440 | tf_op jit(solution)/shard_map/ppermute | solution.py:396
  209.1 21.5 %collective-permute-start.19 = (bf16[2,8,32,256]{3,2,1,0:T(8,128)(2,1)}, bf16[2,8,32,256]{3,2,1,0:T(8,128)(2,1)}, u32[]{:S(2)}, u32[]{:S(2)}) collective-permute-start(bf16[2,8,32,256]{3,2,1,0:T(8,128)(2,1)} %get-tuple-element.110), channel_id=1, source_target_pairs={{0,24},{4,28},{8,0},{12,4},{16,8},{20,12},{24,16},{28,20},{1,25},{... | collective-permute-start | bytes 786440 | tf_op jit(solution)/shard_map/ppermute | solution.py:396
  234.2 149.1 %collective-permute-start.35 = (bf16[8,2,8,32,256]{4,3,2,1,0:T(8,128)(2,1)}, bf16[8,2,8,32,256]{4,3,2,1,0:T(8,128)(2,1)}, u32[]{:S(2)}, u32[]{:S(2)}) collective-permute-start(bf16[8,2,8,32,256]{4,3,2,1,0:T(8,128)(2,1)} %join.6.token_ref.rest_0_), channel_id=1, source_target_pairs={{0,2},{1,3},{2,0},{3,1},{4,6},{5,7},{6,4},{7,5},{8,10},{9,11},{10,... | collective-permute-start | bytes 6291464 | tf_op jit(solution)/shard_map/ppermute | solution.py:403
  244.5 61.7 %collective-permute-start.30 = (bf16[2,8,32,256]{3,2,1,0:T(8,128)(2,1)S(1)}, bf16[2,8,32,256]{3,2,1,0:T(8,128)(2,1)S(1)}, u32[]{:S(2)}, u32[]{:S(2)}) collective-permute-start(bf16[2,8,32,256]{3,2,1,0:T(8,128)(2,1)S(1)} %copy-done.69), channel_id=1, source_target_pairs={{0,12},{4,16},{8,20},{12,24},{16,28},{20,0},{24,4},{28,8},{1,13},{... | collective-permute-start | bytes 786440 | tf_op jit(solution)/shard_map/ppermute | solution.py:396
  244.5 72.0 %collective-permute-start.21 = (bf16[2,2,8,32,256]{4,3,2,1,0:T(8,128)(2,1)S(1)}, bf16[2,2,8,32,256]{4,3,2,1,0:T(8,128)(2,1)S(1)}, u32[]{:S(2)}, u32[]{:S(2)}) collective-permute-start(bf16[2,2,8,32,256]{4,3,2,1,0:T(8,128)(2,1)S(1)} %copy-done.64), channel_id=1, source_target_pairs={{0,4},{4,8},{8,12},{12,16},{16,20},{20,24},{24,28},{28,0},{1,5},{5... | collective-permute-start | bytes 1572872 | tf_op jit(solution)/shard_map/ppermute | solution.py:396
  252.3 74.3 %collective-permute-start.22 = (bf16[2,2,8,32,256]{4,3,2,1,0:T(8,128)(2,1)S(1)}, bf16[2,2,8,32,256]{4,3,2,1,0:T(8,128)(2,1)S(1)}, u32[]{:S(2)}, u32[]{:S(2)}) collective-permute-start(bf16[2,2,8,32,256]{4,3,2,1,0:T(8,128)(2,1)S(1)} %copy-done.63), channel_id=1, source_target_pairs={{0,8},{4,12},{8,16},{12,20},{16,24},{20,28},{24,0},{28,4},{1,9},{5... | collective-permute-start | bytes 1572872 | tf_op jit(solution)/shard_map/ppermute | solution.py:396
  253.5 76.0 %collective-permute-start.23 = (bf16[2,2,8,32,256]{4,3,2,1,0:T(8,128)(2,1)}, bf16[2,2,8,32,256]{4,3,2,1,0:T(8,128)(2,1)S(1)}, u32[]{:S(2)}, u32[]{:S(2)}) collective-permute-start(bf16[2,2,8,32,256]{4,3,2,1,0:T(8,128)(2,1)} %get-tuple-element.114), channel_id=1, source_target_pairs={{0,12},{4,16},{8,20},{12,24},{16,28},{20,0},{24,4},{28,8},{1,13},{... | collective-permute-start | bytes 1572872 | tf_op jit(solution)/shard_map/ppermute | solution.py:396
  316.2 27.2 %collective-permute-start.24 = (bf16[2,2,8,32,256]{4,3,2,1,0:T(8,128)(2,1)}, bf16[2,2,8,32,256]{4,3,2,1,0:T(8,128)(2,1)S(1)}, u32[]{:S(2)}, u32[]{:S(2)}) collective-permute-start(bf16[2,2,8,32,256]{4,3,2,1,0:T(8,128)(2,1)} %get-tuple-element.115), channel_id=1, source_target_pairs={{0,16},{4,20},{8,24},{12,28},{16,0},{20,4},{24,8},{28,12},{1,17},{... | collective-permute-start | bytes 1572872 | tf_op jit(solution)/shard_map/ppermute | solution.py:396
  316.5 34.7 %collective-permute-start.25 = (bf16[2,2,8,32,256]{4,3,2,1,0:T(8,128)(2,1)}, bf16[2,2,8,32,256]{4,3,2,1,0:T(8,128)(2,1)S(1)}, u32[]{:S(2)}, u32[]{:S(2)}) collective-permute-start(bf16[2,2,8,32,256]{4,3,2,1,0:T(8,128)(2,1)} %get-tuple-element.116), channel_id=1, source_target_pairs={{0,20},{4,24},{8,28},{12,0},{16,4},{20,8},{24,12},{28,16},{1,21},{... | collective-permute-start | bytes 1572872 | tf_op jit(solution)/shard_map/ppermute | solution.py:396
  326.6 52.2 %collective-permute-start.26 = (bf16[2,2,8,32,256]{4,3,2,1,0:T(8,128)(2,1)}, bf16[2,2,8,32,256]{4,3,2,1,0:T(8,128)(2,1)S(1)}, u32[]{:S(2)}, u32[]{:S(2)}) collective-permute-start(bf16[2,2,8,32,256]{4,3,2,1,0:T(8,128)(2,1)} %get-tuple-element.117), channel_id=1, source_target_pairs={{0,24},{4,28},{8,0},{12,4},{16,8},{20,12},{24,16},{28,20},{1,25},{... | collective-permute-start | bytes 1572872 | tf_op jit(solution)/shard_map/ppermute | solution.py:396
  329.4 49.4 %collective-permute-start.27 = (bf16[2,2,8,32,256]{4,3,2,1,0:T(8,128)(2,1)}, bf16[2,2,8,32,256]{4,3,2,1,0:T(8,128)(2,1)}, u32[]{:S(2)}, u32[]{:S(2)}) collective-permute-start(bf16[2,2,8,32,256]{4,3,2,1,0:T(8,128)(2,1)} %get-tuple-element.118), channel_id=1, source_target_pairs={{0,28},{4,0},{8,4},{12,8},{16,12},{20,16},{24,20},{28,24},{1,29},{... | collective-permute-start | bytes 1572872 | tf_op jit(solution)/shard_map/ppermute | solution.py:396
  343.4 51.9 %collective-permute-start.32 = (bf16[2,8,32,256]{3,2,1,0:T(8,128)(2,1)}, bf16[2,8,32,256]{3,2,1,0:T(8,128)(2,1)}, u32[]{:S(2)}, u32[]{:S(2)}) collective-permute-start(bf16[2,8,32,256]{3,2,1,0:T(8,128)(2,1)} %get-tuple-element.125), channel_id=1, source_target_pairs={{0,20},{4,24},{8,28},{12,0},{16,4},{20,8},{24,12},{28,16},{1,21},{... | collective-permute-start | bytes 786440 | tf_op jit(solution)/shard_map/ppermute | solution.py:396
  351.2 44.1 %collective-permute-start.33 = (bf16[2,8,32,256]{3,2,1,0:T(8,128)(2,1)}, bf16[2,8,32,256]{3,2,1,0:T(8,128)(2,1)}, u32[]{:S(2)}, u32[]{:S(2)}) collective-permute-start(bf16[2,8,32,256]{3,2,1,0:T(8,128)(2,1)} %get-tuple-element.126), channel_id=1, source_target_pairs={{0,24},{4,28},{8,0},{12,4},{16,8},{20,12},{24,16},{28,20},{1,25},{... | collective-permute-start | bytes 786440 | tf_op jit(solution)/shard_map/ppermute | solution.py:396
  378.8 65.0 %collective-permute-start.36 = (bf16[8,2,8,32,256]{4,3,2,1,0:T(8,128)(2,1)}, bf16[8,2,8,32,256]{4,3,2,1,0:T(8,128)(2,1)}, u32[]{:S(2)}, u32[]{:S(2)}) collective-permute-start(bf16[8,2,8,32,256]{4,3,2,1,0:T(8,128)(2,1)} %join.6.token_ref.rest_0_), channel_id=1, source_target_pairs={{0,1},{1,0},{2,3},{3,2},{4,5},{5,4},{6,7},{7,6},{8,9},{9,8},{10,11... | collective-permute-start | bytes 6291464 | tf_op jit(solution)/shard_map/ppermute | solution.py:412
  383.3 60.6 %collective-permute-start.37 = (bf16[8,2,8,32,256]{4,3,2,1,0:T(8,128)(2,1)}, bf16[8,2,8,32,256]{4,3,2,1,0:T(8,128)(2,1)}, u32[]{:S(2)}, u32[]{:S(2)}) collective-permute-start(bf16[8,2,8,32,256]{4,3,2,1,0:T(8,128)(2,1)} %collective-permute-done.35.rest_1_), channel_id=1, source_target_pairs={{0,1},{1,0},{2,3},{3,2},{4,5},{5,4},{6,7},{7,6},{8,9},{9,8},{10,11... | collective-permute-start | bytes 6291464 | tf_op jit(solution)/shard_map/ppermute | solution.py:412
  398.1 64.5 %collective-permute-start.52 = (bf16[8,2,8,32,256]{4,3,2,1,0:T(8,128)(2,1)}, bf16[8,2,8,32,256]{4,3,2,1,0:T(8,128)(2,1)S(1)}, u32[]{:S(2)}, u32[]{:S(2)}) collective-permute-start(bf16[8,2,8,32,256]{4,3,2,1,0:T(8,128)(2,1)} %join.7.token_ref.rest_0_), channel_id=1, source_target_pairs={{0,2},{1,3},{2,0},{3,1},{4,6},{5,7},{6,4},{7,5},{8,10},{9,11},{10,... | collective-permute-start | bytes 6291464 | tf_op jit(solution)/shard_map/ppermute | solution.py:403
  432.6 24.4 %collective-permute-start.43 = (bf16[2,8,32,256]{3,2,1,0:T(8,128)(2,1)}, bf16[2,8,32,256]{3,2,1,0:T(8,128)(2,1)}, u32[]{:S(2)}, u32[]{:S(2)}) collective-permute-start(bf16[2,8,32,256]{3,2,1,0:T(8,128)(2,1)} %get-tuple-element.133), channel_id=1, source_target_pairs={{0,24},{4,28},{8,0},{12,4},{16,8},{20,12},{24,16},{28,20},{1,25},{... | collective-permute-start | bytes 786440 | tf_op jit(solution)/shard_map/ppermute | solution.py:396
  443.8 121.1 %collective-permute-start.53 = (bf16[8,2,8,32,256]{4,3,2,1,0:T(8,128)(2,1)}, bf16[8,2,8,32,256]{4,3,2,1,0:T(8,128)(2,1)}, u32[]{:S(2)}, u32[]{:S(2)}) collective-permute-start(bf16[8,2,8,32,256]{4,3,2,1,0:T(8,128)(2,1)} %join.7.token_ref.rest_0_), channel_id=1, source_target_pairs={{0,1},{1,0},{2,3},{3,2},{4,5},{5,4},{6,7},{7,6},{8,9},{9,8},{10,11... | collective-permute-start | bytes 6291464 | tf_op jit(solution)/shard_map/ppermute | solution.py:412
  459.8 112.6 %collective-permute-start.76 = (bf16[8,2,8,32,256]{4,3,2,1,0:T(8,128)(2,1)}, bf16[8,2,8,32,256]{4,3,2,1,0:T(8,128)(2,1)}, u32[]{:S(2)}, u32[]{:S(2)}) collective-permute-start(bf16[8,2,8,32,256]{4,3,2,1,0:T(8,128)(2,1)} %join.8.token_ref.rest_0_), channel_id=1, source_target_pairs={{0,2},{1,3},{2,0},{3,1},{4,6},{5,7},{6,4},{7,5},{8,10},{9,11},{10,... | collective-permute-start | bytes 6291464 | tf_op jit(solution)/shard_map/ppermute | solution.py:403
  462.7 121.8 %collective-permute-start.54 = (bf16[8,2,8,32,256]{4,3,2,1,0:T(8,128)(2,1)S(1)}, bf16[8,2,8,32,256]{4,3,2,1,0:T(8,128)(2,1)}, u32[]{:S(2)}, u32[]{:S(2)}) collective-permute-start(bf16[8,2,8,32,256]{4,3,2,1,0:T(8,128)(2,1)S(1)} %collective-permute-done.52.rest_1_), channel_id=1, source_target_pairs={{0,1},{1,0},{2,3},{3,2},{4,5},{5,4},{6,7},{7,6},{8,9},{9,8},{10,11... | collective-permute-start | bytes 6291464 | tf_op jit(solution)/shard_map/ppermute | solution.py:412
  462.7 27.3 %collective-permute-start.47 = (bf16[2,2,8,32,128]{4,3,2,1,0:T(8,128)(2,1)}, bf16[2,2,8,32,128]{4,3,2,1,0:T(8,128)(2,1)S(1)}, u32[]{:S(2)}, u32[]{:S(2)}) collective-permute-start(bf16[2,2,8,32,128]{4,3,2,1,0:T(8,128)(2,1)} %get-tuple-element.137), channel_id=1, source_target_pairs={{0,12},{4,16},{8,20},{12,24},{16,28},{20,0},{24,4},{28,8},{1,13},{... | collective-permute-start | bytes 786440 | tf_op jit(solution)/shard_map/ppermute | solution.py:396
  518.1 21.9 %collective-permute-start.57 = (bf16[2,2,8,32,128]{4,3,2,1,0:T(8,128)(2,1)}, bf16[2,2,8,32,128]{4,3,2,1,0:T(8,128)(2,1)S(1)}, u32[]{:S(2)}, u32[]{:S(2)}) collective-permute-start(bf16[2,2,8,32,128]{4,3,2,1,0:T(8,128)(2,1)} %get-tuple-element.145), channel_id=1, source_target_pairs={{0,12},{4,16},{8,20},{12,24},{16,28},{20,0},{24,4},{28,8},{1,13},{... | collective-permute-start | bytes 786440 | tf_op jit(solution)/shard_map/ppermute | solution.py:396
  557.9 105.8 %collective-permute-start.77 = (bf16[8,2,8,32,256]{4,3,2,1,0:T(8,128)(2,1)}, bf16[8,2,8,32,256]{4,3,2,1,0:T(8,128)(2,1)}, u32[]{:S(2)}, u32[]{:S(2)}) collective-permute-start(bf16[8,2,8,32,256]{4,3,2,1,0:T(8,128)(2,1)} %join.8.token_ref.rest_0_), channel_id=1, source_target_pairs={{0,1},{1,0},{2,3},{3,2},{4,5},{5,4},{6,7},{7,6},{8,9},{9,8},{10,11... | collective-permute-start | bytes 6291464 | tf_op jit(solution)/shard_map/ppermute | solution.py:412
  572.4 91.8 %collective-permute-start.78 = (bf16[8,2,8,32,256]{4,3,2,1,0:T(8,128)(2,1)}, bf16[8,2,8,32,256]{4,3,2,1,0:T(8,128)(2,1)}, u32[]{:S(2)}, u32[]{:S(2)}) collective-permute-start(bf16[8,2,8,32,256]{4,3,2,1,0:T(8,128)(2,1)} %collective-permute-done.76.rest_1_), channel_id=1, source_target_pairs={{0,1},{1,0},{2,3},{3,2},{4,5},{5,4},{6,7},{7,6},{8,9},{9,8},{10,11... | collective-permute-start | bytes 6291464 | tf_op jit(solution)/shard_map/ppermute | solution.py:412
  584.4 21.4 %collective-permute-start.68 = (bf16[2,8,32,128]{3,2,1,0:T(8,128)(2,1)}, bf16[2,8,32,128]{3,2,1,0:T(8,128)(2,1)S(1)}, u32[]{:S(2)}, u32[]{:S(2)}) collective-permute-start(bf16[2,8,32,128]{3,2,1,0:T(8,128)(2,1)} %get-tuple-element.157), channel_id=1, source_target_pairs={{0,28},{4,0},{8,4},{12,8},{16,12},{20,16},{24,20},{28,24},{1,29},{... | collective-permute-start | bytes 393224 | tf_op jit(solution)/shard_map/ppermute | solution.py:396
  613.1 37.0 %collective-permute-start.79 = (bf16[8,2,8,32,128]{4,3,2,1,0:T(8,128)(2,1)}, bf16[8,2,8,32,128]{4,3,2,1,0:T(8,128)(2,1)S(1)}, u32[]{:S(2)}, u32[]{:S(2)}) collective-permute-start(bf16[8,2,8,32,128]{4,3,2,1,0:T(8,128)(2,1)} %join.9.token_ref.rest_3_.rest_4_), channel_id=1, source_target_pairs={{0,2},{1,3},{2,0},{3,1},{4,6},{5,7},{6,4},{7,5},{8,10},{9,11},{10,... | collective-permute-start | bytes 3145736 | tf_op jit(solution)/shard_map/ppermute | solution.py:403
  641.8 21.9 %collective-permute-start.85 = (bf16[8,2,5,32,128]{4,3,2,1,0:T(8,128)(2,1)}, bf16[8,2,5,32,128]{4,3,2,1,0:T(8,128)(2,1)}, u32[]{:S(2)}, u32[]{:S(2)}) collective-permute-start(bf16[8,2,5,32,128]{4,3,2,1,0:T(8,128)(2,1)} %join.11.token_ref.rest_8_), channel_id=1, source_target_pairs={{0,2},{1,3},{2,0},{3,1},{4,6},{5,7},{6,4},{7,5},{8,10},{9,11},{10,... | collective-permute-start | bytes 1966088 | tf_op jit(solution)/shard_map/ppermute | solution.py:403
  650.1 24.7 %collective-permute-start.80 = (bf16[8,2,8,32,128]{4,3,2,1,0:T(8,128)(2,1)S(1)}, bf16[8,2,8,32,128]{4,3,2,1,0:T(8,128)(2,1)S(1)}, u32[]{:S(2)}, u32[]{:S(2)}) collective-permute-start(bf16[8,2,8,32,128]{4,3,2,1,0:T(8,128)(2,1)S(1)} %copy-done), channel_id=1, source_target_pairs={{0,1},{1,0},{2,3},{3,2},{4,5},{5,4},{6,7},{7,6},{8,9},{9,8},{10,11... | collective-permute-start | bytes 3145736 | tf_op jit(solution)/shard_map/ppermute | solution.py:412
  650.2 24.7 %collective-permute-start.81 = (bf16[8,2,8,32,128]{4,3,2,1,0:T(8,128)(2,1)S(1)}, bf16[8,2,8,32,128]{4,3,2,1,0:T(8,128)(2,1)}, u32[]{:S(2)}, u32[]{:S(2)}) collective-permute-start(bf16[8,2,8,32,128]{4,3,2,1,0:T(8,128)(2,1)S(1)} %collective-permute-done.79.rest_4_.rest_5_), channel_id=1, source_target_pairs={{0,1},{1,0},{2,3},{3,2},{4,5},{5,4},{6,7},{7,6},{8,9},{9,8},{10,11... | collective-permute-start | bytes 3145736 | tf_op jit(solution)/shard_map/ppermute | solution.py:412
  663.7 26.4 %collective-permute-start.86 = (bf16[8,2,5,32,128]{4,3,2,1,0:T(8,128)(2,1)}, bf16[8,2,5,32,128]{4,3,2,1,0:T(8,128)(2,1)}, u32[]{:S(2)}, u32[]{:S(2)}) collective-permute-start(bf16[8,2,5,32,128]{4,3,2,1,0:T(8,128)(2,1)} %join.11.token_ref.rest_8_), channel_id=1, source_target_pairs={{0,1},{1,0},{2,3},{3,2},{4,5},{5,4},{6,7},{7,6},{8,9},{9,8},{10,11... | collective-permute-start | bytes 1966088 | tf_op jit(solution)/shard_map/ppermute | solution.py:412
  663.7 26.4 %collective-permute-start.87 = (bf16[8,2,5,32,128]{4,3,2,1,0:T(8,128)(2,1)}, bf16[8,2,5,32,128]{4,3,2,1,0:T(8,128)(2,1)}, u32[]{:S(2)}, u32[]{:S(2)}) collective-permute-start(bf16[8,2,5,32,128]{4,3,2,1,0:T(8,128)(2,1)} %collective-permute-done.85.rest_9_), channel_id=1, source_target_pairs={{0,1},{1,0},{2,3},{3,2},{4,5},{5,4},{6,7},{7,6},{8,9},{9,8},{10,11... | collective-permute-start | bytes 1966088 | tf_op jit(solution)/shard_map/ppermute | solution.py:412
  (118 other events, 2579.7 us)

commit v3 on v2

--- a/solution.py
+++ b/solution.py
@@ -367,11 +367,12 @@
     last = chunks - 1
     order = [("split", n, 0) for n in range(min(2, chunks))]
     for n in range(last):
-        soon = n == last - 1
-        if soon and n >= 1:
+        soon = n == last - 1 and n >= 1
+        if soon:
             order.append(("join", n - 1, 0))
         order.append(("transform", n, 0))
-        if n + 2 < chunks:
+        late = n + 2 == last and n >= 2
+        if n + 2 < chunks and not late:
             order.append(("split", n + 2, 0))
         if n >= 2:
             order.append(("ahead", n - 2, 0))
@@ -379,6 +380,8 @@
             order.append(("join", n - 1, 0))
         if n >= 2:
             order.append(("left", n - 2, 0))
+        if late:
+            order.append(("split", n + 2, 0))
     order += [("transform", last, 0), ("join", last - 1, 0), ("ahead", last - 2, 0)]
     order += [("join", last, g) for g in range(groups)]
     order += [("left", last - 2, 0), ("ahead", last - 1, 0)]

time: 712 us -> 764 us (1.073)
  starting transfers between devices: 272 us -> 314 us
  waiting for transfers between devices: 294 us -> 302 us
    ppermute x70, starting transfers between devices: 265 us -> 305 us  [exchange(): lax.ppermute(pieces[shift], 'kt', [(d, (d + shift) % count) for d in rang...]
    ppermute x6, waiting for transfers between devices: 19.9 us -> 29.1 us  [across_chips(): lax.ppermute(block, 'tile', [(t, (t // 2 + shift) % chips * 2 + t % 2) fo...]
  transfers between devices with their start and end apart: 88 -> 88, of which waited for: 35 -> 28; matrix products, arithmetic and copies ran while one was open for 0% -> 0% of each run, Pallas kernels for 15% -> 14%
where the time goes in v3:
time: 764 us; the launch traced here: 763 us
  starting transfers between devices  314 us (41%)
  waiting for transfers between devices  302 us (40%)
  Pallas kernels  139 us (18%)
  local copies, waits for them, and re-layouts  7.85 us (1%)
    ppermute x70, starting transfers between devices, exchange(): lax.ppermute(pieces[shift], 'kt', [(d, (d + shift) % count) for d in rang...  305 us
    ppermute x70, waiting for transfers between devices, exchange(): lax.ppermute(pieces[shift], 'kt', [(d, (d + shift) % count) for d in rang...  273 us
    pallas_call x2, Pallas kernels, screen_call(): pl.pallas_call(kernel, grid_spec=pltpu.PrefetchScalarGridSpec(num_scalar_...  35.2 us
    pallas_call x5, Pallas kernels, polar_call(): pl.pallas_call(polar_kernel(count, local), grid=(width // LANES, rows //...  34.9 us
    pallas_call x3, Pallas kernels, left_call(): pl.pallas_call(kernel, grid_spec=pltpu.PrefetchScalarGridSpec(num_scalar_...  31.4 us
    ppermute x6, waiting for transfers between devices, across_chips(): lax.ppermute(block, 'tile', [(t, (t // 2 + shift) % chips * 2 + t % 2) fo...  29.1 us
    pallas_call x5, Pallas kernels, split_call(): pl.pallas_call(kernel, grid_spec=pltpu.PrefetchScalarGridSpec(num_scalar_...  21.3 us
    pallas_call x6, Pallas kernels, join_call(): pl.pallas_call(kernel, grid=(momenta // part,), in_specs=[ANY] + [pl.Bloc...  15.8 us
  transfers between devices with their start and end apart: 88, of which 28 were waited for; matrix products, arithmetic and copies ran while one was open for 0% of the time, Pallas kernels for 14%

profile of v3, /device:TPU:0, one launch (start us, length us, event | category | flops | bytes accessed | tf_op | source)
XLA Modules:
  0.0 763.4 jit_solution(10805766734894801969)
XLA Ops:
  16.3 8.2 %collective-permute-done.rest_1_ = bf16[2,2,8,32,256]{4,3,2,1,0:T(8,128)(2,1)S(1)} collective-permute-done((bf16[2,2,8,32,256]{4,3,2,1,0:T(8,128)(2,1)}, bf16[2,2,8,32,256]{4,3,2,1,0:T(8,128)(2,1)S(1)}, u32[]{:S(2)}, u32[]{:S(2)}) %collective-permute-start) | collective-permute-done | bytes 524320 | tf_op jit(solution)/shard_map/ppermute | solution.py:399
  26.3 4.7 shard_map.38
  31.0 5.8 collective-permute-start.6
  36.8 31.8 %collective-permute-done.2.rest_3_ = bf16[2,2,8,32,256]{4,3,2,1,0:T(8,128)(2,1)S(1)} collective-permute-done((bf16[2,2,8,32,256]{4,3,2,1,0:T(8,128)(2,1)}, bf16[2,2,8,32,256]{4,3,2,1,0:T(8,128)(2,1)S(1)}, u32[]{:S(2)}, u32[]{:S(2)}) %collective-permute-start.2) | collective-permute-done | bytes 524320 | tf_op jit(solution)/shard_map/ppermute | solution.py:399
  69.4 22.1 %collective-permute-start.8 = (bf16[2,2,8,32,256]{4,3,2,1,0:T(8,128)(2,1)}, bf16[2,2,8,32,256]{4,3,2,1,0:T(8,128)(2,1)S(1)}, u32[]{:S(2)}, u32[]{:S(2)}) collective-permute-start(bf16[2,2,8,32,256]{4,3,2,1,0:T(8,128)(2,1)} %get-tuple-element.97), channel_id=1, source_target_pairs={{0,8},{4,12},{8,16},{12,20},{16,24},{20,28},{24,0},{28,4},{1,9},{5... | collective-permute-start | bytes 1572872 | tf_op jit(solution)/shard_map/ppermute | solution.py:399
  91.5 11.5 %collective-permute-start.9 = (bf16[2,2,8,32,256]{4,3,2,1,0:T(8,128)(2,1)}, bf16[2,2,8,32,256]{4,3,2,1,0:T(8,128)(2,1)S(1)}, u32[]{:S(2)}, u32[]{:S(2)}) collective-permute-start(bf16[2,2,8,32,256]{4,3,2,1,0:T(8,128)(2,1)} %get-tuple-element.98), channel_id=1, source_target_pairs={{0,12},{4,16},{8,20},{12,24},{16,28},{20,0},{24,4},{28,8},{1,13},{... | collective-permute-start | bytes 1572872 | tf_op jit(solution)/shard_map/ppermute | solution.py:399
  107.1 29.4 %collective-permute-start.11 = (bf16[2,2,8,32,256]{4,3,2,1,0:T(8,128)(2,1)}, bf16[2,2,8,32,256]{4,3,2,1,0:T(8,128)(2,1)S(1)}, u32[]{:S(2)}, u32[]{:S(2)}) collective-permute-start(bf16[2,2,8,32,256]{4,3,2,1,0:T(8,128)(2,1)} %get-tuple-element.100), channel_id=1, source_target_pairs={{0,20},{4,24},{8,28},{12,0},{16,4},{20,8},{24,12},{28,16},{1,21},{... | collective-permute-start | bytes 1572872 | tf_op jit(solution)/shard_map/ppermute | solution.py:399
  140.2 8.3 %polar.5 = (bf16[2,8,32,256]{3,2,1,0:T(8,128)(2,1)}, bf16[2,8,32,256]{3,2,1,0:T(8,128)(2,1)}, bf16[2,8,32,256]{3,2,1,0:T(8,128)(2,1)}, bf16[2,8,32,256]{3,2,1,0:...) custom-call(s32[1]{0:T(128)} %bitcast.token_ref.me_ref, ...), custom_call_target="tpu_custom_call" | custom-call | tf_op jit(solution)/shard_map/polar/pallas_call | solution.py:214
  148.5 10.1 %collective-permute-done.9.rest_3_ = bf16[2,2,8,32,256]{4,3,2,1,0:T(8,128)(2,1)S(1)} collective-permute-done((bf16[2,2,8,32,256]{4,3,2,1,0:T(8,128)(2,1)}, bf16[2,2,8,32,256]{4,3,2,1,0:T(8,128)(2,1)S(1)}, u32[]{:S(2)}, u32[]{:S(2)}) %collective-permute-start.9) | collective-permute-done | bytes 524320 | tf_op jit(solution)/shard_map/ppermute | solution.py:399
  158.9 22.6 %collective-permute-start.15 = (bf16[2,8,32,256]{3,2,1,0:T(8,128)(2,1)}, bf16[2,8,32,256]{3,2,1,0:T(8,128)(2,1)S(1)}, u32[]{:S(2)}, u32[]{:S(2)}) collective-permute-start(bf16[2,8,32,256]{3,2,1,0:T(8,128)(2,1)} %get-tuple-element.106), channel_id=1, source_target_pairs={{0,8},{4,12},{8,16},{12,20},{16,24},{20,28},{24,0},{28,4},{1,9},{5... | collective-permute-start | bytes 786440 | tf_op jit(solution)/shard_map/ppermute | solution.py:399
  181.4 10.8 %collective-permute-start.16 = (bf16[2,8,32,256]{3,2,1,0:T(8,128)(2,1)}, bf16[2,8,32,256]{3,2,1,0:T(8,128)(2,1)S(1)}, u32[]{:S(2)}, u32[]{:S(2)}) collective-permute-start(bf16[2,8,32,256]{3,2,1,0:T(8,128)(2,1)} %get-tuple-element.107), channel_id=1, source_target_pairs={{0,12},{4,16},{8,20},{12,24},{16,28},{20,0},{24,4},{28,8},{1,13},{... | collective-permute-start | bytes 786440 | tf_op jit(solution)/shard_map/ppermute | solution.py:399
  196.9 12.2 %collective-permute-start.18 = (bf16[2,8,32,256]{3,2,1,0:T(8,128)(2,1)}, bf16[2,8,32,256]{3,2,1,0:T(8,128)(2,1)S(1)}, u32[]{:S(2)}, u32[]{:S(2)}) collective-permute-start(bf16[2,8,32,256]{3,2,1,0:T(8,128)(2,1)} %get-tuple-element.109), channel_id=1, source_target_pairs={{0,20},{4,24},{8,28},{12,0},{16,4},{20,8},{24,12},{28,16},{1,21},{... | collective-permute-start | bytes 786440 | tf_op jit(solution)/shard_map/ppermute | solution.py:399
  209.1 4.8 collective-permute-start.19
  213.9 4.7 shard_map.39
  218.7 8.2 %polar.6 = (bf16[2,8,32,256]{3,2,1,0:T(8,128)(2,1)}, bf16[2,8,32,256]{3,2,1,0:T(8,128)(2,1)}, bf16[2,8,32,256]{3,2,1,0:T(8,128)(2,1)}, bf16[2,8,32,256]{3,2,1,0:...) custom-call(s32[1]{0:T(128)} %bitcast.token_ref.me_ref, ...), custom_call_target="tpu_custom_call" | custom-call | tf_op jit(solution)/shard_map/polar/pallas_call | solution.py:214
  238.3 6.2 collective-permute-start.29
  244.6 7.4 collective-permute-done.28.rest_1_
  256.9 54.7 %collective-permute-done.30.rest_3_ = bf16[2,8,32,256]{3,2,1,0:T(8,128)(2,1)S(1)} collective-permute-done((bf16[2,8,32,256]{3,2,1,0:T(8,128)(2,1)}, bf16[2,8,32,256]{3,2,1,0:T(8,128)(2,1)S(1)}, u32[]{:S(2)}, u32[]{:S(2)}) %collective-permute-start.30) | collective-permute-done | bytes 262176 | tf_op jit(solution)/shard_map/ppermute | solution.py:399
  319.4 29.7 %collective-permute-done.24.rest_4_ = bf16[2,2,8,32,256]{4,3,2,1,0:T(8,128)(2,1)S(1)} collective-permute-done((bf16[2,2,8,32,256]{4,3,2,1,0:T(8,128)(2,1)}, bf16[2,2,8,32,256]{4,3,2,1,0:T(8,128)(2,1)S(1)}, u32[]{:S(2)}, u32[]{:S(2)}) %collective-permute-start.24) | collective-permute-done | bytes 524320 | tf_op jit(solution)/shard_map/ppermute | solution.py:399
  349.2 35.6 %collective-permute-start.33 = (bf16[2,8,32,256]{3,2,1,0:T(8,128)(2,1)}, bf16[2,8,32,256]{3,2,1,0:T(8,128)(2,1)}, u32[]{:S(2)}, u32[]{:S(2)}) collective-permute-start(bf16[2,8,32,256]{3,2,1,0:T(8,128)(2,1)} %get-tuple-element.125), channel_id=1, source_target_pairs={{0,24},{4,28},{8,0},{12,4},{16,8},{20,12},{24,16},{28,20},{1,25},{... | collective-permute-start | bytes 786440 | tf_op jit(solution)/shard_map/ppermute | solution.py:399
  384.8 17.8 %collective-permute-start.34 = (bf16[2,8,32,256]{3,2,1,0:T(8,128)(2,1)}, bf16[2,8,32,256]{3,2,1,0:T(8,128)(2,1)}, u32[]{:S(2)}, u32[]{:S(2)}) collective-permute-start(bf16[2,8,32,256]{3,2,1,0:T(8,128)(2,1)} %get-tuple-element.126), channel_id=1, source_target_pairs={{0,28},{4,0},{8,4},{12,8},{16,12},{20,16},{24,20},{28,24},{1,29},{... | collective-permute-start | bytes 786440 | tf_op jit(solution)/shard_map/ppermute | solution.py:399
  402.7 8.2 %polar.7 = (bf16[2,8,32,256]{3,2,1,0:T(8,128)(2,1)}, bf16[2,8,32,256]{3,2,1,0:T(8,128)(2,1)}, bf16[2,8,32,256]{3,2,1,0:T(8,128)(2,1)}, bf16[2,8,32,256]{3,2,1,0:...) custom-call(s32[1]{0:T(128)} %bitcast.token_ref.me_ref, ...), custom_call_target="tpu_custom_call" | custom-call | tf_op jit(solution)/shard_map/polar/pallas_call | solution.py:214
  415.0 7.0 collective-permute-start.38
  422.5 8.0 %collective-permute-done.38.rest_1_ = bf16[2,8,32,256]{3,2,1,0:T(8,128)(2,1)S(1)} collective-permute-done((bf16[2,8,32,256]{3,2,1,0:T(8,128)(2,1)S(1)}, bf16[2,8,32,256]{3,2,1,0:T(8,128)(2,1)S(1)}, u32[]{:S(2)}, u32[]{:S(2)}) %collective-permute-start.38) | collective-permute-done | bytes 262176 | tf_op jit(solution)/shard_map/ppermute | solution.py:399
  432.2 20.2 %collective-permute-done.40.rest_3_ = bf16[2,8,32,256]{3,2,1,0:T(8,128)(2,1)S(1)} collective-permute-done((bf16[2,8,32,256]{3,2,1,0:T(8,128)(2,1)}, bf16[2,8,32,256]{3,2,1,0:T(8,128)(2,1)S(1)}, u32[]{:S(2)}, u32[]{:S(2)}) %collective-permute-start.40) | collective-permute-done | bytes 262176 | tf_op jit(solution)/shard_map/ppermute | solution.py:399
  452.4 9.3 %collective-permute-done.52.rest_1_ = bf16[8,2,8,32,256]{4,3,2,1,0:T(8,128)(2,1)} collective-permute-done((bf16[8,2,8,32,256]{4,3,2,1,0:T(8,128)(2,1)}, bf16[8,2,8,32,256]{4,3,2,1,0:T(8,128)(2,1)}, u32[]{:S(2)}, u32[]{:S(2)}) %collective-permute-start.52) | collective-permute-done | bytes 2097184 | tf_op jit(solution)/shard_map/ppermute | solution.py:406
  472.1 10.5 %left.3.token_ref.rest_0_.rest_1_ = bf16[2,8,256,256]{3,2,1,0:T(8,128)(2,1)} custom-call(s32[6]{0:T(128)} %stack.27.index_ref, bf16[2,8,1024,1024]{3,2,1,0:T(8,128)(2,1)} %coulomb_ref.3, bf16[8,2,8,32,256]{4,3,2,1,0:T(8,128)(2,1)} %join.7.token_ref.rest_0_, bf16[8,2,8,32,256]{4,3,2,1,0:T(8,128)(2,1)} %join.6.token_ref.rest_0_, ...), custom_call_target="tpu_custom_call" | custom-call | tf_op jit(solution)/shard_map/left/pallas_call | solution.py:285
  490.5 5.1 collective-permute-start.45
  500.0 5.4 collective-permute-done.45.rest_1_
  508.2 18.9 %collective-permute-done.47.rest_3_ = bf16[2,2,8,32,128]{4,3,2,1,0:T(8,128)(2,1)S(1)} collective-permute-done((bf16[2,2,8,32,128]{4,3,2,1,0:T(8,128)(2,1)S(1)}, bf16[2,2,8,32,128]{4,3,2,1,0:T(8,128)(2,1)S(1)}, u32[]{:S(2)}, u32[]{:S(2)}) %collective-permute-start.47) | collective-permute-done | bytes 262176 | tf_op jit(solution)/shard_map/ppermute | solution.py:399
  531.5 6.8 collective-permute-done.49.rest_5_
  541.9 6.2 collective-permute-done.51.rest_7_
  548.1 5.1 polar.8
  555.9 6.7 collective-permute-done.62.rest_1_
  564.0 24.1 %collective-permute-done.64.rest_3_ = bf16[2,8,32,128]{3,2,1,0:T(8,128)(2,1)S(1)} collective-permute-done((bf16[2,8,32,128]{3,2,1,0:T(8,128)(2,1)}, bf16[2,8,32,128]{3,2,1,0:T(8,128)(2,1)S(1)}, u32[]{:S(2)}, u32[]{:S(2)}) %collective-permute-start.64) | collective-permute-done | bytes 131104 | tf_op jit(solution)/shard_map/ppermute | solution.py:399
  588.4 10.9 %collective-permute-done.56.rest_2_ = bf16[2,2,8,32,128]{4,3,2,1,0:T(8,128)(2,1)S(1)} collective-permute-done((bf16[2,2,8,32,128]{4,3,2,1,0:T(8,128)(2,1)}, bf16[2,2,8,32,128]{4,3,2,1,0:T(8,128)(2,1)S(1)}, u32[]{:S(2)}, u32[]{:S(2)}) %collective-permute-start.56) | collective-permute-done | bytes 262176 | tf_op jit(solution)/shard_map/ppermute | solution.py:399
  599.3 20.3 %collective-permute-start.59 = (bf16[2,2,8,32,128]{4,3,2,1,0:T(8,128)(2,1)}, bf16[2,2,8,32,128]{4,3,2,1,0:T(8,128)(2,1)S(1)}, u32[]{:S(2)}, u32[]{:S(2)}) collective-permute-start(bf16[2,2,8,32,128]{4,3,2,1,0:T(8,128)(2,1)} %get-tuple-element.147), channel_id=1, source_target_pairs={{0,20},{4,24},{8,28},{12,0},{16,4},{20,8},{24,12},{28,16},{1,21},{... | collective-permute-start | bytes 786440 | tf_op jit(solution)/shard_map/ppermute | solution.py:399
  619.6 6.5 collective-permute-start.60
  637.8 5.2 collective-permute-start.68
  643.0 10.4 %left.4.token_ref.rest_1_.rest_2_ = bf16[2,8,256,256]{3,2,1,0:T(8,128)(2,1)} custom-call(s32[6]{0:T(128)} %stack.27.index_ref, bf16[2,8,1024,1024]{3,2,1,0:T(8,128)(2,1)} %coulomb_ref.3, bf16[2,8,32,128]{3,2,1,0:T(8,128)(2,1)} %get-tuple-element.142.token_ref.rest_0_, bf16[8,2,8,32,256]{4,3,2,1,0:T(8,128)(2,1)} %join.7.token_ref.rest_0_, ...), custom_call_target="tpu_custom_call" | custom-call | tf_op jit(solution)/shard_map/left/pallas_call | solution.py:285
  653.5 5.1 polar.9
  661.9 5.0 collective-permute-done.69.rest_1_
  673.5 4.8 collective-permute-done.72.rest_4_
  695.1 6.8 collective-permute-done.82.rest_8_
  702.4 13.1 %collective-permute-done.85.rest_9_ = bf16[8,2,5,32,128]{4,3,2,1,0:T(8,128)(2,1)} collective-permute-done((bf16[8,2,5,32,128]{4,3,2,1,0:T(8,128)(2,1)}, bf16[8,2,5,32,128]{4,3,2,1,0:T(8,128)(2,1)}, u32[]{:S(2)}, u32[]{:S(2)}) %collective-permute-start.85) | collective-permute-done | bytes 655392 | tf_op jit(solution)/shard_map/ppermute | solution.py:406
  716.0 10.5 %left.5.rest_2_.rest_3_ = bf16[2,8,256,256]{3,2,1,0:T(8,128)(2,1)} custom-call(s32[6]{0:T(128)} %stack.27.index_ref, bf16[2,8,1024,1024]{3,2,1,0:T(8,128)(2,1)} %coulomb_ref.3, bf16[8,2,5,32,128]{4,3,2,1,0:T(8,128)(2,1)} %join.11.token_ref.rest_8_, bf16[8,2,8,32,256]{4,3,2,1,0:T(8,128)(2,1)} %join.8.token_ref.rest_0_, ...), custom_call_target="tpu_custom_call" | custom-call | tf_op jit(solution)/shard_map/left/pallas_call | solution.py:285
  727.3 14.3 %shard_map.42.rest_0_ = f32[2,8,256,1024]{3,2,1,0:T(8,128)} custom-call(s32[6]{0:T(128)} %stack.27.index_ref, bf16[2,8,1024,1024]{3,2,1,0:T(8,128)(2,1)} %coulomb_ref.3, bf16[2,8,256,256]{3,2,1,0:T(8,128)(2,1)} %left.3.token_ref.rest_0_.rest_1_, bf16[2,8,256,256]{3,2,1,0:T(8,128)(2,1)} %left.4.token_ref.rest_1_.rest_2_, ...), custom_call_target="tpu_custom_call" | custom-call | tf_op jit(solution)/shard_map/pallas_call | solution.py:340
  742.5 20.9 %shard_map.43 = f32[2,8,256,1024]{3,2,1,0:T(8,128)} custom-call(s32[6]{0:T(128)} %stack.27.index_ref, bf16[2,8,1024,1024]{3,2,1,0:T(8,128)(2,1)} %coulomb_ref.3, f32[2,8,256,1024]{3,2,1,0:T(8,128)} %shard_map.42.rest_0_, bf16[2,8,256,256]{3,2,1,0:T(8,128)(2,1)} %left.3.token_ref.rest_0_.rest_1_, ...), custom_call_target="tpu_custom_call", output_to_operand_aliasing={{}: (2, {})} | custom-call | tf_op jit(solution)/shard_map/pallas_call | solution.py:340
  (298 shorter events, 140.8 us)
Async XLA Ops:
  9.9 58.7 %collective-permute-start.2 = (bf16[2,2,8,32,256]{4,3,2,1,0:T(8,128)(2,1)}, bf16[2,2,8,32,256]{4,3,2,1,0:T(8,128)(2,1)S(1)}, u32[]{:S(2)}, u32[]{:S(2)}) collective-permute-start(bf16[2,2,8,32,256]{4,3,2,1,0:T(8,128)(2,1)} %get-tuple-element.89), channel_id=1, source_target_pairs={{0,12},{4,16},{8,20},{12,24},{16,28},{20,0},{24,4},{28,8},{1,13},{... | collective-permute-start | bytes 1572872 | tf_op jit(solution)/shard_map/ppermute | solution.py:399
  12.4 56.4 %collective-permute-start.3 = (bf16[2,2,8,32,256]{4,3,2,1,0:T(8,128)(2,1)}, bf16[2,2,8,32,256]{4,3,2,1,0:T(8,128)(2,1)S(1)}, u32[]{:S(2)}, u32[]{:S(2)}) collective-permute-start(bf16[2,2,8,32,256]{4,3,2,1,0:T(8,128)(2,1)} %get-tuple-element.90), channel_id=1, source_target_pairs={{0,16},{4,20},{8,24},{12,28},{16,0},{20,4},{24,8},{28,12},{1,17},{... | collective-permute-start | bytes 1572872 | tf_op jit(solution)/shard_map/ppermute | solution.py:399
  13.7 77.9 %collective-permute-start.4 = (bf16[2,2,8,32,256]{4,3,2,1,0:T(8,128)(2,1)}, bf16[2,2,8,32,256]{4,3,2,1,0:T(8,128)(2,1)S(1)}, u32[]{:S(2)}, u32[]{:S(2)}) collective-permute-start(bf16[2,2,8,32,256]{4,3,2,1,0:T(8,128)(2,1)} %get-tuple-element.91), channel_id=1, source_target_pairs={{0,20},{4,24},{8,28},{12,0},{16,4},{20,8},{24,12},{28,16},{1,21},{... | collective-permute-start | bytes 1572872 | tf_op jit(solution)/shard_map/ppermute | solution.py:399
  24.5 78.5 %collective-permute-start.5 = (bf16[2,2,8,32,256]{4,3,2,1,0:T(8,128)(2,1)}, bf16[2,2,8,32,256]{4,3,2,1,0:T(8,128)(2,1)S(1)}, u32[]{:S(2)}, u32[]{:S(2)}) collective-permute-start(bf16[2,2,8,32,256]{4,3,2,1,0:T(8,128)(2,1)} %get-tuple-element.92), channel_id=1, source_target_pairs={{0,24},{4,28},{8,0},{12,4},{16,8},{20,12},{24,16},{28,20},{1,25},{... | collective-permute-start | bytes 1572872 | tf_op jit(solution)/shard_map/ppermute | solution.py:399
  31.0 76.0 %collective-permute-start.6 = (bf16[2,2,8,32,256]{4,3,2,1,0:T(8,128)(2,1)}, bf16[2,2,8,32,256]{4,3,2,1,0:T(8,128)(2,1)S(1)}, u32[]{:S(2)}, u32[]{:S(2)}) collective-permute-start(bf16[2,2,8,32,256]{4,3,2,1,0:T(8,128)(2,1)} %get-tuple-element.93), channel_id=1, source_target_pairs={{0,28},{4,0},{8,4},{12,8},{16,12},{20,16},{24,20},{28,24},{1,29},{... | collective-permute-start | bytes 1572872 | tf_op jit(solution)/shard_map/ppermute | solution.py:399
  68.6 67.9 %collective-permute-start.7 = (bf16[2,2,8,32,256]{4,3,2,1,0:T(8,128)(2,1)}, bf16[2,2,8,32,256]{4,3,2,1,0:T(8,128)(2,1)S(1)}, u32[]{:S(2)}, u32[]{:S(2)}) collective-permute-start(bf16[2,2,8,32,256]{4,3,2,1,0:T(8,128)(2,1)} %get-tuple-element.96), channel_id=1, source_target_pairs={{0,4},{4,8},{8,12},{12,16},{16,20},{20,24},{24,28},{28,0},{1,5},{5... | collective-permute-start | bytes 1572872 | tf_op jit(solution)/shard_map/ppermute | solution.py:399
  69.4 70.8 %collective-permute-start.8 = (bf16[2,2,8,32,256]{4,3,2,1,0:T(8,128)(2,1)}, bf16[2,2,8,32,256]{4,3,2,1,0:T(8,128)(2,1)S(1)}, u32[]{:S(2)}, u32[]{:S(2)}) collective-permute-start(bf16[2,2,8,32,256]{4,3,2,1,0:T(8,128)(2,1)} %get-tuple-element.97), channel_id=1, source_target_pairs={{0,8},{4,12},{8,16},{12,20},{16,24},{20,28},{24,0},{28,4},{1,9},{5... | collective-permute-start | bytes 1572872 | tf_op jit(solution)/shard_map/ppermute | solution.py:399
  91.5 67.1 %collective-permute-start.9 = (bf16[2,2,8,32,256]{4,3,2,1,0:T(8,128)(2,1)}, bf16[2,2,8,32,256]{4,3,2,1,0:T(8,128)(2,1)S(1)}, u32[]{:S(2)}, u32[]{:S(2)}) collective-permute-start(bf16[2,2,8,32,256]{4,3,2,1,0:T(8,128)(2,1)} %get-tuple-element.98), channel_id=1, source_target_pairs={{0,12},{4,16},{8,20},{12,24},{16,28},{20,0},{24,4},{28,8},{1,13},{... | collective-permute-start | bytes 1572872 | tf_op jit(solution)/shard_map/ppermute | solution.py:399
  103.0 55.9 %collective-permute-start.10 = (bf16[2,2,8,32,256]{4,3,2,1,0:T(8,128)(2,1)}, bf16[2,2,8,32,256]{4,3,2,1,0:T(8,128)(2,1)S(1)}, u32[]{:S(2)}, u32[]{:S(2)}) collective-permute-start(bf16[2,2,8,32,256]{4,3,2,1,0:T(8,128)(2,1)} %get-tuple-element.99), channel_id=1, source_target_pairs={{0,16},{4,20},{8,24},{12,28},{16,0},{20,4},{24,8},{28,12},{1,17},{... | collective-permute-start | bytes 1572872 | tf_op jit(solution)/shard_map/ppermute | solution.py:399
  107.1 74.4 %collective-permute-start.11 = (bf16[2,2,8,32,256]{4,3,2,1,0:T(8,128)(2,1)}, bf16[2,2,8,32,256]{4,3,2,1,0:T(8,128)(2,1)S(1)}, u32[]{:S(2)}, u32[]{:S(2)}) collective-permute-start(bf16[2,2,8,32,256]{4,3,2,1,0:T(8,128)(2,1)} %get-tuple-element.100), channel_id=1, source_target_pairs={{0,20},{4,24},{8,28},{12,0},{16,4},{20,8},{24,12},{28,16},{1,21},{... | collective-permute-start | bytes 1572872 | tf_op jit(solution)/shard_map/ppermute | solution.py:399
  136.5 55.7 %collective-permute-start.12 = (bf16[2,2,8,32,256]{4,3,2,1,0:T(8,128)(2,1)}, bf16[2,2,8,32,256]{4,3,2,1,0:T(8,128)(2,1)S(1)}, u32[]{:S(2)}, u32[]{:S(2)}) collective-permute-start(bf16[2,2,8,32,256]{4,3,2,1,0:T(8,128)(2,1)} %get-tuple-element.101), channel_id=1, source_target_pairs={{0,24},{4,28},{8,0},{12,4},{16,8},{20,12},{24,16},{28,20},{1,25},{... | collective-permute-start | bytes 1572872 | tf_op jit(solution)/shard_map/ppermute | solution.py:399
  140.2 56.8 %collective-permute-start.13 = (bf16[2,2,8,32,256]{4,3,2,1,0:T(8,128)(2,1)}, bf16[2,2,8,32,256]{4,3,2,1,0:T(8,128)(2,1)}, u32[]{:S(2)}, u32[]{:S(2)}) collective-permute-start(bf16[2,2,8,32,256]{4,3,2,1,0:T(8,128)(2,1)} %get-tuple-element.102), channel_id=1, source_target_pairs={{0,28},{4,0},{8,4},{12,8},{16,12},{20,16},{24,20},{28,24},{1,29},{... | collective-permute-start | bytes 1572872 | tf_op jit(solution)/shard_map/ppermute | solution.py:399
  158.6 50.5 %collective-permute-start.14 = (bf16[2,8,32,256]{3,2,1,0:T(8,128)(2,1)}, bf16[2,8,32,256]{3,2,1,0:T(8,128)(2,1)S(1)}, u32[]{:S(2)}, u32[]{:S(2)}) collective-permute-start(bf16[2,8,32,256]{3,2,1,0:T(8,128)(2,1)} %get-tuple-element.105), channel_id=1, source_target_pairs={{0,4},{4,8},{8,12},{12,16},{16,20},{20,24},{24,28},{28,0},{1,5},{5... | collective-permute-start | bytes 786440 | tf_op jit(solution)/shard_map/ppermute | solution.py:399
  158.9 55.0 %collective-permute-start.15 = (bf16[2,8,32,256]{3,2,1,0:T(8,128)(2,1)}, bf16[2,8,32,256]{3,2,1,0:T(8,128)(2,1)S(1)}, u32[]{:S(2)}, u32[]{:S(2)}) collective-permute-start(bf16[2,8,32,256]{3,2,1,0:T(8,128)(2,1)} %get-tuple-element.106), channel_id=1, source_target_pairs={{0,8},{4,12},{8,16},{12,20},{16,24},{20,28},{24,0},{28,4},{1,9},{5... | collective-permute-start | bytes 786440 | tf_op jit(solution)/shard_map/ppermute | solution.py:399
  181.4 49.1 %collective-permute-start.16 = (bf16[2,8,32,256]{3,2,1,0:T(8,128)(2,1)}, bf16[2,8,32,256]{3,2,1,0:T(8,128)(2,1)S(1)}, u32[]{:S(2)}, u32[]{:S(2)}) collective-permute-start(bf16[2,8,32,256]{3,2,1,0:T(8,128)(2,1)} %get-tuple-element.107), channel_id=1, source_target_pairs={{0,12},{4,16},{8,20},{12,24},{16,28},{20,0},{24,4},{28,8},{1,13},{... | collective-permute-start | bytes 786440 | tf_op jit(solution)/shard_map/ppermute | solution.py:399
  192.2 38.4 %collective-permute-start.17 = (bf16[2,8,32,256]{3,2,1,0:T(8,128)(2,1)}, bf16[2,8,32,256]{3,2,1,0:T(8,128)(2,1)S(1)}, u32[]{:S(2)}, u32[]{:S(2)}) collective-permute-start(bf16[2,8,32,256]{3,2,1,0:T(8,128)(2,1)} %get-tuple-element.108), channel_id=1, source_target_pairs={{0,16},{4,20},{8,24},{12,28},{16,0},{20,4},{24,8},{28,12},{1,17},{... | collective-permute-start | bytes 786440 | tf_op jit(solution)/shard_map/ppermute | solution.py:399
  196.9 33.7 %collective-permute-start.18 = (bf16[2,8,32,256]{3,2,1,0:T(8,128)(2,1)}, bf16[2,8,32,256]{3,2,1,0:T(8,128)(2,1)S(1)}, u32[]{:S(2)}, u32[]{:S(2)}) collective-permute-start(bf16[2,8,32,256]{3,2,1,0:T(8,128)(2,1)} %get-tuple-element.109), channel_id=1, source_target_pairs={{0,20},{4,24},{8,28},{12,0},{16,4},{20,8},{24,12},{28,16},{1,21},{... | collective-permute-start | bytes 786440 | tf_op jit(solution)/shard_map/ppermute | solution.py:399
  234.3 180.2 %collective-permute-start.35 = (bf16[8,2,8,32,256]{4,3,2,1,0:T(8,128)(2,1)}, bf16[8,2,8,32,256]{4,3,2,1,0:T(8,128)(2,1)}, u32[]{:S(2)}, u32[]{:S(2)}) collective-permute-start(bf16[8,2,8,32,256]{4,3,2,1,0:T(8,128)(2,1)} %join.6.token_ref.rest_0_), channel_id=1, source_target_pairs={{0,2},{1,3},{2,0},{3,1},{4,6},{5,7},{6,4},{7,5},{8,10},{9,11},{10,... | collective-permute-start | bytes 6291464 | tf_op jit(solution)/shard_map/ppermute | solution.py:406
  244.5 67.8 %collective-permute-start.21 = (bf16[2,2,8,32,256]{4,3,2,1,0:T(8,128)(2,1)S(1)}, bf16[2,2,8,32,256]{4,3,2,1,0:T(8,128)(2,1)S(1)}, u32[]{:S(2)}, u32[]{:S(2)}) collective-permute-start(bf16[2,2,8,32,256]{4,3,2,1,0:T(8,128)(2,1)S(1)} %copy-done.62), channel_id=1, source_target_pairs={{0,4},{4,8},{8,12},{12,16},{16,20},{20,24},{24,28},{28,0},{1,5},{5... | collective-permute-start | bytes 1572872 | tf_op jit(solution)/shard_map/ppermute | solution.py:399
  244.6 67.8 %collective-permute-start.22 = (bf16[2,2,8,32,256]{4,3,2,1,0:T(8,128)(2,1)S(1)}, bf16[2,2,8,32,256]{4,3,2,1,0:T(8,128)(2,1)S(1)}, u32[]{:S(2)}, u32[]{:S(2)}) collective-permute-start(bf16[2,2,8,32,256]{4,3,2,1,0:T(8,128)(2,1)S(1)} %copy-done.61), channel_id=1, source_target_pairs={{0,8},{4,12},{8,16},{12,20},{16,24},{20,28},{24,0},{28,4},{1,9},{5... | collective-permute-start | bytes 1572872 | tf_op jit(solution)/shard_map/ppermute | solution.py:399
  252.0 63.1 %collective-permute-start.23 = (bf16[2,2,8,32,256]{4,3,2,1,0:T(8,128)(2,1)}, bf16[2,2,8,32,256]{4,3,2,1,0:T(8,128)(2,1)S(1)}, u32[]{:S(2)}, u32[]{:S(2)}) collective-permute-start(bf16[2,2,8,32,256]{4,3,2,1,0:T(8,128)(2,1)} %get-tuple-element.114), channel_id=1, source_target_pairs={{0,12},{4,16},{8,20},{12,24},{16,28},{20,0},{24,4},{28,8},{1,13},{... | collective-permute-start | bytes 1572872 | tf_op jit(solution)/shard_map/ppermute | solution.py:399
  253.1 58.4 %collective-permute-start.30 = (bf16[2,8,32,256]{3,2,1,0:T(8,128)(2,1)}, bf16[2,8,32,256]{3,2,1,0:T(8,128)(2,1)S(1)}, u32[]{:S(2)}, u32[]{:S(2)}) collective-permute-start(bf16[2,8,32,256]{3,2,1,0:T(8,128)(2,1)} %get-tuple-element.122), channel_id=1, source_target_pairs={{0,12},{4,16},{8,20},{12,24},{16,28},{20,0},{24,4},{28,8},{1,13},{... | collective-permute-start | bytes 786440 | tf_op jit(solution)/shard_map/ppermute | solution.py:399
  312.3 36.8 %collective-permute-start.24 = (bf16[2,2,8,32,256]{4,3,2,1,0:T(8,128)(2,1)}, bf16[2,2,8,32,256]{4,3,2,1,0:T(8,128)(2,1)S(1)}, u32[]{:S(2)}, u32[]{:S(2)}) collective-permute-start(bf16[2,2,8,32,256]{4,3,2,1,0:T(8,128)(2,1)} %get-tuple-element.115), channel_id=1, source_target_pairs={{0,16},{4,20},{8,24},{12,28},{16,0},{20,4},{24,8},{28,12},{1,17},{... | collective-permute-start | bytes 1572872 | tf_op jit(solution)/shard_map/ppermute | solution.py:399
  312.3 36.8 %collective-permute-start.25 = (bf16[2,2,8,32,256]{4,3,2,1,0:T(8,128)(2,1)}, bf16[2,2,8,32,256]{4,3,2,1,0:T(8,128)(2,1)S(1)}, u32[]{:S(2)}, u32[]{:S(2)}) collective-permute-start(bf16[2,2,8,32,256]{4,3,2,1,0:T(8,128)(2,1)} %get-tuple-element.116), channel_id=1, source_target_pairs={{0,20},{4,24},{8,28},{12,0},{16,4},{20,8},{24,12},{28,16},{1,21},{... | collective-permute-start | bytes 1572872 | tf_op jit(solution)/shard_map/ppermute | solution.py:399
  312.4 36.8 %collective-permute-start.26 = (bf16[2,2,8,32,256]{4,3,2,1,0:T(8,128)(2,1)}, bf16[2,2,8,32,256]{4,3,2,1,0:T(8,128)(2,1)S(1)}, u32[]{:S(2)}, u32[]{:S(2)}) collective-permute-start(bf16[2,2,8,32,256]{4,3,2,1,0:T(8,128)(2,1)} %get-tuple-element.117), channel_id=1, source_target_pairs={{0,24},{4,28},{8,0},{12,4},{16,8},{20,12},{24,16},{28,20},{1,25},{... | collective-permute-start | bytes 1572872 | tf_op jit(solution)/shard_map/ppermute | solution.py:399
  315.1 69.7 %collective-permute-start.27 = (bf16[2,2,8,32,256]{4,3,2,1,0:T(8,128)(2,1)}, bf16[2,2,8,32,256]{4,3,2,1,0:T(8,128)(2,1)}, u32[]{:S(2)}, u32[]{:S(2)}) collective-permute-start(bf16[2,2,8,32,256]{4,3,2,1,0:T(8,128)(2,1)} %get-tuple-element.118), channel_id=1, source_target_pairs={{0,28},{4,0},{8,4},{12,8},{16,12},{20,16},{24,20},{28,24},{1,29},{... | collective-permute-start | bytes 1572872 | tf_op jit(solution)/shard_map/ppermute | solution.py:399
  349.1 61.8 %collective-permute-start.31 = (bf16[2,8,32,256]{3,2,1,0:T(8,128)(2,1)}, bf16[2,8,32,256]{3,2,1,0:T(8,128)(2,1)}, u32[]{:S(2)}, u32[]{:S(2)}) collective-permute-start(bf16[2,8,32,256]{3,2,1,0:T(8,128)(2,1)} %get-tuple-element.123), channel_id=1, source_target_pairs={{0,16},{4,20},{8,24},{12,28},{16,0},{20,4},{24,8},{28,12},{1,17},{... | collective-permute-start | bytes 786440 | tf_op jit(solution)/shard_map/ppermute | solution.py:399
  349.1 61.8 %collective-permute-start.32 = (bf16[2,8,32,256]{3,2,1,0:T(8,128)(2,1)}, bf16[2,8,32,256]{3,2,1,0:T(8,128)(2,1)}, u32[]{:S(2)}, u32[]{:S(2)}) collective-permute-start(bf16[2,8,32,256]{3,2,1,0:T(8,128)(2,1)} %get-tuple-element.124), channel_id=1, source_target_pairs={{0,20},{4,24},{8,28},{12,0},{16,4},{20,8},{24,12},{28,16},{1,21},{... | collective-permute-start | bytes 786440 | tf_op jit(solution)/shard_map/ppermute | solution.py:399
  349.2 61.7 %collective-permute-start.33 = (bf16[2,8,32,256]{3,2,1,0:T(8,128)(2,1)}, bf16[2,8,32,256]{3,2,1,0:T(8,128)(2,1)}, u32[]{:S(2)}, u32[]{:S(2)}) collective-permute-start(bf16[2,8,32,256]{3,2,1,0:T(8,128)(2,1)} %get-tuple-element.125), channel_id=1, source_target_pairs={{0,24},{4,28},{8,0},{12,4},{16,8},{20,12},{24,16},{28,20},{1,25},{... | collective-permute-start | bytes 786440 | tf_op jit(solution)/shard_map/ppermute | solution.py:399
  384.8 26.1 %collective-permute-start.34 = (bf16[2,8,32,256]{3,2,1,0:T(8,128)(2,1)}, bf16[2,8,32,256]{3,2,1,0:T(8,128)(2,1)}, u32[]{:S(2)}, u32[]{:S(2)}) collective-permute-start(bf16[2,8,32,256]{3,2,1,0:T(8,128)(2,1)} %get-tuple-element.126), channel_id=1, source_target_pairs={{0,28},{4,0},{8,4},{12,8},{16,12},{20,16},{24,20},{28,24},{1,29},{... | collective-permute-start | bytes 786440 | tf_op jit(solution)/shard_map/ppermute | solution.py:399
  413.9 47.8 %collective-permute-start.52 = (bf16[8,2,8,32,256]{4,3,2,1,0:T(8,128)(2,1)}, bf16[8,2,8,32,256]{4,3,2,1,0:T(8,128)(2,1)}, u32[]{:S(2)}, u32[]{:S(2)}) collective-permute-start(bf16[8,2,8,32,256]{4,3,2,1,0:T(8,128)(2,1)} %join.7.token_ref.rest_0_), channel_id=1, source_target_pairs={{0,2},{1,3},{2,0},{3,1},{4,6},{5,7},{6,4},{7,5},{8,10},{9,11},{10,... | collective-permute-start | bytes 6291464 | tf_op jit(solution)/shard_map/ppermute | solution.py:406
  414.4 51.1 %collective-permute-start.36 = (bf16[8,2,8,32,256]{4,3,2,1,0:T(8,128)(2,1)S(1)}, bf16[8,2,8,32,256]{4,3,2,1,0:T(8,128)(2,1)S(1)}, u32[]{:S(2)}, u32[]{:S(2)}) collective-permute-start(bf16[8,2,8,32,256]{4,3,2,1,0:T(8,128)(2,1)S(1)} %copy-done), channel_id=1, source_target_pairs={{0,1},{1,0},{2,3},{3,2},{4,5},{5,4},{6,7},{7,6},{8,9},{9,8},{10,11... | collective-permute-start | bytes 6291464 | tf_op jit(solution)/shard_map/ppermute | solution.py:415
  414.5 57.1 %collective-permute-start.37 = (bf16[8,2,8,32,256]{4,3,2,1,0:T(8,128)(2,1)}, bf16[8,2,8,32,256]{4,3,2,1,0:T(8,128)(2,1)}, u32[]{:S(2)}, u32[]{:S(2)}) collective-permute-start(bf16[8,2,8,32,256]{4,3,2,1,0:T(8,128)(2,1)} %collective-permute-done.35.rest_1_), channel_id=1, source_target_pairs={{0,1},{1,0},{2,3},{3,2},{4,5},{5,4},{6,7},{7,6},{8,9},{9,8},{10,11... | collective-permute-start | bytes 6291464 | tf_op jit(solution)/shard_map/ppermute | solution.py:415
  431.7 30.0 %collective-permute-start.41 = (bf16[2,8,32,256]{3,2,1,0:T(8,128)(2,1)}, bf16[2,8,32,256]{3,2,1,0:T(8,128)(2,1)S(1)}, u32[]{:S(2)}, u32[]{:S(2)}) collective-permute-start(bf16[2,8,32,256]{3,2,1,0:T(8,128)(2,1)} %get-tuple-element.131), channel_id=1, source_target_pairs={{0,16},{4,20},{8,24},{12,28},{16,0},{20,4},{24,8},{28,12},{1,17},{... | collective-permute-start | bytes 786440 | tf_op jit(solution)/shard_map/ppermute | solution.py:399
  452.4 103.5 %collective-permute-start.53 = (bf16[8,2,8,32,256]{4,3,2,1,0:T(8,128)(2,1)}, bf16[8,2,8,32,256]{4,3,2,1,0:T(8,128)(2,1)}, u32[]{:S(2)}, u32[]{:S(2)}) collective-permute-start(bf16[8,2,8,32,256]{4,3,2,1,0:T(8,128)(2,1)} %join.7.token_ref.rest_0_), channel_id=1, source_target_pairs={{0,1},{1,0},{2,3},{3,2},{4,5},{5,4},{6,7},{7,6},{8,9},{9,8},{10,11... | collective-permute-start | bytes 6291464 | tf_op jit(solution)/shard_map/ppermute | solution.py:415
  461.7 126.6 %collective-permute-start.54 = (bf16[8,2,8,32,256]{4,3,2,1,0:T(8,128)(2,1)}, bf16[8,2,8,32,256]{4,3,2,1,0:T(8,128)(2,1)}, u32[]{:S(2)}, u32[]{:S(2)}) collective-permute-start(bf16[8,2,8,32,256]{4,3,2,1,0:T(8,128)(2,1)} %collective-permute-done.52.rest_1_), channel_id=1, source_target_pairs={{0,1},{1,0},{2,3},{3,2},{4,5},{5,4},{6,7},{7,6},{8,9},{9,8},{10,11... | collective-permute-start | bytes 6291464 | tf_op jit(solution)/shard_map/ppermute | solution.py:415
  489.9 140.8 %collective-permute-start.76 = (bf16[8,2,8,32,256]{4,3,2,1,0:T(8,128)(2,1)}, bf16[8,2,8,32,256]{4,3,2,1,0:T(8,128)(2,1)}, u32[]{:S(2)}, u32[]{:S(2)}) collective-permute-start(bf16[8,2,8,32,256]{4,3,2,1,0:T(8,128)(2,1)} %join.8.token_ref.rest_0_), channel_id=1, source_target_pairs={{0,2},{1,3},{2,0},{3,1},{4,6},{5,7},{6,4},{7,5},{8,10},{9,11},{10,... | collective-permute-start | bytes 6291464 | tf_op jit(solution)/shard_map/ppermute | solution.py:406
  555.9 32.2 %collective-permute-start.64 = (bf16[2,8,32,128]{3,2,1,0:T(8,128)(2,1)}, bf16[2,8,32,128]{3,2,1,0:T(8,128)(2,1)S(1)}, u32[]{:S(2)}, u32[]{:S(2)}) collective-permute-start(bf16[2,8,32,128]{3,2,1,0:T(8,128)(2,1)} %get-tuple-element.153), channel_id=1, source_target_pairs={{0,12},{4,16},{8,20},{12,24},{16,28},{20,0},{24,4},{28,8},{1,13},{... | collective-permute-start | bytes 393224 | tf_op jit(solution)/shard_map/ppermute | solution.py:399
  588.1 31.5 %collective-permute-start.57 = (bf16[2,2,8,32,128]{4,3,2,1,0:T(8,128)(2,1)}, bf16[2,2,8,32,128]{4,3,2,1,0:T(8,128)(2,1)S(1)}, u32[]{:S(2)}, u32[]{:S(2)}) collective-permute-start(bf16[2,2,8,32,128]{4,3,2,1,0:T(8,128)(2,1)} %get-tuple-element.145), channel_id=1, source_target_pairs={{0,12},{4,16},{8,20},{12,24},{16,28},{20,0},{24,4},{28,8},{1,13},{... | collective-permute-start | bytes 786440 | tf_op jit(solution)/shard_map/ppermute | solution.py:399
  588.3 37.8 %collective-permute-start.58 = (bf16[2,2,8,32,128]{4,3,2,1,0:T(8,128)(2,1)}, bf16[2,2,8,32,128]{4,3,2,1,0:T(8,128)(2,1)S(1)}, u32[]{:S(2)}, u32[]{:S(2)}) collective-permute-start(bf16[2,2,8,32,128]{4,3,2,1,0:T(8,128)(2,1)} %get-tuple-element.146), channel_id=1, source_target_pairs={{0,16},{4,20},{8,24},{12,28},{16,0},{20,4},{24,8},{28,12},{1,17},{... | collective-permute-start | bytes 786440 | tf_op jit(solution)/shard_map/ppermute | solution.py:399
  588.4 127.1 %collective-permute-start.77 = (bf16[8,2,8,32,256]{4,3,2,1,0:T(8,128)(2,1)S(1)}, bf16[8,2,8,32,256]{4,3,2,1,0:T(8,128)(2,1)}, u32[]{:S(2)}, u32[]{:S(2)}) collective-permute-start(bf16[8,2,8,32,256]{4,3,2,1,0:T(8,128)(2,1)S(1)} %copy-done.1), channel_id=1, source_target_pairs={{0,1},{1,0},{2,3},{3,2},{4,5},{5,4},{6,7},{7,6},{8,9},{9,8},{10,11... | collective-permute-start | bytes 6291464 | tf_op jit(solution)/shard_map/ppermute | solution.py:415
  599.3 31.4 %collective-permute-start.59 = (bf16[2,2,8,32,128]{4,3,2,1,0:T(8,128)(2,1)}, bf16[2,2,8,32,128]{4,3,2,1,0:T(8,128)(2,1)S(1)}, u32[]{:S(2)}, u32[]{:S(2)}) collective-permute-start(bf16[2,2,8,32,128]{4,3,2,1,0:T(8,128)(2,1)} %get-tuple-element.147), channel_id=1, source_target_pairs={{0,20},{4,24},{8,28},{12,0},{16,4},{20,8},{24,12},{28,16},{1,21},{... | collective-permute-start | bytes 786440 | tf_op jit(solution)/shard_map/ppermute | solution.py:399
  630.7 85.3 %collective-permute-start.78 = (bf16[8,2,8,32,256]{4,3,2,1,0:T(8,128)(2,1)}, bf16[8,2,8,32,256]{4,3,2,1,0:T(8,128)(2,1)}, u32[]{:S(2)}, u32[]{:S(2)}) collective-permute-start(bf16[8,2,8,32,256]{4,3,2,1,0:T(8,128)(2,1)} %collective-permute-done.76.rest_1_), channel_id=1, source_target_pairs={{0,1},{1,0},{2,3},{3,2},{4,5},{5,4},{6,7},{7,6},{8,9},{9,8},{10,11... | collective-permute-start | bytes 6291464 | tf_op jit(solution)/shard_map/ppermute | solution.py:415
  630.7 27.8 %collective-permute-start.66 = (bf16[2,8,32,128]{3,2,1,0:T(8,128)(2,1)}, bf16[2,8,32,128]{3,2,1,0:T(8,128)(2,1)S(1)}, u32[]{:S(2)}, u32[]{:S(2)}) collective-permute-start(bf16[2,8,32,128]{3,2,1,0:T(8,128)(2,1)} %get-tuple-element.155), channel_id=1, source_target_pairs={{0,20},{4,24},{8,28},{12,0},{16,4},{20,8},{24,12},{28,16},{1,21},{... | collective-permute-start | bytes 393224 | tf_op jit(solution)/shard_map/ppermute | solution.py:399
  630.8 27.8 %collective-permute-start.67 = (bf16[2,8,32,128]{3,2,1,0:T(8,128)(2,1)}, bf16[2,8,32,128]{3,2,1,0:T(8,128)(2,1)}, u32[]{:S(2)}, u32[]{:S(2)}) collective-permute-start(bf16[2,8,32,128]{3,2,1,0:T(8,128)(2,1)} %get-tuple-element.156), channel_id=1, source_target_pairs={{0,24},{4,28},{8,0},{12,4},{16,8},{20,12},{24,16},{28,20},{1,25},{... | collective-permute-start | bytes 393224 | tf_op jit(solution)/shard_map/ppermute | solution.py:399
  666.9 35.0 %collective-permute-start.79 = (bf16[8,2,8,32,128]{4,3,2,1,0:T(8,128)(2,1)}, bf16[8,2,8,32,128]{4,3,2,1,0:T(8,128)(2,1)}, u32[]{:S(2)}, u32[]{:S(2)}) collective-permute-start(bf16[8,2,8,32,128]{4,3,2,1,0:T(8,128)(2,1)} %join.9.token_ref.rest_3_.rest_4_), channel_id=1, source_target_pairs={{0,2},{1,3},{2,0},{3,1},{4,6},{5,7},{6,4},{7,5},{8,10},{9,11},{10,... | collective-permute-start | bytes 3145736 | tf_op jit(solution)/shard_map/ppermute | solution.py:406
  715.5 26.2 %collective-permute-start.86 = (bf16[8,2,5,32,128]{4,3,2,1,0:T(8,128)(2,1)}, bf16[8,2,5,32,128]{4,3,2,1,0:T(8,128)(2,1)}, u32[]{:S(2)}, u32[]{:S(2)}) collective-permute-start(bf16[8,2,5,32,128]{4,3,2,1,0:T(8,128)(2,1)} %join.11.token_ref.rest_8_), channel_id=1, source_target_pairs={{0,1},{1,0},{2,3},{3,2},{4,5},{5,4},{6,7},{7,6},{8,9},{9,8},{10,11... | collective-permute-start | bytes 1966088 | tf_op jit(solution)/shard_map/ppermute | solution.py:415
  715.5 26.2 %collective-permute-start.87 = (bf16[8,2,5,32,128]{4,3,2,1,0:T(8,128)(2,1)}, bf16[8,2,5,32,128]{4,3,2,1,0:T(8,128)(2,1)S(1)}, u32[]{:S(2)}, u32[]{:S(2)}) collective-permute-start(bf16[8,2,5,32,128]{4,3,2,1,0:T(8,128)(2,1)} %collective-permute-done.85.rest_9_), channel_id=1, source_target_pairs={{0,1},{1,0},{2,3},{3,2},{4,5},{5,4},{6,7},{7,6},{8,9},{9,8},{10,11... | collective-permute-start | bytes 1966088 | tf_op jit(solution)/shard_map/ppermute | solution.py:415
  (114 other events, 2637.0 us)
